TPU v7x, 16 devices: a whole 2x2x2 slice. The times are simulated.
16 devices in a mesh: fsdp: 16 (over z, y, x, core).
Axes of the slice: x: 2, y: 2, z: 2, core: 2. Of those that a mesh axis runs over, the one named last changes fastest.
Arguments:
- hidden: bfloat16 [16, 512, 1536], P('fsdp')
- grad_out: bfloat16 [16, 512, 1536], P('fsdp')
- positions: int32 [16, 512], P('fsdp')
- gain_attn: bfloat16 [1536], P('fsdp')
- w_q: bfloat16 [1536, 1536], P('fsdp')
- b_q: bfloat16 [1536], P('fsdp')
- w_k: bfloat16 [1536, 256], P('fsdp')
- b_k: bfloat16 [256], P('fsdp')
- w_v: bfloat16 [1536, 256], P('fsdp')
- b_v: bfloat16 [256], P('fsdp')
- w_o: bfloat16 [1536, 1536], P('fsdp')
- gain_mlp: bfloat16 [1536], P('fsdp')
- w_gate: bfloat16 [1536, 8960], P('fsdp')
- w_up: bfloat16 [1536, 8960], P('fsdp')
- w_down: bfloat16 [8960, 1536], P('fsdp')
Outputs:
- output 1: bfloat16 [16, 512, 1536], P('fsdp')
- output 2: bfloat16 [16, 512, 1536], P('fsdp')
- output 3: float32 [1536], P('fsdp')
- output 4: float32 [1536, 1536], P('fsdp')
- output 5: float32 [1536], P('fsdp')
- output 6: float32 [1536, 256], P('fsdp')
- output 7: float32 [256], P('fsdp')
- output 8: float32 [1536, 256], P('fsdp')
- output 9: float32 [256], P('fsdp')
- output 10: float32 [1536, 1536], P('fsdp')
- output 11: float32 [1536], P('fsdp')
- output 12: float32 [1536, 8960], P('fsdp')
- output 13: float32 [1536, 8960], P('fsdp')
- output 14: float32 [8960, 1536], P('fsdp')
All inputs are finite; a program needn't handle non-finite values.
Results may differ from a plain program's by a relative error of at most 0.0171064.
Values are sent between devices in bfloat16 or wider.
A program may use at most 1 GiB of HBM per device.

v0:
```python
import math
import jax
import jax.numpy as jnp
from jax import lax
from jax.sharding import PartitionSpec as P

HEAD_DIM = 128
NORM_EPS = 1e-6
ROPE_THETA = 1000000.0
FSDP_AXIS = 'fsdp'


def matmul_f32(eq_form, lhs_arr, rhs_arr):
    return jnp.einsum(eq_form, lhs_arr, rhs_arr, preferred_element_type=jnp.float32)


def rope_tables(positions):
    inv_freq = 1.0 / jnp.power(ROPE_THETA, jnp.arange(0, HEAD_DIM, 2).astype(jnp.float32) / HEAD_DIM)
    angles = positions.astype(jnp.float32)[:, :, None] * inv_freq
    angles = jnp.concatenate([angles, angles], axis=-1)[:, :, None, :]
    return jnp.cos(angles), jnp.sin(angles)


def rotate_half(vec_in):
    half_dim = vec_in.shape[-1] // 2
    return jnp.concatenate([-vec_in[..., half_dim:], vec_in[..., :half_dim]], axis=-1)


def rotate_half_t(vec_in):
    half_dim = vec_in.shape[-1] // 2
    return jnp.concatenate([vec_in[..., half_dim:], -vec_in[..., :half_dim]], axis=-1)


def norm_fwd(hidden, gain_vec):
    x_f32 = hidden.astype(jnp.float32)
    inv_rms = lax.rsqrt(jnp.mean(x_f32 * x_f32, axis=-1, keepdims=True) + NORM_EPS)
    return (x_f32 * inv_rms * gain_vec.astype(jnp.float32)).astype(jnp.bfloat16), inv_rms


def norm_bwd(hidden, inv_rms, gain_vec, d_normed):
    unit_rows = hidden.astype(jnp.float32) * inv_rms
    d_gain = jnp.sum(d_normed * unit_rows, axis=(0, 1))
    d_unit = d_normed * gain_vec.astype(jnp.float32)
    d_hidden = inv_rms * (d_unit - unit_rows * jnp.mean(d_unit * unit_rows, axis=-1, keepdims=True))
    return d_hidden, d_gain


def layer_fwd(hidden, positions, weights):
    gain_attn, w_q, b_q, w_k, b_k, w_v, b_v, w_o, gain_mlp, w_gate, w_up, w_down = weights
    n_batch = hidden.shape[0]
    n_seq = hidden.shape[1]
    n_heads = w_q.shape[1] // HEAD_DIM
    n_kv = w_k.shape[1] // HEAD_DIM
    q_per_kv = n_heads // n_kv
    cos_t, sin_t = rope_tables(positions)
    normed_attn, inv_attn = norm_fwd(hidden, gain_attn)
    q_lin = (matmul_f32('bsd,de->bse', normed_attn, w_q) + b_q.astype(jnp.float32)).reshape(n_batch, n_seq, n_heads, HEAD_DIM)
    k_lin = (matmul_f32('bsd,de->bse', normed_attn, w_k) + b_k.astype(jnp.float32)).reshape(n_batch, n_seq, n_kv, HEAD_DIM)
    v_states = (matmul_f32('bsd,de->bse', normed_attn, w_v) + b_v.astype(jnp.float32)).astype(jnp.bfloat16)
    v_states = v_states.reshape(n_batch, n_seq, n_kv, HEAD_DIM)
    q_states = (q_lin * cos_t + rotate_half(q_lin) * sin_t).astype(jnp.bfloat16)
    q_states = q_states.reshape(n_batch, n_seq, n_kv, q_per_kv, HEAD_DIM)
    k_states = (k_lin * cos_t + rotate_half(k_lin) * sin_t).astype(jnp.bfloat16)
    scores = matmul_f32('bqkgd,bskd->bkgqs', q_states, k_states) / math.sqrt(HEAD_DIM)
    causal = lax.broadcasted_iota(jnp.int32, (n_seq, n_seq), 0) >= lax.broadcasted_iota(jnp.int32, (n_seq, n_seq), 1)
    attn_probs = jax.nn.softmax(jnp.where(causal, scores, -1e30), axis=-1)
    attn_out = matmul_f32('bkgqs,bskd->bqkgd', attn_probs.astype(jnp.bfloat16), v_states).astype(jnp.bfloat16)
    attn_out = attn_out.reshape(n_batch, n_seq, n_heads * HEAD_DIM)
    resid_mid = (hidden.astype(jnp.float32) + matmul_f32('bse,ed->bsd', attn_out, w_o)).astype(jnp.bfloat16)
    normed_mlp, inv_mlp = norm_fwd(resid_mid, gain_mlp)
    gate_pre = matmul_f32('bsd,df->bsf', normed_mlp, w_gate)
    up_proj = matmul_f32('bsd,df->bsf', normed_mlp, w_up)
    act_mlp = (jax.nn.silu(gate_pre) * up_proj).astype(jnp.bfloat16)
    layer_out = (resid_mid.astype(jnp.float32) + matmul_f32('bsf,fd->bsd', act_mlp, w_down)).astype(jnp.bfloat16)
    saved_acts = {'cos_t': cos_t, 'sin_t': sin_t, 'normed_attn': normed_attn, 'inv_attn': inv_attn, 'q_states': q_states, 'k_states': k_states, 'v_states': v_states, 'attn_probs': attn_probs, 'attn_out': attn_out, 'resid_mid': resid_mid, 'normed_mlp': normed_mlp, 'inv_mlp': inv_mlp, 'gate_pre': gate_pre, 'up_proj': up_proj, 'act_mlp': act_mlp}
    return layer_out, saved_acts


def layer_bwd(hidden, grad_out, saved_acts, weights):
    gain_attn, w_q, b_q, w_k, b_k, w_v, b_v, w_o, gain_mlp, w_gate, w_up, w_down = weights
    n_batch = hidden.shape[0]
    n_seq = hidden.shape[1]
    n_heads = w_q.shape[1] // HEAD_DIM
    n_kv = w_k.shape[1] // HEAD_DIM
    q_per_kv = n_heads // n_kv
    cos_t = saved_acts['cos_t']
    sin_t = saved_acts['sin_t']
    d_w_down = matmul_f32('bsf,bsd->fd', saved_acts['act_mlp'], grad_out)
    d_act = matmul_f32('bsd,fd->bsf', grad_out, w_down).astype(jnp.bfloat16).astype(jnp.float32)
    gate_pre = saved_acts['gate_pre']
    gate_sig = jax.nn.sigmoid(gate_pre)
    d_gate = (d_act * saved_acts['up_proj'] * gate_sig * (1.0 + gate_pre * (1.0 - gate_sig))).astype(jnp.bfloat16)
    d_up = (d_act * gate_pre * gate_sig).astype(jnp.bfloat16)
    normed_mlp = saved_acts['normed_mlp']
    d_w_gate = matmul_f32('bsd,bsf->df', normed_mlp, d_gate)
    d_w_up = matmul_f32('bsd,bsf->df', normed_mlp, d_up)
    d_normed_mlp = (matmul_f32('bsf,df->bsd', d_gate, w_gate) + matmul_f32('bsf,df->bsd', d_up, w_up)).astype(jnp.bfloat16).astype(jnp.float32)
    d_resid_norm, d_gain_mlp = norm_bwd(saved_acts['resid_mid'], saved_acts['inv_mlp'], gain_mlp, d_normed_mlp)
    d_resid = (grad_out.astype(jnp.float32) + d_resid_norm).astype(jnp.bfloat16)
    d_w_o = matmul_f32('bse,bsd->ed', saved_acts['attn_out'], d_resid)
    d_attn = matmul_f32('bsd,ed->bse', d_resid, w_o).astype(jnp.bfloat16).reshape(n_batch, n_seq, n_kv, q_per_kv, HEAD_DIM)
    attn_probs = saved_acts['attn_probs']
    d_v_states = matmul_f32('bkgqs,bqkgd->bskd', attn_probs.astype(jnp.bfloat16), d_attn).astype(jnp.bfloat16)
    d_probs = matmul_f32('bqkgd,bskd->bkgqs', d_attn, saved_acts['v_states'])
    d_scores = (attn_probs * (d_probs - jnp.sum(attn_probs * d_probs, axis=-1, keepdims=True)) / math.sqrt(HEAD_DIM)).astype(jnp.bfloat16)
    d_q_rot = matmul_f32('bkgqs,bskd->bqkgd', d_scores, saved_acts['k_states']).astype(jnp.bfloat16).astype(jnp.float32)
    d_q_rot = d_q_rot.reshape(n_batch, n_seq, n_heads, HEAD_DIM)
    d_k_rot = matmul_f32('bkgqs,bqkgd->bskd', d_scores, saved_acts['q_states']).astype(jnp.bfloat16).astype(jnp.float32)
    d_q_lin = (d_q_rot * cos_t + rotate_half_t(d_q_rot * sin_t)).reshape(n_batch, n_seq, n_heads * HEAD_DIM)
    d_k_lin = (d_k_rot * cos_t + rotate_half_t(d_k_rot * sin_t)).reshape(n_batch, n_seq, n_kv * HEAD_DIM)
    d_v_lin = d_v_states.reshape(n_batch, n_seq, n_kv * HEAD_DIM)
    d_b_q = jnp.sum(d_q_lin, axis=(0, 1))
    d_b_k = jnp.sum(d_k_lin, axis=(0, 1))
    d_b_v = jnp.sum(d_v_lin.astype(jnp.float32), axis=(0, 1))
    d_q_bf = d_q_lin.astype(jnp.bfloat16)
    d_k_bf = d_k_lin.astype(jnp.bfloat16)
    normed_attn = saved_acts['normed_attn']
    d_w_q = matmul_f32('bsd,bse->de', normed_attn, d_q_bf)
    d_w_k = matmul_f32('bsd,bse->de', normed_attn, d_k_bf)
    d_w_v = matmul_f32('bsd,bse->de', normed_attn, d_v_lin)
    d_normed_attn = (matmul_f32('bse,de->bsd', d_q_bf, w_q) + matmul_f32('bse,de->bsd', d_k_bf, w_k) + matmul_f32('bse,de->bsd', d_v_lin, w_v)).astype(jnp.bfloat16).astype(jnp.float32)
    d_hidden_norm, d_gain_attn = norm_bwd(hidden, saved_acts['inv_attn'], gain_attn, d_normed_attn)
    grad_hidden = (d_resid.astype(jnp.float32) + d_hidden_norm).astype(jnp.bfloat16)
    grad_list = (d_gain_attn, d_w_q, d_b_q, d_w_k, d_b_k, d_w_v, d_b_v, d_w_o, d_gain_mlp, d_w_gate, d_w_up, d_w_down)
    return grad_hidden, grad_list


def gather_all(shards):
    return tuple(lax.all_gather(w_shard, FSDP_AXIS, axis=0, tiled=True) for w_shard in shards)


def solution(mesh):
    act_spec = P(FSDP_AXIS, None, None)
    mat_spec = P(FSDP_AXIS, None)
    vec_spec = P(FSDP_AXIS)
    param_specs = (vec_spec, mat_spec, vec_spec, mat_spec, vec_spec, mat_spec, vec_spec, mat_spec, vec_spec, mat_spec, mat_spec, mat_spec)
    in_specs_all = (act_spec, act_spec, mat_spec) + param_specs
    out_specs_all = (act_spec, act_spec) + param_specs

    def local_step(hidden, grad_out, positions, *shards):
        full_fwd = gather_all(shards)
        layer_out, saved_acts = layer_fwd(hidden, positions, full_fwd)
        shards_bwd, saved_acts = lax.optimization_barrier((shards, saved_acts))
        full_bwd = gather_all(shards_bwd)
        grad_hidden, grad_list = layer_bwd(hidden, grad_out, saved_acts, full_bwd)
        grad_shards = tuple(lax.psum_scatter(grad_part, FSDP_AXIS, scatter_dimension=0, tiled=True) for grad_part in grad_list)
        return (layer_out, grad_hidden) + grad_shards

    return jax.shard_map(local_step, mesh=mesh, in_specs=in_specs_all, out_specs=out_specs_all, check_vma=False)
```

profile of v0, /device:TPU:0, one launch (start us, length us, event | category | flops | bytes accessed | tf_op | source)
XLA Modules:
  0.0 1981.7 jit_solution(4709725592085561868)
XLA Ops:
  11.4 35.4 %all-reduce.14 = (bf16[1536]{0:T(1024)(128)(2,1)S(1)}, bf16[256]{0:T(256)(128)(2,1)S(1)}, bf16[1536]{0:T(1024)(128)(2,1)S(1)}, bf16[256]{0:T(256)(128)(2,1)S(1)}, bf16[1536]{0:T(1024)(128)(2,1)S(1)}) all-reduce(bf16[1536]{0:T(1024)(128)(2,1)S(1)} %dynamic-update-slice, ...), channel_id=1, replica_groups=mesh['fsdp'=16] {'fsdp'}, use_global_device_ids=true, to_apply=%add | all-reduce | flops 5120 | bytes 20480
  46.8 0.8 iota_compare_fusion
  47.7 1.7 fusion.142
  49.8 15.3 all_gather.66
  66.2 1.0 slice_negate_fusion.3
  67.2 0.9 fusion.135
  68.0 13.8 all_gather.64
  81.8 1.3 fusion.120
  83.1 6.6 convolution_add_fusion.2
  89.7 2.4 copy.59
  93.5 2.6 fusion.11
  96.1 3.5 fusion.10
  99.7 3.9 fusion.9
  103.6 4.5 copy-done
  108.1 2.1 fusion.70
  110.2 6.3 fusion.51
  116.6 2.1 fusion.62
  119.1 85.3 %all-gather.15.cloned.1.call-done = bf16[1536,8960]{1,0:T(8,128)(2,1)} async-done(((bf16[96,8960]{1,0:T(8,128)(2,1)}), bf16[1536,8960]{1,0:T(8,128)(2,1)}) %all-gather.15.cloned.1.call-update) | async-done | bytes 27525136 | tf_op jit(solution)/shard_map/all_gather | solution.py:129
  204.5 23.4 %fusion.93 = f32[512,8960]{1,0:T(8,128)} fusion(bf16[1536,8960]{1,0:T(8,128)(2,1)} %all-gather.15.cloned.1.call-done, bf16[1,512,1536]{2,1,0:T(8,128)(2,1)S(1)} %fusion.53), kind=kOutput, calls=%fused_computation.124 | convolution fusion | flops 14092861440 | bytes 47448064 | tf_op jit(solution)/shard_map/bsd,df->bsf/dot_general | solution.py:14
  227.9 90.2 %all-gather.17.cloned.1.call-done = bf16[1536,8960]{1,0:T(8,128)(2,1)} async-done(((bf16[96,8960]{1,0:T(8,128)(2,1)}), bf16[1536,8960]{1,0:T(8,128)(2,1)}) %all-gather.17.cloned.1.call-update) | async-done | bytes 27525136 | tf_op jit(solution)/shard_map/all_gather | solution.py:129
  318.1 33.3 %multiply_convert_fusion = (bf16[512,8960]{1,0:T(8,128)(2,1)}, f32[512,8960]{1,0:T(8,128)}) fusion(f32[512,8960]{1,0:T(8,128)} %fusion.93, bf16[1536,8960]{1,0:T(8,128)(2,1)} %all-gather.17.cloned.1.call-done, bf16[1,512,1536]{2,1,0:T(8,128)(2,1)S(1)} %fusion.53), kind=kOutput, calls=%fused_computation.8 | convolution fusion | flops 14120386560 | bytes 74973184 | tf_op jit(solution)/shard_map/bsd,df->bsf/dot_general | solution.py:14
  354.8 32.7 %all-reduce.13 = (bf16[1536]{0:T(1024)(128)(2,1)S(1)}, bf16[1536]{0:T(1024)(128)(2,1)}) all-reduce(bf16[1536]{0:T(1024)(128)(2,1)S(1)} %dynamic-update-slice.5, bf16[1536]{0:T(1024)(128)(2,1)S(1)} %dynamic-update-slice.6), channel_id=1, replica_groups=mesh['fsdp'=16] {'fsdp'}, use_global_device_ids=true, to_apply=%add.5 | all-reduce | flops 3072 | bytes 12288
  387.6 76.6 %all-gather.21.cloned.1.call-done = bf16[8960,1536]{1,0:T(8,128)(2,1)} async-done(((bf16[560,1536]{1,0:T(8,128)(2,1)}), bf16[8960,1536]{1,0:T(8,128)(2,1)}) %all-gather.21.cloned.1.call-update) | async-done | bytes 27525136 | tf_op jit(solution)/shard_map/all_gather | solution.py:129
  464.2 55.7 %fusion.2 = (bf16[1,512,8960]{2,1,0:T(8,128)(2,1)}, bf16[8960,512]{0,1:T(8,128)(2,1)}) fusion(f32[1,512,8960]{2,1,0:T(8,128)} %bitcast.379, f32[1,512,8960]{2,1,0:T(8,128)} %bitcast.376, bf16[8960,1536]{1,0:T(8,128)(2,1)} %all-gather.21.cloned.1.call-done, bf16[1,512,1536]{2,1,0:T(8,128)(2,1)S(1)} %copy-done.35), kind=kOutput, calls=%fused_computation.4 | convolution fusion | flops 14147911680 | bytes 84148224 | tf_op jit(solution)/shard_map/bsd,fd->bsf/dot_general | solution.py:14
  519.9 57.9 %all-gather.25.cloned.1.call-done = bf16[1536,8960]{1,0:T(8,128)(2,1)} async-done(((bf16[96,8960]{1,0:T(8,128)(2,1)}), bf16[1536,8960]{1,0:T(8,128)(2,1)}) %all-gather.25.cloned.1.call-update) | async-done | bytes 27525136 | tf_op jit(solution)/shard_map/all_gather | solution.py:129
  577.8 24.8 %fusion.16 = f32[512,1536]{1,0:T(8,128)} fusion(bf16[1536,8960]{1,0:T(8,128)(2,1)} %all-gather.25.cloned.1.call-done, f32[1,512,8960]{2,1,0:T(8,128)} %bitcast.377, bf16[8960,512]{0,1:T(8,128)(2,1)} %get-tuple-element.103), kind=kOutput, calls=%fused_computation.25 | convolution fusion | flops 14124974080 | bytes 58195968 | tf_op jit(solution)/shard_map/bsf,df->bsd/dot_general | solution.py:14
  602.7 88.9 %all-gather.23.cloned.1.call-done = bf16[1536,8960]{1,0:T(8,128)(2,1)} async-done(((bf16[96,8960]{1,0:T(8,128)(2,1)}), bf16[1536,8960]{1,0:T(8,128)(2,1)}) %all-gather.23.cloned.1.call-update) | async-done | bytes 27525136 | tf_op jit(solution)/shard_map/all_gather | solution.py:129
  691.6 23.7 %fusion.43 = (f32[1536]{0:T(1024)}, f32[512]{0:T(512)S(1)}, bf16[512,1536]{1,0:T(8,128)(2,1)}) fusion(bf16[1,512,1536]{2,1,0:T(8,128)(2,1)S(1)} %copy-done.24, f32[512]{0:T(512)S(1)} %copy-done.52, f32[1536]{0:T(1024)S(1)} %convert_element_type.282, f32[512,1536]{1,0:T(8,128)} %fusion.16, bf16[1536,8960]{1,0:T(8,128)(2,1)} %all-gather.23.cloned.1.call-done, ...), kind=kOutput, calls=%fused_computation.66 | convolution fusion | flops 14100723712 | bytes 43008000 | tf_op jit(solution)/shard_map/bsf,df->bsd/dot_general | solution.py:14
  715.3 2.9 fusion.41
  718.2 12.3 all-gather.27.cloned.1.call-done
  730.5 6.1 convolution_convert_fusion.1
  736.6 1.7 copy.67
  738.3 7.6 convert_reduce_fusion
  746.6 1.8 fusion.79
  748.4 10.9 fusion.5
  759.4 10.2 fusion.22
  769.6 2.1 broadcast_multiply_fusion.1
  772.2 0.7 fusion.150
  773.0 1.8 fusion.81
  774.8 8.1 fusion.77
  783.0 0.9 copy-done.43
  783.8 3.8 bitcast_convert_fusion
  788.9 1.0 copy-done.1
  789.9 2.6 add_convert_fusion
  792.4 5.4 fusion.83
  797.9 1.3 copy-done.36
  799.2 26.8 %fusion.12 = f32[8960,1536]{1,0:T(8,128)} fusion(bf16[1,512,8960]{2,1,0:T(8,128)(2,1)} %bitcast.380, bf16[1,512,1536]{2,1,0:T(8,128)(2,1)S(1)} %copy-done.36), kind=kOutput, calls=%fused_computation.21 | convolution fusion | flops 14092861440 | bytes 65798144 | tf_op jit(solution)/shard_map/bsf,bsd->fd/dot_general | solution.py:14
  826.1 1.3 copy-done.28
  827.5 36.3 %fusion.14 = f32[1536,8960]{1,0:T(8,128)} fusion(bf16[1,512,1536]{2,1,0:T(8,128)(2,1)S(1)} %copy-done.28, f32[1,512,8960]{2,1,0:T(8,128)} %bitcast.378, bf16[8960,512]{0,1:T(8,128)(2,1)} %get-tuple-element.103), kind=kOutput, calls=%fused_computation.23 | convolution fusion | flops 14124974080 | bytes 84148224 | tf_op jit(solution)/shard_map/bsd,bsf->df/dot_general | solution.py:14
  863.9 26.4 %fusion.18 = f32[1536,8960]{1,0:T(8,128)} fusion(bf16[1,512,8960]{2,1,0:T(8,128)(2,1)} %get-tuple-element.102, bf16[1,512,1536]{2,1,0:T(8,128)(2,1)S(1)} %copy-done.28), kind=kOutput, calls=%fused_computation.27 | convolution fusion | flops 14092861440 | bytes 65798144 | tf_op jit(solution)/shard_map/bsd,bsf->df/dot_general | solution.py:14
  891.0 13.7 all_gather.81
  904.7 12.9 all_gather.82
  917.7 22.4 %fusion.54 = bf16[1,512,1536]{2,1,0:T(8,128)(2,1)} fusion(bf16[1,512,1536]{2,1,0:T(8,128)(2,1)} %copy-done.23, bf16[512,8960]{1,0:T(8,128)(2,1)} %get-tuple-element.100, bf16[8960,1536]{1,0:T(8,128)(2,1)} %all-gather.19.cloned.1.call-done), kind=kOutput, calls=%fused_computation.77 | convolution fusion | flops 14095220736 | bytes 39845888 | tf_op jit(solution)/shard_map/bsf,fd->bsd/dot_general | solution.py:14
  940.7 3.9 fusion.65
  944.7 5.1 fusion.157
  950.5 0.7 copy-done.5
  951.5 2.6 fusion.50
  954.1 32.3 %all-reduce.12 = (f32[1536]{0:T(1024)S(1)}, f32[1536]{0:T(1024)S(1)}, f32[256]{0:T(256)S(1)}, f32[256]{0:T(256)S(1)}, f32[1536]{0:T(1024)S(1)}) all-reduce(f32[1536]{0:T(1024)S(1)} %get-tuple-element.64, f32[1536]{0:T(1024)S(1)} %reduce_sum.113, f32[256]{0:T(256)S(1)} %bitcast.375, ...), channel_id=2, replica_groups=mesh['fsdp'=16] {'fsdp'}, use_global_device_ids=true, to_apply=%region_8.9.clone | all-reduce | flops 5120 | bytes 40960
  989.4 3.6 fusion.48
  992.9 82.8 %reduce-scatter.14.cloned.1.call-done = f32[96,1536]{1,0:T(8,128)} async-done(((f32[1536,1536]{1,0:T(8,128)}), f32[96,1536]{1,0:T(8,128)}) %reduce-scatter.14.cloned.1.call-update) | async-done | bytes 589840 | tf_op jit(solution)/shard_map/reduce_scatter | solution.py:146
  1075.7 84.6 %reduce-scatter.8.cloned.1.call-done = f32[96,1536]{1,0:T(8,128)} async-done(((f32[1536,1536]{1,0:T(8,128)}), f32[96,1536]{1,0:T(8,128)}) %reduce-scatter.8.cloned.1.call-update) | async-done | bytes 589840 | tf_op jit(solution)/shard_map/reduce_scatter | solution.py:146
  1160.3 271.5 %reduce-scatter.20.cloned.1.call-done = f32[560,1536]{1,0:T(8,128)} async-done(((f32[8960,1536]{1,0:T(8,128)}), f32[560,1536]{1,0:T(8,128)}) %reduce-scatter.20.cloned.1.call-update) | async-done | bytes 3440656 | tf_op jit(solution)/shard_map/reduce_scatter | solution.py:146
  1431.8 271.5 %reduce-scatter.18.cloned.1.call-done = f32[96,8960]{1,0:T(8,128)} async-done(((f32[1536,8960]{1,0:T(8,128)}), f32[96,8960]{1,0:T(8,128)}) %reduce-scatter.18.cloned.1.call-update) | async-done | bytes 3440656 | tf_op jit(solution)/shard_map/reduce_scatter | solution.py:146
  1703.2 271.4 %reduce-scatter.16.cloned.1.call-done = f32[96,8960]{1,0:T(8,128)} async-done(((f32[1536,8960]{1,0:T(8,128)}), f32[96,8960]{1,0:T(8,128)}) %reduce-scatter.16.cloned.1.call-update) | async-done | bytes 3440656 | tf_op jit(solution)/shard_map/reduce_scatter | solution.py:146
  (204 shorter events, 18.9 us)
Async XLA Ops:
  7.2 2.9 copy-start.57
  7.2 3.0 copy-start.58
  7.2 3.2 copy-start.59
  7.2 3.4 copy-start.62
  7.2 3.7 copy-start.60
  7.2 3.9 copy-start.61
  7.2 42.1 %copy-start.4 = (bf16[1,512,1536]{2,1,0:T(8,128)(2,1)S(1)}, bf16[1,512,1536]{2,1,0:T(8,128)(2,1)}, u32[]{:S(2)}) copy-start(bf16[1,512,1536]{2,1,0:T(8,128)(2,1)} %param.15) | copy-start | bytes 4718596
  7.3 75.9 %all-gather.11.cloned.1.call-start = ((), (), s32[]{:S(2)}) async-start(), calls=%async_computation.7 | async-start | bytes 5013504 | tf_op jit(solution)/shard_map/all_gather | solution.py:129
  8.0 102.2 %all-gather.13.cloned.1.call-start = ((), (), s32[]{:S(2)}) async-start(), calls=%async_computation.8 | async-start | bytes 5013504 | tf_op jit(solution)/shard_map/all_gather | solution.py:129
  8.7 41.0 %copy-start.45 = (bf16[96,256]{1,0:T(8,128)(2,1)S(1)}, bf16[96,256]{1,0:T(8,128)(2,1)}, u32[]{:S(2)}) copy-start(bf16[96,256]{1,0:T(8,128)(2,1)} %param.21) | copy-start | bytes 147460
  8.7 195.7 %all-gather.15.cloned.1.call-start = ((), (), s32[]{:S(2)}) async-start(), calls=%async_computation.9 | async-start | bytes 29245440 | tf_op jit(solution)/shard_map/all_gather | solution.py:129
  9.5 308.6 %all-gather.17.cloned.1.call-start = ((), (), s32[]{:S(2)}) async-start(), calls=%async_computation.10 | async-start | bytes 29245440 | tf_op jit(solution)/shard_map/all_gather | solution.py:129
  10.1 454.1 %all-gather.21.cloned.1.call-start = ((), (), s32[]{:S(2)}) async-start(), calls=%async_computation.12 | async-start | bytes 29245440 | tf_op jit(solution)/shard_map/all_gather | solution.py:129
  49.4 17.8 copy-start.16
  49.8 16.4 copy-start.49
  65.5 17.6 copy-start.6
  65.5 2.5 copy-start.47
  92.7 3.4 copy-start.12
  92.7 3.4 copy-start.14
  99.7 8.4 copy-start.37
  103.6 4.5 copy-start
  110.2 6.4 copy-start.13
  110.2 6.4 copy-start.15
  110.2 6.4 copy-start.18
  116.6 2.1 copy-start.23
  116.6 2.1 copy-start.51
  119.1 199.0 %copy-start.27 = (bf16[1,512,1536]{2,1,0:T(8,128)(2,1)}, bf16[1,512,1536]{2,1,0:T(8,128)(2,1)S(1)}, u32[]{:S(2)}) copy-start(bf16[1,512,1536]{2,1,0:T(8,128)(2,1)S(1)} %fusion.53) | copy-start | bytes 4718596
  351.5 112.7 %copy-start.35 = (bf16[1,512,1536]{2,1,0:T(8,128)(2,1)S(1)}, bf16[1,512,1536]{2,1,0:T(8,128)(2,1)}, u32[]{:S(2)}) copy-start(bf16[1,512,1536]{2,1,0:T(8,128)(2,1)} %param.16) | copy-start | bytes 4718596
  351.5 226.4 %all-gather.25.cloned.1.call-start = ((), (), s32[]{:S(2)}) async-start(), calls=%async_computation.14 | async-start | bytes 29245440 | tf_op jit(solution)/shard_map/all_gather | solution.py:129
  352.0 339.6 %all-gather.23.cloned.1.call-start = ((), (), s32[]{:S(2)}) async-start(), calls=%async_computation.13 | async-start | bytes 29245440 | tf_op jit(solution)/shard_map/all_gather | solution.py:129
  352.8 377.7 %all-gather.27.cloned.1.call-start = ((), (), s32[]{:S(2)}) async-start(), calls=%async_computation.15 | async-start | bytes 5013504 | tf_op jit(solution)/shard_map/all_gather | solution.py:129
  353.5 564.1 %all-gather.19.cloned.1.call-start = ((), (), s32[]{:S(2)}) async-start(), calls=%async_computation.11 | async-start | bytes 29245440 | tf_op jit(solution)/shard_map/all_gather | solution.py:129
  354.3 590.4 %all-gather.29.cloned.1.call-start = ((), (), s32[]{:S(2)}) async-start(), calls=%async_computation.16 | async-start | bytes 5013504 | tf_op jit(solution)/shard_map/all_gather | solution.py:129
  387.5 605.4 %reduce-scatter.12.cloned.1.call-start = ((), (), s32[]{:S(2)}) async-start(), calls=%async_computation.19 | async-start | bytes 1671168 | tf_op jit(solution)/shard_map/reduce_scatter | solution.py:146
  577.8 113.8 %copy-start.24 = (bf16[1,512,1536]{2,1,0:T(8,128)(2,1)S(1)}, bf16[1,512,1536]{2,1,0:T(8,128)(2,1)}, u32[]{:S(2)}) copy-start(bf16[1,512,1536]{2,1,0:T(8,128)(2,1)} %copy-done.23) | copy-start | bytes 4718596
  577.8 113.8 %copy-start.52 = (f32[512]{0:T(512)S(1)}, f32[512]{0:T(512)}, u32[]{:S(2)}) copy-start(f32[512]{0:T(512)} %copy-done.51) | copy-start | bytes 6148
  718.2 18.4 copy-start.25
  738.3 8.3 copy-start.7
  745.9 2.5 copy-start.38
  759.3 233.6 %reduce-scatter.10.cloned.1.call-start = ((), (), s32[]{:S(2)}) async-start(), calls=%async_computation.18 | async-start | bytes 1671168 | tf_op jit(solution)/shard_map/reduce_scatter | solution.py:146
  759.4 10.2 copy-start.22
  759.4 10.2 copy-start.31
  769.6 2.6 copy-start.3
  769.6 2.6 copy-start.20
  773.0 9.9 copy-start.33
  774.7 301.0 %reduce-scatter.14.cloned.1.call-start = ((), (), s32[]{:S(2)}) async-start(), calls=%async_computation.20 | async-start | bytes 10027008 | tf_op jit(solution)/shard_map/reduce_scatter | solution.py:146
  782.9 377.4 %reduce-scatter.8.cloned.1.call-start = ((), (), s32[]{:S(2)}) async-start(), calls=%async_computation.17 | async-start | bytes 10027008 | tf_op jit(solution)/shard_map/reduce_scatter | solution.py:146
  787.6 2.3 copy-start.1
  788.9 3.6 copy-start.8
  788.9 3.6 copy-start.10
  797.8 633.9 %reduce-scatter.20.cloned.1.call-start = ((), (), s32[]{:S(2)}) async-start(), calls=%async_computation.23 | async-start | bytes 58490880 | tf_op jit(solution)/shard_map/reduce_scatter | solution.py:146
  826.1 877.2 %reduce-scatter.18.cloned.1.call-start = ((), (), s32[]{:S(2)}) async-start(), calls=%async_computation.22 | async-start | bytes 58490880 | tf_op jit(solution)/shard_map/reduce_scatter | solution.py:146
  863.8 1110.9 %reduce-scatter.16.cloned.1.call-start = ((), (), s32[]{:S(2)}) async-start(), calls=%async_computation.21 | async-start | bytes 58490880 | tf_op jit(solution)/shard_map/reduce_scatter | solution.py:146
  890.2 14.5 copy-start.48
  917.7 22.4 %copy-start.2 = (f32[1,2,128,6,512]{4,2,3,1,0:T(8,128)S(1)}, f32[1,2,128,6,512]{4,2,3,1,0:T(8,128)}, u32[]{:S(2)}) copy-start(f32[1,2,128,6,512]{4,2,3,1,0:T(8,128)} %copy-done.1) | copy-start | bytes 9437188
  917.7 22.4 %copy-start.21 = (f32[1,512,1,128]{1,3,2,0:T(8,128)S(1)}, f32[1,512,1,128]{1,3,2,0:T(8,128)}, u32[]{:S(2)}) copy-start(f32[1,512,1,128]{1,3,2,0:T(8,128)} %get-tuple-element.51) | copy-start | bytes 786436
  917.7 22.4 %copy-start.9 = (f32[1,512,12,64]{1,3,2,0:T(8,128)S(1)}, f32[1,512,12,64]{1,3,2,0:T(8,128)}, u32[]{:S(2)}) copy-start(f32[1,512,12,64]{1,3,2,0:T(8,128)} %copy-done.8) | copy-start | bytes 4718596
  917.7 22.4 %copy-start.11 = (f32[1,512,12,64]{1,3,2,0:T(8,128)S(1)}, f32[1,512,12,64]{1,3,2,0:T(8,128)}, u32[]{:S(2)}) copy-start(f32[1,512,12,64]{1,3,2,0:T(8,128)} %copy-done.10) | copy-start | bytes 4718596
  944.7 5.1 copy-start.32
  944.7 5.1 copy-start.34
  951.5 2.6 copy-start.53
  951.5 2.6 copy-start.54
  951.5 2.6 copy-start.56
  951.5 37.8 %copy-start.26 = (bf16[1,512,1536]{2,1,0:T(8,128)(2,1)S(1)}, bf16[1,512,1536]{2,1,0:T(8,128)(2,1)}, u32[]{:S(2)}) copy-start(bf16[1,512,1536]{2,1,0:T(8,128)(2,1)} %copy-done.25) | copy-start | bytes 4718596
  (16 other events, 19.6 us)
Sparse Core Ops, SparseCore 0:
  10.3 40.4 all-gather.10
  53.0 37.7 all-gather.12
  93.1 111.3 all-gather.14
  206.6 111.4 all-gather.16
  351.6 112.5 all-gather.20
  466.3 111.4 all-gather.24
  580.1 111.4 all-gather.22
  693.8 36.6 all-gather.26
  732.8 111.4 all-gather.18
  846.4 36.6 all-gather.28
  887.6 49.3 reduce-scatter.11
  941.4 49.4 reduce-scatter.9
  996.2 79.4 reduce-scatter.13
  1080.8 79.4 reduce-scatter.7
  1166.0 265.7 reduce-scatter.19
  1437.5 265.7 reduce-scatter.17
  1708.9 265.7 reduce-scatter.15
where the time goes:
time: 1990 us; the launch traced here: 1980 us
  waiting for transfers between devices  1400 us (70%)
  matrix products  348 us (17%)
  blocking collectives  156 us (8%)
  other arithmetic  41.4 us (2%)
  local copies, waits for them, and re-layouts  21.6 us (1%)
    reduce_scatter x7, waiting for transfers between devices, local_step(): lax.psum_scatter(grad_part, FSDP_AXIS, scatter_dimension=0, tiled=True)  982 us
    all_gather x10, waiting for transfers between devices, gather_all(): lax.all_gather(w_shard, FSDP_AXIS, axis=0, tiled=True)  411 us
    dot_general x27, matrix products, matmul_f32(): jnp.einsum(eq_form, lhs_arr, rhs_arr, preferred_element_type=jnp.float32)  348 us
    unnamed x3, blocking collectives  100 us
    all_gather x4, blocking collectives, gather_all(): lax.all_gather(w_shard, FSDP_AXIS, axis=0, tiled=True)  55.7 us
  transfers between devices with their start and end apart: 17, of which 11 were waited for; matrix products, arithmetic and copies ran while one was open for 18% of the time, Pallas kernels for 0%

commit v1 on v0

v1 whole, which is shorter than its diff:
```python
import math
import jax
import jax.numpy as jnp
from jax import lax
from jax.sharding import PartitionSpec as P

HEAD_DIM = 128
NORM_EPS = 1e-6
ROPE_THETA = 1000000.0
AX = 'fsdp'
N_DEV = 16
TP = 8
GROUPS = [list(range(0, 8)), list(range(8, 16))]
Z_PERM = [(i, i ^ 8) for i in range(N_DEV)]
F32 = jnp.float32
BF16 = jnp.bfloat16


def dot(eq_form, lhs_arr, rhs_arr):
    return jnp.einsum(eq_form, lhs_arr, rhs_arr, preferred_element_type=F32)


def rope_tables(positions):
    inv_freq = 1.0 / jnp.power(ROPE_THETA, jnp.arange(0, HEAD_DIM, 2).astype(F32) / HEAD_DIM)
    angles = positions.astype(F32)[:, None] * inv_freq
    angles = jnp.concatenate([angles, angles], axis=-1)[:, None, :]
    return jnp.cos(angles), jnp.sin(angles)


def rotate_half(vec_in):
    half_dim = vec_in.shape[-1] // 2
    return jnp.concatenate([-vec_in[..., half_dim:], vec_in[..., :half_dim]], axis=-1)


def rotate_half_t(vec_in):
    half_dim = vec_in.shape[-1] // 2
    return jnp.concatenate([vec_in[..., half_dim:], -vec_in[..., :half_dim]], axis=-1)


def norm_fwd(hidden, gain_vec):
    x_f32 = hidden.astype(F32)
    inv_rms = lax.rsqrt(jnp.mean(x_f32 * x_f32, axis=-1, keepdims=True) + NORM_EPS)
    return (x_f32 * inv_rms * gain_vec).astype(BF16), inv_rms


def norm_bwd(hidden, inv_rms, gain_vec, d_normed):
    unit_rows = hidden.astype(F32) * inv_rms
    d_gain = jnp.sum(d_normed * unit_rows, axis=0)
    d_unit = d_normed * gain_vec
    d_hidden = inv_rms * (d_unit - unit_rows * jnp.mean(d_unit * unit_rows, axis=-1, keepdims=True))
    return d_hidden, d_gain


def z_pair(arr):
    return lax.ppermute(arr, AX, Z_PERM)


def local_step(hidden, grad_out, positions, gain_attn, w_q, b_q, w_k, b_k, w_v, b_v, w_o, gain_mlp, w_gate, w_up, w_down):
    n_seq, width = hidden.shape[1], hidden.shape[2]
    rows = w_q.shape[0]
    q_width, kv_width = w_q.shape[1], w_k.shape[1]
    n_heads, n_kv = q_width // HEAD_DIM, kv_width // HEAD_DIM
    q_per_kv = n_heads // n_kv
    ff_blk = w_down.shape[0]
    ff_loc = 2 * ff_blk
    half = width // 2
    n_tok = n_seq
    z_idx = lax.axis_index(AX) // TP
    z_zero = z_idx == 0
    hidden = hidden[0]
    grad_out = grad_out[0]

    kvb = jnp.concatenate([b_k, b_v, jnp.zeros((rows - 2 * b_k.shape[0],), BF16)])
    small = jnp.stack([gain_attn, b_q, gain_mlp, kvb], axis=1)
    small = jnp.pad(small, ((0, 0), (0, 124)))
    qkv_loc = jnp.concatenate([w_q, w_k, w_v, small], axis=1)
    qkv_full = lax.all_gather(qkv_loc, AX, axis=0, tiled=True)
    n_qkv = q_width + 2 * kv_width
    w_qkv = qkv_full[:, :n_qkv]
    small_t = qkv_full[:, n_qkv:n_qkv + 4].T.astype(F32)
    gain_a, bias_q, gain_m = small_t[0], small_t[1], small_t[2]
    kvb_full = small_t[3].reshape(N_DEV, rows)
    n_b = b_k.shape[0]
    bias_k = kvb_full[:, :n_b].reshape(kv_width)
    bias_v = kvb_full[:, n_b:2 * n_b].reshape(kv_width)
    bias = jnp.concatenate([bias_q, bias_k, bias_v])
    w_o_full = lax.all_gather(w_o, AX, axis=0, tiled=True)

    gu = jnp.stack([w_gate, w_up], axis=0).reshape(2, rows, 2, TP, ff_blk)
    gu = gu.transpose(3, 0, 1, 2, 4).reshape(TP, 2 * rows, ff_loc)
    gu = lax.all_to_all(gu, AX, 0, 0, axis_index_groups=GROUPS, tiled=True)
    gu = gu.reshape(TP, 2, rows, ff_loc).transpose(1, 0, 2, 3).reshape(2, half, ff_loc)
    gu_other = z_pair(gu)
    gu_lo = jnp.where(z_zero, gu, gu_other)
    gu_hi = jnp.where(z_zero, gu_other, gu)
    w_g = jnp.concatenate([gu_lo[0], gu_hi[0]], axis=0)
    w_u = jnp.concatenate([gu_lo[1], gu_hi[1]], axis=0)
    down_other = z_pair(w_down)
    w_d = jnp.concatenate([jnp.where(z_zero, w_down, down_other), jnp.where(z_zero, down_other, w_down)], axis=0)

    go_all = lax.all_gather(grad_out, AX, axis=0, tiled=True, axis_index_groups=GROUPS)

    cos_t, sin_t = rope_tables(positions[0])
    normed_attn, inv_attn = norm_fwd(hidden, gain_a)
    qkv = dot('sd,de->se', normed_attn, w_qkv) + bias
    q_lin = qkv[:, :q_width].reshape(n_seq, n_heads, HEAD_DIM)
    k_lin = qkv[:, q_width:q_width + kv_width].reshape(n_seq, n_kv, HEAD_DIM)
    v_states = qkv[:, q_width + kv_width:].astype(BF16).reshape(n_seq, n_kv, HEAD_DIM)
    q_states = (q_lin * cos_t + rotate_half(q_lin) * sin_t).astype(BF16).reshape(n_seq, n_kv, q_per_kv, HEAD_DIM)
    k_states = (k_lin * cos_t + rotate_half(k_lin) * sin_t).astype(BF16)
    scores = dot('qkgd,skd->kgqs', q_states, k_states) / math.sqrt(HEAD_DIM)
    causal = lax.broadcasted_iota(jnp.int32, (n_seq, n_seq), 0) >= lax.broadcasted_iota(jnp.int32, (n_seq, n_seq), 1)
    attn_probs = jax.nn.softmax(jnp.where(causal, scores, -1e30), axis=-1)
    attn_out = dot('kgqs,skd->qkgd', attn_probs.astype(BF16), v_states).astype(BF16).reshape(n_seq, q_width)
    resid_mid = (hidden.astype(F32) + dot('se,ed->sd', attn_out, w_o_full)).astype(BF16)
    normed_mlp, inv_mlp = norm_fwd(resid_mid, gain_m)

    h_all = lax.all_gather(normed_mlp, AX, axis=0, tiled=True, axis_index_groups=GROUPS)
    gate_pre = dot('sd,df->sf', h_all, w_g)
    up_proj = dot('sd,df->sf', h_all, w_u)
    act = (jax.nn.silu(gate_pre) * up_proj).astype(BF16)
    d_act = dot('sd,fd->sf', go_all, w_d).astype(BF16).astype(F32)
    gate_sig = jax.nn.sigmoid(gate_pre)
    d_gate = (d_act * up_proj * gate_sig * (1.0 + gate_pre * (1.0 - gate_sig))).astype(BF16)
    d_up = (d_act * gate_pre * gate_sig).astype(BF16)
    dn_part = dot('sf,df->sd', d_gate, w_g) + dot('sf,df->sd', d_up, w_u)
    d_normed_mlp = lax.psum_scatter(dn_part, AX, scatter_dimension=0, tiled=True, axis_index_groups=GROUPS)
    d_normed_mlp = d_normed_mlp.astype(BF16).astype(F32)

    out_part = dot('sf,fd->sd', act, w_d)
    out_sum = lax.psum_scatter(out_part, AX, scatter_dimension=0, tiled=True, axis_index_groups=GROUPS)
    layer_out = (resid_mid.astype(F32) + out_sum).astype(BF16)

    d_wd = dot('sf,sd->fd', act, go_all)
    d_wd_send = lax.dynamic_slice_in_dim(d_wd, (1 - z_idx) * ff_blk, ff_blk, axis=0)
    d_wd_keep = lax.dynamic_slice_in_dim(d_wd, z_idx * ff_blk, ff_blk, axis=0)
    g_w_down = d_wd_keep + z_pair(d_wd_send)
    h_send = lax.dynamic_slice_in_dim(h_all, (1 - z_idx) * half, half, axis=1)
    h_keep = lax.dynamic_slice_in_dim(h_all, z_idx * half, half, axis=1)
    g_g = dot('sd,sf->df', h_keep, d_gate) + z_pair(dot('sd,sf->df', h_send, d_gate))
    g_u = dot('sd,sf->df', h_keep, d_up) + z_pair(dot('sd,sf->df', h_send, d_up))

    def back_rows(grad):
        grad = lax.all_to_all(grad.reshape(TP, rows, ff_loc), AX, 0, 0, axis_index_groups=GROUPS, tiled=True)
        return grad.reshape(TP, rows, 2, ff_blk).transpose(1, 2, 0, 3).reshape(rows, N_DEV * ff_blk)

    g_w_gate = back_rows(g_g)
    g_w_up = back_rows(g_u)

    d_resid_norm, d_gain_m = norm_bwd(resid_mid, inv_mlp, gain_m, d_normed_mlp)
    d_resid = (grad_out.astype(F32) + d_resid_norm).astype(BF16)
    d_w_o = dot('se,sd->ed', attn_out, d_resid)
    d_attn = dot('sd,ed->se', d_resid, w_o_full).astype(BF16).reshape(n_seq, n_kv, q_per_kv, HEAD_DIM)
    d_v_states = dot('kgqs,qkgd->skd', attn_probs.astype(BF16), d_attn).astype(BF16)
    d_probs = dot('qkgd,skd->kgqs', d_attn, v_states)
    d_scores = (attn_probs * (d_probs - jnp.sum(attn_probs * d_probs, axis=-1, keepdims=True)) / math.sqrt(HEAD_DIM)).astype(BF16)
    d_q_rot = dot('kgqs,skd->qkgd', d_scores, k_states).astype(BF16).astype(F32).reshape(n_seq, n_heads, HEAD_DIM)
    d_k_rot = dot('kgqs,qkgd->skd', d_scores, q_states).astype(BF16).astype(F32)
    d_q_lin = (d_q_rot * cos_t + rotate_half_t(d_q_rot * sin_t)).reshape(n_seq, q_width)
    d_k_lin = (d_k_rot * cos_t + rotate_half_t(d_k_rot * sin_t)).reshape(n_seq, kv_width)
    d_v_lin = d_v_states.reshape(n_seq, kv_width)
    d_b_q = jnp.sum(d_q_lin, axis=0)
    d_b_k = jnp.sum(d_k_lin, axis=0)
    d_b_v = jnp.sum(d_v_lin.astype(F32), axis=0)
    d_qkv = jnp.concatenate([d_q_lin.astype(BF16), d_k_lin.astype(BF16), d_v_lin], axis=1)
    d_w_qkv = dot('sd,se->de', normed_attn, d_qkv)
    d_normed_attn = dot('se,de->sd', d_qkv, w_qkv).astype(BF16).astype(F32)
    d_hidden_norm, d_gain_a = norm_bwd(hidden, inv_attn, gain_a, d_normed_attn)
    grad_hidden = (d_resid.astype(F32) + d_hidden_norm).astype(BF16)

    g_w_o = lax.psum_scatter(d_w_o, AX, scatter_dimension=0, tiled=True)
    d_kvb = jnp.concatenate([d_b_k.reshape(N_DEV, n_b), d_b_v.reshape(N_DEV, n_b), jnp.zeros((N_DEV, rows - 2 * n_b), F32)], axis=1)
    d_small = jnp.stack([d_gain_a, d_b_q, d_gain_m, d_kvb.reshape(width)], axis=1)
    d_small = jnp.pad(d_small, ((0, 0), (0, 124)))
    g_qkv = lax.psum_scatter(jnp.concatenate([d_w_qkv, d_small], axis=1), AX, scatter_dimension=0, tiled=True)
    g_w_q = g_qkv[:, :q_width]
    g_w_k = g_qkv[:, q_width:q_width + kv_width]
    g_w_v = g_qkv[:, q_width + kv_width:n_qkv]
    g_small = g_qkv[:, n_qkv:n_qkv + 4].T
    g_kvb = g_small[3]
    return (layer_out[None], grad_hidden[None], g_small[0], g_w_q, g_small[1], g_w_k, g_kvb[:n_b], g_w_v, g_kvb[n_b:2 * n_b],
            g_w_o, g_small[2], g_w_gate, g_w_up, g_w_down)


def solution(mesh):
    act_spec = P(AX, None, None)
    mat_spec = P(AX, None)
    vec_spec = P(AX)
    param_specs = (vec_spec, mat_spec, vec_spec, mat_spec, vec_spec, mat_spec, vec_spec, mat_spec, vec_spec, mat_spec, mat_spec, mat_spec)
    in_specs_all = (act_spec, act_spec, mat_spec) + param_specs
    out_specs_all = (act_spec, act_spec) + param_specs
    return jax.shard_map(local_step, mesh=mesh, in_specs=in_specs_all, out_specs=out_specs_all, check_vma=False)
```

time: 1990 us -> 1240 us (0.62)
  waiting for transfers between devices: 1400 us -> 637 us
  local copies, waits for them, and re-layouts: 21.6 us -> 104 us
  blocking collectives: 156 us -> 76.4 us
  matrix products: 348 us -> 325 us
  other arithmetic: 41.4 us -> 63 us
    reduce_scatter x7 -> x4, waiting for transfers between devices: 982 us -> 275 us  [the longest x1 150 us: local_step(): lax.psum_scatter(out_part, AX, scatter_dimension=0, tiled=True, axis_inde...]
    all_gather x10 -> x4, waiting for transfers between devices: 411 us -> 41.7 us  [the longest x1 41.6 us: local_step(): qkv_full = lax.all_gather(qkv_loc, AX, axis=0, tiled=True)]
    ppermute x0 -> x5, waiting for transfers between devices: none -> 319 us  [z_pair(): return lax.ppermute(arr, AX, Z_PERM)]
    unnamed x3 -> x0, blocking collectives: 100 us -> none
    all_to_all x0 -> x1, blocking collectives: none -> 76.4 us  [local_step(): gu = lax.all_to_all(gu, AX, 0, 0, axis_index_groups=GROUPS, tiled=True)]
    all_gather x4 -> x0, blocking collectives: 55.7 us -> none  [gather_all(): lax.all_gather(w_shard, FSDP_AXIS, axis=0, tiled=True)]
    reshape x0 -> x12, local copies, waits for them, and re-layouts: none -> 36.7 us  [the longest x4 21.3 us: back_rows(): grad.reshape(TP, rows, 2, ff_blk).transpose(1, 2, 0, 3)]
    dot_general x27 -> x22, matrix products: 348 us -> 314 us  [dot(): return jnp.einsum(eq_form, lhs_arr, rhs_arr, preferred_element_type=F32)]
  transfers between devices with their start and end apart: 17 -> 15, of which waited for: 11 -> 7; matrix products, arithmetic and copies ran while one was open for 18% -> 24% of each run, Pallas kernels for 0% -> 0%
where the time goes in v1:
time: 1240 us; the launch traced here: 1230 us
  waiting for transfers between devices  637 us (51%)
  matrix products  325 us (26%)
  local copies, waits for them, and re-layouts  104 us (8%)
  blocking collectives  76.4 us (6%)
  other arithmetic  63 us (5%)
  starting transfers between devices  15.2 us (1%)
  between operations  14.9 us (1%)
    ppermute x5, waiting for transfers between devices, z_pair(): return lax.ppermute(arr, AX, Z_PERM)  319 us
    dot_general x22, matrix products, dot(): return jnp.einsum(eq_form, lhs_arr, rhs_arr, preferred_element_type=F32)  314 us
    reduce_scatter x1, waiting for transfers between devices, local_step(): lax.psum_scatter(out_part, AX, scatter_dimension=0, tiled=True, axis_inde...  150 us
    reduce_scatter x1, waiting for transfers between devices, local_step(): lax.psum_scatter(dn_part, AX, scatter_dimension=0, tiled=True, axis_index...  125 us
    all_to_all x1, blocking collectives, local_step(): gu = lax.all_to_all(gu, AX, 0, 0, axis_index_groups=GROUPS, tiled=True)  76.4 us
    all_gather x1, waiting for transfers between devices, local_step(): qkv_full = lax.all_gather(qkv_loc, AX, axis=0, tiled=True)  41.6 us
  transfers between devices with their start and end apart: 15, of which 7 were waited for; matrix products, arithmetic and copies ran while one was open for 24% of the time, Pallas kernels for 0%

profile of v1, /device:TPU:0, one launch (start us, length us, event | category | flops | bytes accessed | tf_op | source)
XLA Modules:
  0.0 1234.6 jit_solution(5263535476507295028)
XLA Ops:
  15.2 41.6 %all-gather.6.cloned.1.call-done = bf16[1536,2176]{1,0:T(8,128)(2,1)} async-done(((bf16[96,2176]{1,0:T(8,128)(2,1)}), bf16[1536,2176]{1,0:T(8,128)(2,1)}) %all-gather.6.cloned.1.call-update) | async-done | bytes 6684688 | tf_op jit(solution)/shard_map/all_gather | solution.py:77
  59.7 5.6 fusion.72
  65.4 2.0 slice.151
  68.9 2.5 copy.105
  71.4 2.0 copy.146
  76.3 2.0 fusion.109
  79.2 2.0 fusion.64
  81.3 10.7 fusion.139
  92.0 5.9 fusion.83
  97.9 5.8 fusion.57
  107.1 4.2 stack.41
  111.3 2.8 copy.111
  114.1 3.9 stack.42
  119.5 7.6 maximum_bitcast_fusion
  127.2 7.8 reshape.224
  135.0 76.4 %all_to_all.15 = bf16[8,192,1120]{2,1,0:T(8,128)(2,1)S(1)} all-to-all(bf16[8,192,1120]{2,1,0:T(8,128)(2,1)S(1)} %reshape.224), channel_id=1, replica_groups={{0,1,2,3,4,5,6,7},{8,9,10,11,12,13,14,15}}, dimensions={0} | all-to-all | bytes 6881280 | tf_op jit(solution)/shard_map/all_to_all | solution.py:91
  211.7 3.5 copy.114
  217.2 110.8 %collective-permute-done.1 = bf16[560,1536]{1,0:T(8,128)(2,1)} collective-permute-done((bf16[560,1536]{1,0:T(8,128)(2,1)}, bf16[560,1536]{1,0:T(8,128)(2,1)}, u32[]{:S(2)}, u32[]{:S(2)}) %collective-permute-start.1) | collective-permute-done | bytes 1720352 | tf_op jit(solution)/shard_map/ppermute | solution.py:55
  328.0 4.0 broadcast_select_fusion.3
  332.0 5.7 copy.115
  337.7 2.6 broadcast_select_fusion.1
  340.3 2.3 slice_bitcast_fusion.2
  342.7 22.0 %fusion.81 = f32[4096,1120]{0,1:T(8,128)} fusion(bf16[4096,1536]{1,0:T(8,128)(2,1)} %all-gather.10.cloned.1.call-done, bf16[768,1120]{1,0:T(8,128)(2,1)} %get-tuple-element.34, bf16[768,1120]{1,0:T(8,128)(2,1)} %get-tuple-element.66), kind=kOutput, calls=%fused_computation.108 | convolution fusion | flops 14099742720 | bytes 34373632 | tf_op jit(solution)/shard_map/sd,df->sf/dot_general | solution.py:20
  364.6 21.1 %fusion.79 = f32[4096,1120]{0,1:T(8,128)} fusion(bf16[4096,1536]{1,0:T(8,128)(2,1)} %all-gather.10.cloned.1.call-done, bf16[768,1120]{1,0:T(8,128)(2,1)S(1)} %get-tuple-element.35, bf16[768,1120]{1,0:T(8,128)(2,1)S(1)} %get-tuple-element.65), kind=kOutput, calls=%fused_computation.106 | convolution fusion | flops 14099742720 | bytes 34373632 | tf_op jit(solution)/shard_map/sd,df->sf/dot_general | solution.py:20
  385.8 33.1 %fusion.4 = (bf16[4096,1120]{0,1:T(8,128)(2,1)}, bf16[4096,1120]{0,1:T(8,128)(2,1)}, bf16[4096,1120]{0,1:T(8,128)(2,1)}) fusion(f32[4096,1120]{0,1:T(8,128)} %fusion.79, f32[4096,1120]{0,1:T(8,128)} %fusion.81, bf16[1,4096,1536]{2,1,0:T(8,128)(2,1)} %all-gather.12.cloned.1.call-done, bf16[560,1536]{1,0:T(8,128)(2,1)} %get-tuple-element.37, ...), kind=kOutput, calls=%fused_computation.6 | convolution fusion | flops 14182318080 | bytes 80248832 | tf_op jit(solution)/shard_map/sd,fd->sf/dot_general | solution.py:20
  418.9 22.8 %fusion.80 = f32[4096,1536]{1,0:T(8,128)} fusion(bf16[4096,1120]{0,1:T(8,128)(2,1)} %get-tuple-element.27, bf16[768,1120]{1,0:T(8,128)(2,1)} %get-tuple-element.34, bf16[768,1120]{1,0:T(8,128)(2,1)} %get-tuple-element.66), kind=kOutput, calls=%fused_computation.107 | convolution fusion | flops 14099742720 | bytes 37781504 | tf_op jit(solution)/shard_map/sf,df->sd/dot_general | solution.py:20
  441.7 28.1 %convolution_add_fusion = f32[4096,1536]{1,0:T(8,128)} fusion(f32[4096,1536]{1,0:T(8,128)} %fusion.80, bf16[4096,1120]{0,1:T(8,128)(2,1)} %get-tuple-element.29, bf16[768,1120]{1,0:T(8,128)(2,1)S(1)} %get-tuple-element.35, bf16[768,1120]{1,0:T(8,128)(2,1)S(1)} %get-tuple-element.65), kind=kOutput, calls=%fused_computation.11 | convolution fusion | flops 14106034176 | bytes 62947328 | tf_op jit(solution)/shard_map/sf,df->sd/dot_general | solution.py:20
  471.7 21.8 %fusion.82 = f32[4096,1536]{1,0:T(8,128)} fusion(bf16[4096,1120]{0,1:T(8,128)(2,1)} %get-tuple-element.28, bf16[560,1536]{1,0:T(8,128)(2,1)S(1)} %copy-done.18, bf16[560,1536]{1,0:T(8,128)(2,1)S(1)} %copy-done.17), kind=kOutput, calls=%fused_computation.109 | convolution fusion | flops 14099742720 | bytes 37781504 | tf_op jit(solution)/shard_map/sf,fd->sd/dot_general | solution.py:20
  493.7 124.6 %reduce-scatter.7.cloned.1.call-done = f32[512,1536]{1,0:T(8,128)} async-done(((f32[4096,1536]{1,0:T(8,128)}), f32[512,1536]{1,0:T(8,128)}) %reduce-scatter.7.cloned.1.call-update) | async-done | bytes 3145744 | tf_op jit(solution)/shard_map/reduce_scatter | solution.py:127
  618.3 2.7 fusion.56
  621.1 149.9 %reduce-scatter.5.cloned.1.call-done = f32[512,1536]{1,0:T(8,128)} async-done(((f32[4096,1536]{1,0:T(8,128)}), f32[512,1536]{1,0:T(8,128)}) %reduce-scatter.5.cloned.1.call-update) | async-done | bytes 3145744 | tf_op jit(solution)/shard_map/reduce_scatter | solution.py:131
  771.0 5.2 fusion.53
  777.3 5.0 convolution_convert_fusion.1
  784.2 6.3 fusion.113
  790.5 17.7 %fusion.87 = f32[2,128,6,512]{3,1,2,0:T(8,128)S(1)} fusion(bf16[512,2,128,1]{0,2,3,1:T(8,128)(2,1)} %fusion.109, f32[2,512,512,6]{2,1,3,0:T(8,128)} %fusion.113, f32[2,6,512,512]{2,3,1,0:T(8,128)} %get-tuple-element.57, f32[2,6,512]{2,1,0:T(8,128)S(1)} %copy-done.35), kind=kOutput, calls=%fused_computation.119 | convolution fusion | flops 828905984 | bytes 28598272 | tf_op jit(solution)/shard_map/kgqs,skd->qkgd/dot_general | solution.py:20
  808.2 19.2 %broadcast_multiply_fusion = (f32[512,2,128]{0,2,1:T(8,128)}, f32[512,2,128]{0,2,1:T(8,128)}) fusion(f32[512,128]{0,1:T(8,128)S(1)} %copy-done.16, bf16[512,2,6,128]{0,3,2,1:T(8,128)(2,1)} %fusion.64, f32[2,512,512,6]{2,1,3,0:T(8,128)} %fusion.113, f32[2,6,512,512]{2,3,1,0:T(8,128)} %get-tuple-element.57, f32[2,6,512]{2,1,0:T(8,128)S(1)} %copy-done.35), kind=kOutput, calls=%fused_computation.153 | convolution fusion | flops 827726336 | bytes 28073984 | tf_op jit(solution)/shard_map/kgqs,qkgd->skd/dot_general | solution.py:20
  827.3 8.0 convert_reduce_fusion
  837.1 2.1 fusion.67
  842.3 10.3 fusion.102
  852.6 8.5 fusion.61
  861.5 10.7 select_maximum_fusion
  872.3 11.7 fusion.24
  885.4 12.9 %fusion.22 = f32[768,1120]{0,1:T(8,128)} fusion(bf16[4096,1120]{0,1:T(8,128)(2,1)} %get-tuple-element.27, bf16[4096,1536]{1,0:T(8,128)(2,1)} %all-gather.10.cloned.1.call-done, s32[]{:T(128)S(6)} %select_n.54), kind=kOutput, calls=%fused_computation.35 | convolution fusion | flops 7046430720 | bytes 18907140 | tf_op jit(solution)/shard_map/sd,sf->df/dot_general | solution.py:20
  899.0 5.1 fusion.140
  904.1 94.0 %collective-permute-done.3 = f32[768,1120]{0,1:T(8,128)} collective-permute-done((f32[768,1120]{0,1:T(8,128)S(1)}, f32[768,1120]{0,1:T(8,128)}, u32[]{:S(2)}, u32[]{:S(2)}) %collective-permute-start.3) | collective-permute-done | bytes 3440672 | tf_op jit(solution)/shard_map/ppermute | solution.py:55
  998.0 12.2 fusion.40
  1010.3 3.1 copy.126
  1013.4 3.8 all-to-all-start.2
  1017.2 17.7 %fusion.10 = f32[1120,1536]{1,0:T(8,128)S(1)} fusion(bf16[4096,1120]{0,1:T(8,128)(2,1)} %get-tuple-element.28, bf16[1,4096,1536]{2,1,0:T(8,128)(2,1)} %all-gather.12.cloned.1.call-done), kind=kOutput, calls=%fused_computation.20 | convolution fusion | flops 14092861440 | bytes 28639232 | tf_op jit(solution)/shard_map/sf,sd->fd/dot_general | solution.py:20
  1035.0 2.2 constant_dynamic-slice_fusion
  1038.8 2.5 collective-permute-start.4
  1041.3 55.1 %collective-permute-done.2 = f32[768,1120]{0,1:T(8,128)} collective-permute-done((f32[768,1120]{0,1:T(8,128)}, f32[768,1120]{0,1:T(8,128)}, u32[]{:S(2)}, u32[]{:S(2)}) %collective-permute-start.2) | collective-permute-done | bytes 3440672 | tf_op jit(solution)/shard_map/ppermute | solution.py:55
  1096.4 13.3 %fusion.43 = f32[768,1120]{0,1:T(8,128)} fusion(f32[768,1120]{0,1:T(8,128)} %collective-permute-done.2, bf16[4096,1120]{0,1:T(8,128)(2,1)} %get-tuple-element.27, bf16[4096,1536]{1,0:T(8,128)(2,1)} %all-gather.10.cloned.1.call-done, s32[]{:T(128)S(6)} %select_n.53), kind=kOutput, calls=%fused_computation.60 | convolution fusion | flops 7047290880 | bytes 22347780 | tf_op jit(solution)/shard_map/sd,sf->df/dot_general | solution.py:20
  1109.7 5.2 copy.124
  1114.9 4.5 all-to-all-start.1
  1119.4 59.3 %collective-permute-done.4 = f32[560,1536]{1,0:T(8,128)} collective-permute-done((f32[560,1536]{1,0:T(8,128)}, f32[560,1536]{1,0:T(8,128)}, u32[]{:S(2)}, u32[]{:S(2)}) %collective-permute-start.4) | collective-permute-done | bytes 3440672 | tf_op jit(solution)/shard_map/ppermute | solution.py:55
  1178.7 5.4 dynamic-slice_add_fusion
  1184.1 4.1 reshape.237
  1188.2 6.4 copy.127
  1194.5 5.6 reshape.238
  1200.1 5.9 reshape.234
  1206.0 6.4 copy.125
  1212.4 5.7 reshape.235
  1218.2 3.6 fusion.89
  (153 shorter events, 43.2 us)
Async XLA Ops:
  7.2 7.6 copy-start.11
  7.2 49.6 %all-gather.6.cloned.1.call-start = ((), (), s32[]{:S(2)}) async-start(), calls=%async_computation.7 | async-start | bytes 7102464 | tf_op jit(solution)/shard_map/all_gather | solution.py:77
  10.8 87.1 %all-gather.8.cloned.1.call-start = ((), (), s32[]{:S(2)}) async-start(), calls=%async_computation.8 | async-start | bytes 5013504 | tf_op jit(solution)/shard_map/all_gather | solution.py:87
  11.5 331.1 %all-gather.10.cloned.1.call-start = ((), (), s32[]{:S(2)}) async-start(), calls=%async_computation.9 | async-start | bytes 14155776 | tf_op jit(solution)/shard_map/all_gather | solution.py:118
  14.8 63.8 %copy-start.2 = (f32[512,128]{0,1:T(8,128)}, f32[512,128]{0,1:T(8,128)S(1)}, u32[]{:S(2)}) copy-start(f32[512,128]{0,1:T(8,128)S(1)} %get-tuple-element.52) | copy-start | bytes 786436
  15.2 50.2 %copy-start.29 = (f32[512]{0:T(512)}, f32[512]{0:T(512)S(1)}, u32[]{:S(2)}) copy-start(f32[512]{0:T(512)S(1)} %add_rsqrt_fusion.1) | copy-start | bytes 6148
  59.4 6.0 copy-start.25
  59.4 44.4 %copy-start.23 = (f32[1536]{0:T(1024)}, f32[1536]{0:T(1024)S(1)}, u32[]{:S(2)}) copy-start(f32[1536]{0:T(1024)S(1)} %get-tuple-element.18) | copy-start | bytes 18436
  78.3 0.9 copy-start.15
  81.2 10.7 copy-start.20
  91.9 5.9 copy-start.34
  92.0 5.9 copy-start.12
  97.9 5.8 copy-start.31
  103.7 1.1 copy-start
  103.7 1.1 copy-start.27
  106.5 279.3 %all-gather.12.cloned.1.call-start = ((), (), s32[]{:S(2)}) async-start(), calls=%async_computation.14 | async-start | bytes 14155776 | tf_op jit(solution)/shard_map/all_gather | solution.py:101
  107.1 511.3 %reduce-scatter.7.cloned.1.call-start = ((), (), s32[]{:S(2)}) async-start(), calls=%async_computation.11 | async-start | bytes 28311552 | tf_op jit(solution)/shard_map/reduce_scatter | solution.py:127
  118.0 1.5 copy-start.4
  215.2 116.8 %collective-permute-start = (bf16[2,768,1120]{1,2,0:T(8,128)(2,1)}, bf16[2,768,1120]{1,2,0:T(8,128)(2,1)}, u32[]{:S(2)}, u32[]{:S(2)}) collective-permute-start(bf16[2,768,1120]{1,2,0:T(8,128)(2,1)} %copy.114), channel_id=1, source_target_pairs={{0,8},{1,9},{2,10},{3,11},{4,12},{5,13},{6,14},{7,15},{8,0},{9,1},... | collective-permute-start | bytes 10321928 | tf_op jit(solution)/shard_map/ppermute | solution.py:55
  216.7 111.3 %collective-permute-start.1 = (bf16[560,1536]{1,0:T(8,128)(2,1)}, bf16[560,1536]{1,0:T(8,128)(2,1)}, u32[]{:S(2)}, u32[]{:S(2)}) collective-permute-start(bf16[560,1536]{1,0:T(8,128)(2,1)} %param.29), channel_id=1, source_target_pairs={{0,8},{1,9},{2,10},{3,11},{4,12},{5,13},{6,14},{7,15},{8,0},{9,1},... | collective-permute-start | bytes 5160968 | tf_op jit(solution)/shard_map/ppermute | solution.py:55
  469.7 1.5 copy-start.17
  469.7 2.0 copy-start.18
  469.8 301.3 %reduce-scatter.5.cloned.1.call-start = ((), (), s32[]{:S(2)}) async-start(), calls=%async_computation.10 | async-start | bytes 28311552 | tf_op jit(solution)/shard_map/reduce_scatter | solution.py:131
  493.5 124.8 %copy-start.1 = (bf16[512,1536]{1,0:T(8,128)(2,1)S(1)}, bf16[512,1536]{1,0:T(8,128)(2,1)}, u32[]{:S(2)}) copy-start(bf16[512,1536]{1,0:T(8,128)(2,1)} %copy-done) | copy-start | bytes 4718596
  493.5 124.8 %copy-start.24 = (f32[1536]{0:T(1024)S(1)}, f32[1536]{0:T(1024)}, u32[]{:S(2)}) copy-start(f32[1536]{0:T(1024)} %copy-done.23) | copy-start | bytes 18436
  493.5 124.8 %copy-start.28 = (f32[512]{0:T(512)S(1)}, f32[512]{0:T(512)}, u32[]{:S(2)}) copy-start(f32[512]{0:T(512)} %copy-done.27) | copy-start | bytes 6148
  493.6 277.4 %copy-start.6 = (bf16[1,512,1536]{2,1,0:T(8,128)(2,1)S(1)}, bf16[1,512,1536]{2,1,0:T(8,128)(2,1)}, u32[]{:S(2)}) copy-start(bf16[1,512,1536]{2,1,0:T(8,128)(2,1)} %param.16) | copy-start | bytes 4718596
  493.6 728.2 %reduce-scatter.9.cloned.1.call-start = ((), (), s32[]{:S(2)}) async-start(), calls=%async_computation.12 | async-start | bytes 14204928 | tf_op jit(solution)/shard_map/reduce_scatter | solution.py:175
  776.2 1.1 copy-start.7
  777.3 6.9 copy-start.21
  783.0 1.1 copy-start.10
  784.2 6.3 copy-start.35
  790.5 17.7 %copy-start.16 = (f32[512,128]{0,1:T(8,128)S(1)}, f32[512,128]{0,1:T(8,128)}, u32[]{:S(2)}) copy-start(f32[512,128]{0,1:T(8,128)} %get-tuple-element.53) | copy-start | bytes 786436
  836.1 1.0 copy-start.3
  837.1 2.1 copy-start.22
  840.0 2.3 copy-start.26
  840.0 2.3 copy-start.30
  842.2 10.4 copy-start.13
  842.2 10.4 copy-start.19
  842.3 10.3 copy-start.33
  872.2 355.3 %reduce-scatter.11.cloned.1.call-start = ((), (), s32[]{:S(2)}) async-start(), calls=%async_computation.13 | async-start | bytes 10027008 | tf_op jit(solution)/shard_map/reduce_scatter | solution.py:171
  884.0 114.1 %collective-permute-start.3 = (f32[768,1120]{0,1:T(8,128)S(1)}, f32[768,1120]{0,1:T(8,128)}, u32[]{:S(2)}, u32[]{:S(2)}) collective-permute-start(f32[768,1120]{0,1:T(8,128)S(1)} %fusion.24), channel_id=1, source_target_pairs={{0,8},{1,9},{2,10},{3,11},{4,12},{5,13},{6,14},{7,15},{8,0},{9,1},... | collective-permute-start | bytes 10321928 | tf_op jit(solution)/shard_map/ppermute | solution.py:55
  885.4 13.5 %copy-start.8 = (bf16[512,1536]{1,0:T(8,128)(2,1)S(1)}, bf16[512,1536]{1,0:T(8,128)(2,1)}, u32[]{:S(2)}) copy-start(bf16[512,1536]{1,0:T(8,128)(2,1)} %copy-done.7) | copy-start | bytes 4718596
  885.4 13.5 %copy-start.32 = (bf16[2,128,6,512]{3,1,2,0:T(8,128)(2,1)S(1)}, bf16[2,128,6,512]{3,1,2,0:T(8,128)(2,1)}, u32[]{:S(2)}) copy-start(bf16[2,128,6,512]{3,1,2,0:T(8,128)(2,1)} %copy-done.31) | copy-start | bytes 4718596
  898.4 198.0 %collective-permute-start.2 = (f32[768,1120]{0,1:T(8,128)}, f32[768,1120]{0,1:T(8,128)}, u32[]{:S(2)}, u32[]{:S(2)}) collective-permute-start(f32[768,1120]{0,1:T(8,128)} %fusion.22), channel_id=1, source_target_pairs={{0,8},{1,9},{2,10},{3,11},{4,12},{5,13},{6,14},{7,15},{8,0},{9,1},... | collective-permute-start | bytes 10321928 | tf_op jit(solution)/shard_map/ppermute | solution.py:55
  1013.4 101.5 %all-to-all-start.2 = ((f32[8,96,1120]{2,1,0:T(8,128)}), f32[8,96,1120]{2,1,0:T(8,128)S(1)}, u32[]{:S(2)}, u32[]{:S(2)}) async-start(f32[8,96,1120]{2,1,0:T(8,128)} %bitcast.222), calls=%async_computation.6 | async-start | bytes 7077888 | tf_op jit(solution)/shard_map/all_to_all | solution.py:144
  1035.0 3.8 copy-start.5
  1038.8 139.9 %collective-permute-start.4 = (f32[560,1536]{1,0:T(8,128)}, f32[560,1536]{1,0:T(8,128)}, u32[]{:S(2)}, u32[]{:S(2)}) collective-permute-start(f32[560,1536]{1,0:T(8,128)} %constant_dynamic-slice_fusion), channel_id=1, source_target_pairs={{0,8},{1,9},{2,10},{3,11},{4,12},{5,13},{6,14},{7,15},{8,0},{9,1},... | collective-permute-start | bytes 10321928 | tf_op jit(solution)/shard_map/ppermute | solution.py:55
  1114.9 85.2 %all-to-all-start.1 = ((f32[8,96,1120]{2,1,0:T(8,128)}), f32[8,96,1120]{2,1,0:T(8,128)}, u32[]{:S(2)}, u32[]{:S(2)}) async-start(f32[8,96,1120]{2,1,0:T(8,128)} %bitcast.221), calls=%async_computation.5 | async-start | bytes 7077888 | tf_op jit(solution)/shard_map/all_to_all | solution.py:144
  1212.4 5.7 copy-start.9
  1212.4 5.7 copy-start.14
Sparse Core Ops, SparseCore 0:
  10.9 45.8 all-gather.5
  59.0 36.6 all-gather.7
  106.6 104.6 all-gather.9
  213.0 69.5 all-gather.11
  469.9 148.4 reduce-scatter.6
  621.8 149.2 reduce-scatter.4
  872.4 137.3 reduce-scatter.8
  1015.0 109.9 reduce-scatter.10

commit v2 on v1

v2 whole, which is shorter than its diff:
```python
import math
import jax
import jax.numpy as jnp
from jax import lax
from jax.experimental import pallas as pl
from jax.experimental.pallas import tpu as pltpu
from jax.sharding import PartitionSpec as P

HEAD_DIM = 128
NORM_EPS = 1e-6
ROPE_THETA = 1000000.0
AX = 'fsdp'
N_DEV = 16
TP = 8
GROUPS = [list(range(0, 8)), list(range(8, 16))]
Z_PERM = [(i, i ^ 8) for i in range(N_DEV)]
F32 = jnp.float32
BF16 = jnp.bfloat16
CHUNKS = 2


def dot(eq_form, lhs_arr, rhs_arr):
    return jnp.einsum(eq_form, lhs_arr, rhs_arr, preferred_element_type=F32)


def rope_tables(positions):
    inv_freq = 1.0 / jnp.power(ROPE_THETA, jnp.arange(0, HEAD_DIM, 2).astype(F32) / HEAD_DIM)
    angles = positions.astype(F32)[:, None] * inv_freq
    cos_h, sin_h = jnp.cos(angles), jnp.sin(angles)
    return jnp.concatenate([cos_h, cos_h], axis=-1), jnp.concatenate([-sin_h, sin_h], axis=-1)


def rope(vec, cos_t, sin_t):
    return vec * cos_t + pltpu.roll(vec, HEAD_DIM // 2, 1) * sin_t


def rope_t(vec, cos_t, sin_t):
    return vec * cos_t - pltpu.roll(vec, HEAD_DIM // 2, 1) * sin_t


def dot_nt(lhs, rhs):
    return lax.dot_general(lhs, rhs, (((1,), (1,)), ((), ())), preferred_element_type=F32)


def dot_nn(lhs, rhs):
    return lax.dot_general(lhs, rhs, (((1,), (0,)), ((), ())), preferred_element_type=F32)


def dot_tn(lhs, rhs):
    return lax.dot_general(lhs, rhs, (((0,), (0,)), ((), ())), preferred_element_type=F32)


SCALE = 1.0 / math.sqrt(HEAD_DIM)


def attn_fwd_kernel(q_ref, k_ref, v_ref, cos_ref, sin_ref, o_ref):
    cos_t, sin_t = cos_ref[...], sin_ref[...]
    q_rot = rope(q_ref[...], cos_t, sin_t).astype(BF16)
    k_rot = rope(k_ref[...], cos_t, sin_t).astype(BF16)
    scores = dot_nt(q_rot, k_rot) * SCALE
    keep = lax.broadcasted_iota(jnp.int32, scores.shape, 0) >= lax.broadcasted_iota(jnp.int32, scores.shape, 1)
    scores = jnp.where(keep, scores, -1e30)
    probs = jnp.exp(scores - jnp.max(scores, axis=1, keepdims=True))
    probs = probs * (1.0 / jnp.sum(probs, axis=1, keepdims=True))
    o_ref[...] = dot_nn(probs.astype(BF16), v_ref[...].astype(BF16)).astype(BF16)


def attn_fwd(qkv, cos_t, sin_t, n_heads, n_kv):
    n_seq = qkv.shape[0]
    group = n_heads // n_kv
    tab = pl.BlockSpec((n_seq, HEAD_DIM), lambda h: (0, 0))
    return pl.pallas_call(
        attn_fwd_kernel,
        grid=(n_heads,),
        in_specs=[
            pl.BlockSpec((n_seq, HEAD_DIM), lambda h: (0, h)),
            pl.BlockSpec((n_seq, HEAD_DIM), lambda h: (0, n_heads + h // group)),
            pl.BlockSpec((n_seq, HEAD_DIM), lambda h: (0, n_heads + n_kv + h // group)),
            tab, tab,
        ],
        out_specs=pl.BlockSpec((n_seq, HEAD_DIM), lambda h: (0, h)),
        out_shape=jax.ShapeDtypeStruct((n_seq, n_heads * HEAD_DIM), BF16),
        compiler_params=pltpu.CompilerParams(vmem_limit_bytes=40 << 20),
        cost_estimate=pl.CostEstimate(flops=8 << 30, bytes_accessed=6 << 20, transcendentals=3 << 20),
        name='attn_fwd',
    )(qkv, qkv, qkv, cos_t, sin_t)


def attn_bwd_kernel(q_ref, k_ref, v_ref, do_ref, cos_ref, sin_ref, dq_ref, dk_ref, dv_ref, bq_ref, bk_ref, bv_ref, dk_acc, dv_acc):
    step = pl.program_id(1)
    cos_t, sin_t = cos_ref[...], sin_ref[...]
    q_rot = rope(q_ref[...], cos_t, sin_t).astype(BF16)
    k_rot = rope(k_ref[...], cos_t, sin_t).astype(BF16)
    v_st = v_ref[...].astype(BF16)
    d_out = do_ref[...]
    scores = dot_nt(k_rot, q_rot) * SCALE
    keep = lax.broadcasted_iota(jnp.int32, scores.shape, 1) >= lax.broadcasted_iota(jnp.int32, scores.shape, 0)
    scores = jnp.where(keep, scores, -1e30)
    probs = jnp.exp(scores - jnp.max(scores, axis=0, keepdims=True))
    probs = probs * (1.0 / jnp.sum(probs, axis=0, keepdims=True))
    d_v = dot_nn(probs.astype(BF16), d_out)
    d_probs = dot_nt(v_st, d_out)
    d_sc = (probs * (d_probs - jnp.sum(probs * d_probs, axis=0, keepdims=True)) * SCALE).astype(BF16)
    d_k = dot_nn(d_sc, q_rot)
    d_q = dot_tn(d_sc, k_rot).astype(BF16).astype(F32)
    d_q = rope_t(d_q, cos_t, sin_t)
    dq_ref[...] = d_q.astype(BF16)
    bq_ref[...] = jnp.sum(d_q, axis=0, keepdims=True)

    @pl.when(step == 0)
    def _():
        dk_acc[...] = d_k
        dv_acc[...] = d_v

    @pl.when(step > 0)
    def _():
        dk_acc[...] += d_k
        dv_acc[...] += d_v

    @pl.when(step == pl.num_programs(1) - 1)
    def _():
        d_k_all = rope_t(dk_acc[...].astype(BF16).astype(F32), cos_t, sin_t)
        dk_ref[...] = d_k_all.astype(BF16)
        bk_ref[...] = jnp.sum(d_k_all, axis=0, keepdims=True)
        d_v_all = dv_acc[...].astype(BF16)
        dv_ref[...] = d_v_all
        bv_ref[...] = jnp.sum(d_v_all.astype(F32), axis=0, keepdims=True)


def attn_bwd(qkv, d_attn, cos_t, sin_t, n_heads, n_kv):
    n_seq = qkv.shape[0]
    group = n_heads // n_kv
    tab = pl.BlockSpec((n_seq, HEAD_DIM), lambda j, g: (0, 0))
    blk_h = pl.BlockSpec((n_seq, HEAD_DIM), lambda j, g: (0, j * group + g))
    blk_kv = pl.BlockSpec((n_seq, HEAD_DIM), lambda j, g: (0, j))
    vec_h = pl.BlockSpec((1, HEAD_DIM), lambda j, g: (0, j * group + g))
    vec_kv = pl.BlockSpec((1, HEAD_DIM), lambda j, g: (0, j))
    q_width, kv_width = n_heads * HEAD_DIM, n_kv * HEAD_DIM
    return pl.pallas_call(
        attn_bwd_kernel,
        grid=(n_kv, group),
        in_specs=[
            blk_h,
            pl.BlockSpec((n_seq, HEAD_DIM), lambda j, g: (0, n_heads + j)),
            pl.BlockSpec((n_seq, HEAD_DIM), lambda j, g: (0, n_heads + n_kv + j)),
            blk_h, tab, tab,
        ],
        out_specs=[blk_h, blk_kv, blk_kv, vec_h, vec_kv, vec_kv],
        out_shape=[
            jax.ShapeDtypeStruct((n_seq, q_width), BF16),
            jax.ShapeDtypeStruct((n_seq, kv_width), BF16),
            jax.ShapeDtypeStruct((n_seq, kv_width), BF16),
            jax.ShapeDtypeStruct((1, q_width), F32),
            jax.ShapeDtypeStruct((1, kv_width), F32),
            jax.ShapeDtypeStruct((1, kv_width), F32),
        ],
        scratch_shapes=[pltpu.VMEM((n_seq, HEAD_DIM), F32), pltpu.VMEM((n_seq, HEAD_DIM), F32)],
        compiler_params=pltpu.CompilerParams(vmem_limit_bytes=40 << 20),
        cost_estimate=pl.CostEstimate(flops=16 << 30, bytes_accessed=10 << 20, transcendentals=3 << 20),
        name='attn_bwd',
    )(qkv, qkv, qkv, d_attn, cos_t, sin_t)


GRAD_BLK = 256


def attn_grads_kernel(n_o, n_all, lhs_o_ref, lhs_h_ref, rhs_o_ref, rhs_h_ref, small_ref, out_ref):
    step = pl.program_id(0)

    @pl.when(step < n_o)
    def _():
        out_ref[...] = dot_nn(lhs_o_ref[...], rhs_o_ref[...])

    @pl.when(jnp.logical_and(step >= n_o, step < n_all))
    def _():
        out_ref[...] = dot_nn(lhs_h_ref[...], rhs_h_ref[...])

    @pl.when(step == n_all)
    def _():
        out_ref[...] = small_ref[...]


def attn_grads(lhs_o, rhs_o, lhs_h, rhs_h, small):
    width, n_seq = lhs_o.shape
    n_o, n_h = rhs_o.shape[1] // GRAD_BLK, rhs_h.shape[1] // GRAD_BLK
    n_all = n_o + n_h
    full = pl.BlockSpec((width, n_seq), lambda j: (0, 0))
    return pl.pallas_call(
        lambda *refs: attn_grads_kernel(n_o, n_all, *refs),
        grid=(n_all + 1,),
        in_specs=[
            full, full,
            pl.BlockSpec((n_seq, GRAD_BLK), lambda j: (0, jnp.minimum(j, n_o - 1))),
            pl.BlockSpec((n_seq, GRAD_BLK), lambda j: (0, jnp.clip(j - n_o, 0, n_h - 1))),
            pl.BlockSpec((width, GRAD_BLK), lambda j: (0, 0)),
        ],
        out_specs=pl.BlockSpec((width, GRAD_BLK), lambda j: (0, j)),
        out_shape=jax.ShapeDtypeStruct((width, (n_all + 1) * GRAD_BLK), F32),
        compiler_params=pltpu.CompilerParams(vmem_limit_bytes=40 << 20),
        cost_estimate=pl.CostEstimate(flops=12 << 30, bytes_accessed=32 << 20, transcendentals=0),
        name='attn_grads',
    )(lhs_o, lhs_h, rhs_o, rhs_h, small)


def norm_fwd(hidden, gain_vec):
    x_f32 = hidden.astype(F32)
    inv_rms = lax.rsqrt(jnp.mean(x_f32 * x_f32, axis=-1, keepdims=True) + NORM_EPS)
    return (x_f32 * inv_rms * gain_vec).astype(BF16), inv_rms


def norm_bwd(hidden, inv_rms, gain_vec, d_normed):
    unit_rows = hidden.astype(F32) * inv_rms
    d_gain = jnp.sum(d_normed * unit_rows, axis=0)
    d_unit = d_normed * gain_vec
    d_hidden = inv_rms * (d_unit - unit_rows * jnp.mean(d_unit * unit_rows, axis=-1, keepdims=True))
    return d_hidden, d_gain


def z_pair(arr):
    return lax.ppermute(arr, AX, Z_PERM)


barrier = lax.optimization_barrier


def group_gather(arr):
    return lax.all_gather(arr, AX, axis=0, tiled=True, axis_index_groups=GROUPS)


def group_scatter(arr):
    return lax.psum_scatter(arr, AX, scatter_dimension=0, tiled=True, axis_index_groups=GROUPS)


def local_step(hidden, grad_out, positions, gain_attn, w_q, b_q, w_k, b_k, w_v, b_v, w_o, gain_mlp, w_gate, w_up, w_down):
    n_seq, width = hidden.shape[1], hidden.shape[2]
    rows = w_q.shape[0]
    q_width, kv_width = w_q.shape[1], w_k.shape[1]
    n_heads, n_kv = q_width // HEAD_DIM, kv_width // HEAD_DIM
    ff_blk = w_down.shape[0]
    ff_loc = 2 * ff_blk
    half = width // 2
    dev = lax.axis_index(AX)
    z_idx, rank = dev // TP, dev % TP
    z_zero = z_idx == 0
    hidden = hidden[0]
    grad_out = grad_out[0]

    kvb = jnp.concatenate([b_k, b_v, jnp.zeros((rows - 2 * b_k.shape[0],), BF16)])
    small = jnp.stack([gain_attn, b_q, gain_mlp, kvb], axis=1)
    small = jnp.pad(small, ((0, 0), (0, 124)))
    qkv_loc = jnp.concatenate([w_q, w_k, w_v, small], axis=1)
    qkv_full = lax.all_gather(qkv_loc, AX, axis=0, tiled=True)
    n_qkv = q_width + 2 * kv_width
    w_o_full = lax.all_gather(w_o, AX, axis=0, tiled=True)
    down_other = z_pair(w_down)

    gu = jnp.stack([w_gate, w_up], axis=0).reshape(2, rows, 2, TP, ff_blk)
    gu = gu.transpose(3, 0, 1, 2, 4).reshape(TP, 2, rows, ff_loc)
    gu, hidden = barrier((gu, hidden))
    gu_rows = jnp.zeros((2, TP, rows, ff_loc), BF16)
    for d in range(TP):
        piece = lax.dynamic_index_in_dim(gu, rank ^ d, 0, keepdims=False)
        if d:
            piece = lax.ppermute(piece, AX, [(i, i ^ d) for i in range(N_DEV)])
        gu_rows = lax.dynamic_update_slice(gu_rows, piece[:, None], (0, rank ^ d, 0, 0))
    gu_rows = gu_rows.reshape(2, half, ff_loc)

    w_qkv = qkv_full[:, :n_qkv]
    small_t = qkv_full[:, n_qkv:n_qkv + 4].T.astype(F32)
    gain_a, bias_q, gain_m = small_t[0], small_t[1], small_t[2]
    kvb_full = small_t[3].reshape(N_DEV, rows)
    n_b = b_k.shape[0]
    bias = jnp.concatenate([bias_q, kvb_full[:, :n_b].reshape(kv_width), kvb_full[:, n_b:2 * n_b].reshape(kv_width)])
    cos_t, sin_t = rope_tables(positions[0])
    normed_attn, inv_attn = norm_fwd(hidden, gain_a)
    qkv = dot('sd,de->se', normed_attn, w_qkv) + bias
    qkv, gu_rows = barrier((qkv, gu_rows))
    gu_other = z_pair(gu_rows)
    attn_out = attn_fwd(qkv, cos_t, sin_t, n_heads, n_kv)
    resid_mid = (hidden.astype(F32) + dot('se,ed->sd', attn_out, w_o_full)).astype(BF16)
    normed_mlp, inv_mlp = norm_fwd(resid_mid, gain_m)
    normed_mlp, grad_out = barrier((normed_mlp, grad_out))

    n_ch = n_seq // CHUNKS
    h_all = [group_gather(normed_mlp[c * n_ch:(c + 1) * n_ch]) for c in range(CHUNKS)]
    go_all = [group_gather(grad_out[c * n_ch:(c + 1) * n_ch]) for c in range(CHUNKS)]

    gu_lo = jnp.where(z_zero, gu_rows, gu_other)
    gu_hi = jnp.where(z_zero, gu_other, gu_rows)
    w_g = jnp.concatenate([gu_lo[0], gu_hi[0]], axis=0)
    w_u = jnp.concatenate([gu_lo[1], gu_hi[1]], axis=0)
    w_d = jnp.concatenate([jnp.where(z_zero, w_down, down_other), jnp.where(z_zero, down_other, w_down)], axis=0)

    pre = []
    for c in range(CHUNKS):
        gate_pre = dot('sd,df->sf', h_all[c], w_g)
        up_proj = dot('sd,df->sf', h_all[c], w_u)
        pre.append((gate_pre, up_proj))
    acts, d_gates, d_ups, dn_sums = [], [], [], []
    for c in range(CHUNKS):
        gate_pre, up_proj = pre[c]
        act = (jax.nn.silu(gate_pre) * up_proj).astype(BF16)
        d_act = dot('sd,fd->sf', go_all[c], w_d).astype(BF16).astype(F32)
        gate_sig = jax.nn.sigmoid(gate_pre)
        d_gate = (d_act * up_proj * gate_sig * (1.0 + gate_pre * (1.0 - gate_sig))).astype(BF16)
        d_up = (d_act * gate_pre * gate_sig).astype(BF16)
        dn_part = dot('sf,df->sd', d_gate, w_g) + dot('sf,df->sd', d_up, w_u)
        dn_sums.append(group_scatter(dn_part))
        acts.append(act)
        d_gates.append(d_gate)
        d_ups.append(d_up)
    dn_part, acts, d_gates, d_ups, h_all = barrier((dn_part, acts, d_gates, d_ups, h_all))

    def token_dot(eq_form, lhs_list, rhs_list):
        total = dot(eq_form, lhs_list[0], rhs_list[0])
        for lhs, rhs in zip(lhs_list[1:], rhs_list[1:]):
            total = total + dot(eq_form, lhs, rhs)
        return total

    h_send = [lax.dynamic_slice_in_dim(h, (1 - z_idx) * half, half, axis=1) for h in h_all]
    h_keep = [lax.dynamic_slice_in_dim(h, z_idx * half, half, axis=1) for h in h_all]
    gg_send = token_dot('sd,sf->df', h_send, d_gates)
    gu_send = token_dot('sd,sf->df', h_send, d_ups)
    d_wd = token_dot('sf,sd->fd', acts, go_all)
    wd_send = lax.dynamic_slice_in_dim(d_wd, (1 - z_idx) * ff_blk, ff_blk, axis=0)
    wd_keep = lax.dynamic_slice_in_dim(d_wd, z_idx * ff_blk, ff_blk, axis=0)
    gg_recv, gu_recv, wd_recv = z_pair(gg_send), z_pair(gu_send), z_pair(wd_send)
    gg_keep = token_dot('sd,sf->df', h_keep, d_gates)
    gu_keep = token_dot('sd,sf->df', h_keep, d_ups)
    out_part = [dot('sf,fd->sd', act, w_d) for act in acts]
    dn_sums, gg_keep, gu_keep, out_part, wd_keep = barrier((dn_sums, gg_keep, gu_keep, out_part, wd_keep))
    d_normed_mlp = jnp.concatenate(dn_sums, axis=0).astype(BF16).astype(F32)
    out_sum = jnp.concatenate([group_scatter(part) for part in out_part], axis=0)
    g_w_down = wd_keep + wd_recv

    def back_rows(grad):
        grad = lax.all_to_all(grad.reshape(TP, rows, ff_loc), AX, 0, 0, axis_index_groups=GROUPS, tiled=True)
        return grad.reshape(TP, rows, 2, ff_blk).transpose(1, 2, 0, 3).reshape(rows, N_DEV * ff_blk)

    g_w_gate = back_rows(gg_keep + gg_recv)
    g_w_up = back_rows(gu_keep + gu_recv)

    d_resid_norm, d_gain_m = norm_bwd(resid_mid, inv_mlp, gain_m, d_normed_mlp)
    d_resid = (grad_out.astype(F32) + d_resid_norm).astype(BF16)
    d_attn = dot('sd,ed->se', d_resid, w_o_full).astype(BF16)
    d_q, d_k, d_v, d_b_q, d_b_k, d_b_v = attn_bwd(qkv, d_attn, cos_t, sin_t, n_heads, n_kv)
    d_qkv = jnp.concatenate([d_q, d_k, d_v], axis=1)
    d_normed_attn = dot('se,de->sd', d_qkv, w_qkv).astype(BF16).astype(F32)
    d_hidden_norm, d_gain_a = norm_bwd(hidden, inv_attn, gain_a, d_normed_attn)
    grad_hidden = (d_resid.astype(F32) + d_hidden_norm).astype(BF16)

    d_kvb = jnp.concatenate([d_b_k.reshape(N_DEV, n_b), d_b_v.reshape(N_DEV, n_b), jnp.zeros((N_DEV, rows - 2 * n_b), F32)], axis=1)
    d_small = jnp.stack([d_gain_a, d_b_q[0], d_gain_m, d_kvb.reshape(width)], axis=1)
    d_small = jnp.pad(d_small, ((0, 0), (0, GRAD_BLK - 4)))
    grads = attn_grads(attn_out.T, d_resid, normed_attn.T, d_qkv, d_small)
    grads = lax.psum_scatter(grads, AX, scatter_dimension=0, tiled=True)
    out_sum, grads = barrier((out_sum, grads))
    layer_out = (resid_mid.astype(F32) + out_sum).astype(BF16)
    g_w_o, g_qkv = grads[:, :width], grads[:, width:]
    g_w_q = g_qkv[:, :q_width]
    g_w_k = g_qkv[:, q_width:q_width + kv_width]
    g_w_v = g_qkv[:, q_width + kv_width:n_qkv]
    g_small = g_qkv[:, n_qkv:n_qkv + 4].T
    g_kvb = g_small[3]
    return (layer_out[None], grad_hidden[None], g_small[0], g_w_q, g_small[1], g_w_k, g_kvb[:n_b], g_w_v, g_kvb[n_b:2 * n_b],
            g_w_o, g_small[2], g_w_gate, g_w_up, g_w_down)


def solution(mesh):
    act_spec = P(AX, None, None)
    mat_spec = P(AX, None)
    vec_spec = P(AX)
    param_specs = (vec_spec, mat_spec, vec_spec, mat_spec, vec_spec, mat_spec, vec_spec, mat_spec, vec_spec, mat_spec, mat_spec, mat_spec)
    in_specs_all = (act_spec, act_spec, mat_spec) + param_specs
    out_specs_all = (act_spec, act_spec) + param_specs

    return jax.shard_map(local_step, mesh=mesh, in_specs=in_specs_all, out_specs=out_specs_all, check_vma=False)
```

time: 1240 us -> 966 us (0.78)
  waiting for transfers between devices: 637 us -> 433 us
  blocking collectives: 76.4 us -> 0 us
  matrix products: 325 us -> 260 us
  Pallas kernels: 0 us -> 45.3 us
  local copies, waits for them, and re-layouts: 104 us -> 126 us
    reduce_scatter x4 -> x5, waiting for transfers between devices: 275 us -> 31.8 us  [the longest x4 31.8 us: group_scatter(): lax.psum_scatter(arr, AX, scatter_dimension=0, tiled=True, axis_index_gro...]
    all_to_all x1 -> x0, blocking collectives: 76.4 us -> none  [local_step(): gu = lax.all_to_all(gu, AX, 0, 0, axis_index_groups=GROUPS, tiled=True)]
    dot_general x22 -> x26, matrix products: 314 us -> 260 us  [dot(): return jnp.einsum(eq_form, lhs_arr, rhs_arr, preferred_element_type=F32)]
    pallas_call x0 -> x3, Pallas kernels: none -> 45.3 us  [the longest x1 18 us: attn_bwd(): pl.pallas_call(attn_bwd_kernel, grid=(n_kv, group), in_specs=[blk_h, pl.B...]
    ppermute x5, waiting for transfers between devices: 319 us -> 361 us  [z_pair(): return lax.ppermute(arr, AX, Z_PERM)]
    all_gather x1, waiting for transfers between devices: 41.6 us -> 0.01 us  [local_step(): qkv_full = lax.all_gather(qkv_loc, AX, axis=0, tiled=True)]
    ppermute x0 -> x7, waiting for transfers between devices: none -> 38.4 us  [local_step(): piece = lax.ppermute(piece, AX, [(i, i ^ d) for i in range(N_DEV)])]
    dynamic_update_slice x0 -> x8, local copies, waits for them, and re-layouts: none -> 12.7 us  [local_step(): lax.dynamic_update_slice(gu_rows, piece[:, None], (0, rank ^ d, 0, 0))]
  transfers between devices with their start and end apart: 15 -> 25, of which waited for: 7 -> 7; matrix products, arithmetic and copies ran while one was open for 24% -> 43% of each run, Pallas kernels for 0% -> 5%
where the time goes in v2:
time: 966 us; the launch traced here: 956 us
  waiting for transfers between devices  433 us (45%)
  matrix products  260 us (27%)
  local copies, waits for them, and re-layouts  126 us (13%)
  other arithmetic  53.8 us (6%)
  Pallas kernels  45.3 us (5%)
  starting transfers between devices  22.2 us (2%)
  between operations  15.5 us (2%)
    ppermute x5, waiting for transfers between devices, z_pair(): return lax.ppermute(arr, AX, Z_PERM)  361 us
    dot_general x26, matrix products, dot(): return jnp.einsum(eq_form, lhs_arr, rhs_arr, preferred_element_type=F32)  260 us
    ppermute x7, waiting for transfers between devices, local_step(): piece = lax.ppermute(piece, AX, [(i, i ^ d) for i in range(N_DEV)])  38.4 us
    reduce_scatter x4, waiting for transfers between devices, group_scatter(): lax.psum_scatter(arr, AX, scatter_dimension=0, tiled=True, axis_index_gro...  31.8 us
    reshape x4, local copies, waits for them, and re-layouts, back_rows(): grad.reshape(TP, rows, 2, ff_blk).transpose(1, 2, 0, 3)  21.1 us
  transfers between devices with their start and end apart: 25, of which 7 were waited for; matrix products, arithmetic and copies ran while one was open for 43% of the time, Pallas kernels for 5%

profile of v2, /device:TPU:0, one launch (start us, length us, event | category | flops | bytes accessed | tf_op | source)
XLA Modules:
  0.0 955.9 jit_solution(11097708305814833917)
XLA Ops:
  11.5 3.9 stack.33
  15.5 2.8 copy.47
  18.3 4.0 stack.34
  23.8 7.6 maximum_bitcast_fusion
  31.4 7.6 reshape.111
  40.8 3.7 collective-permute-start.6
  57.6 26.0 %collective-permute-done.1 = bf16[2,96,1120]{2,1,0:T(8,128)(2,1)S(1)} collective-permute-done((bf16[2,96,1120]{2,1,0:T(8,128)(2,1)S(1)}, bf16[2,96,1120]{2,1,0:T(8,128)(2,1)S(1)}, u32[]{:S(2)}, u32[]{:S(2)}) %collective-permute-start.1) | collective-permute-done | bytes 430112 | tf_op jit(solution)/shard_map/ppermute | solution.py:264
  84.6 12.4 %collective-permute-done.2 = bf16[2,96,1120]{2,1,0:T(8,128)(2,1)S(1)} collective-permute-done((bf16[2,96,1120]{2,1,0:T(8,128)(2,1)S(1)}, bf16[2,96,1120]{2,1,0:T(8,128)(2,1)S(1)}, u32[]{:S(2)}, u32[]{:S(2)}) %collective-permute-start.2) | collective-permute-done | bytes 430112 | tf_op jit(solution)/shard_map/ppermute | solution.py:264
  108.2 5.6 fusion.39.q_ref.k_ref.v_ref
  113.8 12.7 %attn_fwd.1 = bf16[512,1536]{1,0:T(8,128)(2,1)S(1)} custom-call(f32[512,2048]{1,0:T(8,128)S(1)} %fusion.39.q_ref.k_ref.v_ref, f32[512,2048]{1,0:T(8,128)S(1)} %fusion.39.q_ref.k_ref.v_ref, f32[512,2048]{1,0:T(8,128)S(1)} %fusion.39.q_ref.k_ref.v_ref, f32[512,128]{1,0:T(8,128)S(1)} %get-tuple-element.126.cos_ref, f32[512,128]{1,0:T(8,128)S(1)} %get-tuple-element.127.sin_ref), custom_call_target="tpu_custom_call" | custom-call | flops 8589934592 | bytes 6291456 | tf_op jit(solution)/shard_map/attn_fwd/pallas_call | solution.py:72
  128.6 6.1 fusion.37
  139.6 4.4 copy.50
  146.0 111.8 %collective-permute-done.7 = bf16[560,1536]{1,0:T(8,128)(2,1)} collective-permute-done((bf16[560,1536]{1,0:T(8,128)(2,1)}, bf16[560,1536]{1,0:T(8,128)(2,1)}, u32[]{:S(2)}, u32[]{:S(2)}) %collective-permute-start.7) | collective-permute-done | bytes 1720352 | tf_op jit(solution)/shard_map/ppermute | solution.py:220
  257.8 4.1 broadcast_select_fusion.3
  262.0 4.9 copy.51
  266.9 2.6 broadcast_select_fusion.1
  271.9 13.1 %fusion.78 = f32[2048,1120]{0,1:T(8,128)} fusion(bf16[2048,1536]{1,0:T(8,128)(2,1)} %all-gather.13.cloned.1.call-done, bf16[768,1120]{1,0:T(8,128)(2,1)} %get-tuple-element.97, bf16[768,1120]{1,0:T(8,128)(2,1)} %get-tuple-element.129), kind=kOutput, calls=%fused_computation.159 | convolution fusion | flops 7053312000 | bytes 18907136 | tf_op jit(solution)/shard_map/sd,df->sf/dot_general | solution.py:23
  285.0 9.9 %fusion.80 = f32[2048,1120]{0,1:T(8,128)} fusion(bf16[2048,1536]{1,0:T(8,128)(2,1)S(1)} %copy-done.37, bf16[768,1120]{1,0:T(8,128)(2,1)S(1)} %get-tuple-element.98, bf16[768,1120]{1,0:T(8,128)(2,1)S(1)} %get-tuple-element.128), kind=kOutput, calls=%fused_computation.161 | convolution fusion | flops 7053312000 | bytes 18907136 | tf_op jit(solution)/shard_map/sd,df->sf/dot_general | solution.py:23
  294.9 19.7 %multiply_convert_fusion.1 = (bf16[2048,1120]{0,1:T(8,128)(2,1)}, bf16[2048,1120]{0,1:T(8,128)(2,1)}, bf16[2048,1120]{0,1:T(8,128)(2,1)}) fusion(f32[2048,1120]{0,1:T(8,128)} %fusion.80, f32[2048,1120]{0,1:T(8,128)} %fusion.78, bf16[2048,1536]{1,0:T(8,128)(2,1)} %all-gather.11.cloned.1.call-done, bf16[560,1536]{1,0:T(8,128)(2,1)} %get-tuple-element.107, ...), kind=kOutput, calls=%fused_computation.16 | convolution fusion | flops 7094599680 | bytes 41844736 | tf_op jit(solution)/shard_map/sd,fd->sf/dot_general | solution.py:23
  314.6 14.1 %fusion.77 = f32[2048,1536]{1,0:T(8,128)} fusion(bf16[2048,1120]{0,1:T(8,128)(2,1)} %get-tuple-element.50, bf16[768,1120]{1,0:T(8,128)(2,1)} %get-tuple-element.97, bf16[768,1120]{1,0:T(8,128)(2,1)} %get-tuple-element.129), kind=kOutput, calls=%fused_computation.158 | convolution fusion | flops 7053312000 | bytes 20611072 | tf_op jit(solution)/shard_map/sf,df->sd/dot_general | solution.py:23
  328.7 14.8 %convolution_add_fusion.2 = f32[2048,1536]{1,0:T(8,128)} fusion(f32[2048,1536]{1,0:T(8,128)} %fusion.77, bf16[2048,1120]{0,1:T(8,128)(2,1)S(1)} %copy-done.40, bf16[768,1120]{1,0:T(8,128)(2,1)S(1)} %get-tuple-element.98, bf16[768,1120]{1,0:T(8,128)(2,1)S(1)} %get-tuple-element.128), kind=kOutput, calls=%fused_computation.20 | convolution fusion | flops 7056457728 | bytes 33193984 | tf_op jit(solution)/shard_map/sf,df->sd/dot_general | solution.py:23
  343.6 14.1 %fusion.76 = f32[2048,1120]{0,1:T(8,128)} fusion(bf16[2048,1536]{1,0:T(8,128)(2,1)} %all-gather.17.cloned.1.call-done, bf16[768,1120]{1,0:T(8,128)(2,1)} %get-tuple-element.97, bf16[768,1120]{1,0:T(8,128)(2,1)} %get-tuple-element.129), kind=kOutput, calls=%fused_computation.157 | convolution fusion | flops 7053312000 | bytes 18907136 | tf_op jit(solution)/shard_map/sd,df->sf/dot_general | solution.py:23
  357.7 9.8 %fusion.79 = f32[2048,1120]{0,1:T(8,128)} fusion(bf16[2048,1536]{1,0:T(8,128)(2,1)S(1)} %copy-done.38, bf16[768,1120]{1,0:T(8,128)(2,1)S(1)} %get-tuple-element.98, bf16[768,1120]{1,0:T(8,128)(2,1)S(1)} %get-tuple-element.128), kind=kOutput, calls=%fused_computation.160 | convolution fusion | flops 7053312000 | bytes 18907136 | tf_op jit(solution)/shard_map/sd,df->sf/dot_general | solution.py:23
  367.5 20.5 %multiply_convert_fusion = (bf16[2048,1120]{0,1:T(8,128)(2,1)}, bf16[2048,1120]{0,1:T(8,128)(2,1)}, bf16[2048,1120]{0,1:T(8,128)(2,1)}) fusion(f32[2048,1120]{0,1:T(8,128)} %fusion.79, f32[2048,1120]{0,1:T(8,128)} %fusion.76, bf16[2048,1536]{1,0:T(8,128)(2,1)} %all-gather.15.cloned.1.call-done, bf16[560,1536]{1,0:T(8,128)(2,1)} %get-tuple-element.107, ...), kind=kOutput, calls=%fused_computation.15 | convolution fusion | flops 7094599680 | bytes 41844736 | tf_op jit(solution)/shard_map/sd,fd->sf/dot_general | solution.py:23
  388.0 14.7 %fusion.75 = f32[2048,1536]{1,0:T(8,128)} fusion(bf16[2048,1120]{0,1:T(8,128)(2,1)} %get-tuple-element.52, bf16[768,1120]{1,0:T(8,128)(2,1)} %get-tuple-element.97, bf16[768,1120]{1,0:T(8,128)(2,1)} %get-tuple-element.129), kind=kOutput, calls=%fused_computation.156 | convolution fusion | flops 7053312000 | bytes 20611072 | tf_op jit(solution)/shard_map/sf,df->sd/dot_general | solution.py:23
  402.7 15.1 %convolution_add_fusion.1 = f32[2048,1536]{1,0:T(8,128)} fusion(f32[2048,1536]{1,0:T(8,128)} %fusion.75, bf16[2048,1120]{0,1:T(8,128)(2,1)S(1)} %copy-done.39, bf16[768,1120]{1,0:T(8,128)(2,1)S(1)} %get-tuple-element.98, bf16[768,1120]{1,0:T(8,128)(2,1)S(1)} %get-tuple-element.128), kind=kOutput, calls=%fused_computation.19 | convolution fusion | flops 7056457728 | bytes 33193984 | tf_op jit(solution)/shard_map/sf,df->sd/dot_general | solution.py:23
  417.9 11.0 %fusion.86 = f32[1120,1536]{1,0:T(8,128)S(1)} fusion(bf16[2048,1120]{0,1:T(8,128)(2,1)} %get-tuple-element.55, bf16[2048,1536]{1,0:T(8,128)(2,1)} %all-gather.11.cloned.1.call-done), kind=kOutput, calls=%fused_computation.167 | convolution fusion | flops 7046430720 | bytes 17760256 | tf_op jit(solution)/shard_map/sf,sd->fd/dot_general | solution.py:23
  428.9 9.4 convolution_add_fusion
  438.3 4.6 constant_dynamic-slice_fusion
  442.9 6.8 fusion.54
  449.8 3.8 fusion.56
  453.6 5.6 convolution_add_fusion.6
  459.2 5.6 convolution_add_fusion.5
  464.8 11.2 %fusion.73 = f32[2048,1536]{1,0:T(8,128)} fusion(bf16[2048,1120]{0,1:T(8,128)(2,1)S(1)} %bitcast.128, bf16[560,1536]{1,0:T(8,128)(2,1)S(1)} %copy-done.25, bf16[560,1536]{1,0:T(8,128)(2,1)S(1)} %copy-done.24), kind=kOutput, calls=%fused_computation.154 | convolution fusion | flops 7053312000 | bytes 20611072 | tf_op jit(solution)/shard_map/sf,fd->sd/dot_general | solution.py:23
  476.0 13.0 %fusion.74 = f32[2048,1536]{1,0:T(8,128)} fusion(bf16[2048,1120]{0,1:T(8,128)(2,1)} %get-tuple-element.55, bf16[560,1536]{1,0:T(8,128)(2,1)S(1)} %copy-done.25, bf16[560,1536]{1,0:T(8,128)(2,1)S(1)} %copy-done.24), kind=kOutput, calls=%fused_computation.155 | convolution fusion | flops 7053312000 | bytes 20611072 | tf_op jit(solution)/shard_map/sf,fd->sd/dot_general | solution.py:23
  489.0 31.8 %reduce-scatter.8.cloned.1.call-done = f32[256,1536]{1,0:T(8,128)} async-done(((f32[2048,1536]{1,0:T(8,128)}), f32[256,1536]{1,0:T(8,128)}) %reduce-scatter.8.cloned.1.call-update) | async-done | bytes 1572880 | tf_op jit(solution)/shard_map/reduce_scatter | solution.py:231
  529.2 2.6 convolution_convert_fusion.2.do_ref
  531.9 18.0 %attn_bwd.1 = (bf16[512,1536]{1,0:T(8,128)(2,1)S(1)}, bf16[512,256]{1,0:T(8,128)(2,1)S(1)}, bf16[512,256]{1,0:T(8,128)(2,1)S(1)}, f32[1,1536]{1,0:T(1,128)S(1)},...) custom-call(f32[512,2048]{1,0:T(8,128)S(1)} %copy-done.13, f32[512,2048]{1,0:T(8,128)S(1)} %copy-done.13, ...), custom_call_target="tpu_custom_call" | custom-call | flops 17179869184 | bytes 10485760 | tf_op jit(solution)/shard_map/attn_bwd/pallas_call | solution.py:139
  556.7 8.6 fusion.32
  566.5 2.4 pad.9.refs_4_
  568.9 5.0 fusion.59
  573.9 2.6 copy.55.refs_1_
  581.0 14.6 %attn_grads.1 = f32[1536,3840]{1,0:T(8,128)} custom-call(bf16[1536,512]{1,0:T(8,128)(2,1)S(1)} %bitcast.98, bf16[1536,512]{1,0:T(8,128)(2,1)S(1)} %copy-done.4, bf16[512,1536]{1,0:T(8,128)(2,1)S(1)} %fusion.29.refs_2_, bf16[512,2048]{1,0:T(8,128)(2,1)S(1)} %copy-done.6, f32[1536,256]{1,0:T(8,128)S(1)} %copy-done.3), custom_call_target="tpu_custom_call" | custom-call | flops 12884901888 | bytes 33554432 | tf_op jit(solution)/shard_map/attn_grads/pallas_call | solution.py:188
  595.7 6.7 fusion.50
  602.3 6.7 convolution_add_fusion.3
  610.6 5.6 fusion.48
  616.3 6.1 convolution_add_fusion.4
  622.6 63.7 %collective-permute-done.10 = f32[768,1120]{0,1:T(8,128)S(1)} collective-permute-done((f32[768,1120]{0,1:T(8,128)S(1)}, f32[768,1120]{0,1:T(8,128)S(1)}, u32[]{:S(2)}, u32[]{:S(2)}) %collective-permute-start.10) | collective-permute-done | bytes 3440672 | tf_op jit(solution)/shard_map/ppermute | solution.py:220
  686.8 3.0 copy.58
  689.8 3.7 all-to-all-start.1
  695.0 65.2 %collective-permute-done.9 = f32[768,1120]{0,1:T(8,128)} collective-permute-done((f32[768,1120]{0,1:T(8,128)}, f32[768,1120]{0,1:T(8,128)}, u32[]{:S(2)}, u32[]{:S(2)}) %collective-permute-start.9) | collective-permute-done | bytes 3440672 | tf_op jit(solution)/shard_map/ppermute | solution.py:220
  760.2 5.3 add.177
  765.5 5.1 copy.56
  770.7 4.8 all-to-all-start
  775.4 120.4 %collective-permute-done.11 = f32[560,1536]{1,0:T(8,128)} collective-permute-done((f32[560,1536]{1,0:T(8,128)}, f32[560,1536]{1,0:T(8,128)}, u32[]{:S(2)}, u32[]{:S(2)}) %collective-permute-start.11) | collective-permute-done | bytes 3440672 | tf_op jit(solution)/shard_map/ppermute | solution.py:220
  895.8 5.9 add.181
  901.7 4.0 reshape.121
  905.6 6.4 copy.59
  912.0 5.6 reshape.122
  917.7 5.9 reshape.118
  923.6 6.3 copy.57
  929.8 5.6 reshape.119
  935.4 3.9 pad_maximum_fusion.3
  945.5 3.5 fusion.58
  (251 shorter events, 74.7 us)
Async XLA Ops:
  7.2 98.1 %all-gather.7.cloned.1.call-start = ((), (), s32[]{:S(2)}) async-start(), calls=%async_computation.7 | async-start | bytes 7102464 | tf_op jit(solution)/shard_map/all_gather | solution.py:252
  10.7 117.9 %all-gather.9.cloned.1.call-start = ((), (), s32[]{:S(2)}) async-start(), calls=%async_computation.8 | async-start | bytes 5013504 | tf_op jit(solution)/shard_map/all_gather | solution.py:254
  11.4 260.4 %all-gather.13.cloned.1.call-start = ((), (), s32[]{:S(2)}) async-start(), calls=%async_computation.10 | async-start | bytes 7077888 | tf_op jit(solution)/shard_map/all_gather | solution.py:227
  39.1 9.0 copy-start.17
  39.1 8.0 copy-start.36
  40.8 62.6 %collective-permute-start.6 = (bf16[2,96,1120]{2,1,0:T(8,128)(2,1)}, bf16[2,96,1120]{2,1,0:T(8,128)(2,1)}, u32[]{:S(2)}, u32[]{:S(2)}) collective-permute-start(bf16[2,96,1120]{2,1,0:T(8,128)(2,1)} %get-tuple-element.99), channel_id=1, source_target_pairs={{0,7},{1,6},{2,5},{3,4},{4,3},{5,2},{6,1},{7,0},{8,15},{9,14},{10,... | collective-permute-start | bytes 1290248 | tf_op jit(solution)/shard_map/ppermute | solution.py:264
  44.5 57.0 %collective-permute-start.5 = (bf16[2,96,1120]{2,1,0:T(8,128)(2,1)}, bf16[2,96,1120]{2,1,0:T(8,128)(2,1)}, u32[]{:S(2)}, u32[]{:S(2)}) collective-permute-start(bf16[2,96,1120]{2,1,0:T(8,128)(2,1)} %get-tuple-element.100), channel_id=1, source_target_pairs={{0,6},{1,7},{2,4},{3,5},{4,2},{5,3},{6,0},{7,1},{8,14},{9,15},{10,... | collective-permute-start | bytes 1290248 | tf_op jit(solution)/shard_map/ppermute | solution.py:264
  45.2 54.4 %collective-permute-start.4 = (bf16[2,96,1120]{2,1,0:T(8,128)(2,1)}, bf16[2,96,1120]{2,1,0:T(8,128)(2,1)}, u32[]{:S(2)}, u32[]{:S(2)}) collective-permute-start(bf16[2,96,1120]{2,1,0:T(8,128)(2,1)} %get-tuple-element.101), channel_id=1, source_target_pairs={{0,5},{1,4},{2,7},{3,6},{4,1},{5,0},{6,3},{7,2},{8,13},{9,12},{10,... | collective-permute-start | bytes 1290248 | tf_op jit(solution)/shard_map/ppermute | solution.py:264
  46.6 51.2 %collective-permute-start.3 = (bf16[2,96,1120]{2,1,0:T(8,128)(2,1)}, bf16[2,96,1120]{2,1,0:T(8,128)(2,1)}, u32[]{:S(2)}, u32[]{:S(2)}) collective-permute-start(bf16[2,96,1120]{2,1,0:T(8,128)(2,1)} %get-tuple-element.102), channel_id=1, source_target_pairs={{0,4},{1,5},{2,6},{3,7},{4,0},{5,1},{6,2},{7,3},{8,12},{9,13},{10,... | collective-permute-start | bytes 1290248 | tf_op jit(solution)/shard_map/ppermute | solution.py:264
  46.9 7.2 collective-permute-start
  48.1 6.1 copy-start.27
  48.3 65.5 %copy-start.7 = (f32[512,128]{1,0:T(8,128)}, f32[512,128]{1,0:T(8,128)S(1)}, u32[]{:S(2)}) copy-start(f32[512,128]{1,0:T(8,128)S(1)} %get-tuple-element.126.cos_ref) | copy-start | bytes 786436
  48.3 65.5 %copy-start.9 = (f32[512,128]{1,0:T(8,128)}, f32[512,128]{1,0:T(8,128)S(1)}, u32[]{:S(2)}) copy-start(f32[512,128]{1,0:T(8,128)S(1)} %get-tuple-element.127.sin_ref) | copy-start | bytes 786436
  48.3 35.3 %copy-start.26 = (bf16[2,96,1120]{2,1,0:T(8,128)(2,1)S(1)}, bf16[2,96,1120]{2,1,0:T(8,128)(2,1)}, u32[]{:S(2)}) copy-start(bf16[2,96,1120]{2,1,0:T(8,128)(2,1)} %get-tuple-element.103) | copy-start | bytes 1290244
  50.3 57.8 %copy-start.34 = (f32[512]{0:T(512)}, f32[512]{0:T(512)S(1)}, u32[]{:S(2)}) copy-start(f32[512]{0:T(512)S(1)} %add_rsqrt_fusion.1) | copy-start | bytes 6148
  54.2 29.4 %collective-permute-start.1 = (bf16[2,96,1120]{2,1,0:T(8,128)(2,1)S(1)}, bf16[2,96,1120]{2,1,0:T(8,128)(2,1)S(1)}, u32[]{:S(2)}, u32[]{:S(2)}) collective-permute-start(bf16[2,96,1120]{2,1,0:T(8,128)(2,1)S(1)} %copy-done.27), channel_id=1, source_target_pairs={{0,2},{1,3},{2,0},{3,1},{4,6},{5,7},{6,4},{7,5},{8,10},{9,11},{10,... | collective-permute-start | bytes 1290248 | tf_op jit(solution)/shard_map/ppermute | solution.py:264
  83.6 13.4 %collective-permute-start.2 = (bf16[2,96,1120]{2,1,0:T(8,128)(2,1)S(1)}, bf16[2,96,1120]{2,1,0:T(8,128)(2,1)S(1)}, u32[]{:S(2)}, u32[]{:S(2)}) collective-permute-start(bf16[2,96,1120]{2,1,0:T(8,128)(2,1)S(1)} %copy-done.26), channel_id=1, source_target_pairs={{0,3},{1,2},{2,1},{3,0},{4,7},{5,6},{6,5},{7,4},{8,11},{9,10},{10,... | collective-permute-start | bytes 1290248 | tf_op jit(solution)/shard_map/ppermute | solution.py:264
  99.6 8.6 copy-start.21
  107.8 6.0 copy-start.32
  107.8 27.0 %copy-start.28 = (f32[1536]{0:T(1024)}, f32[1536]{0:T(1024)S(1)}, u32[]{:S(2)}) copy-start(f32[1536]{0:T(1024)S(1)} %get-tuple-element.76) | copy-start | bytes 18436
  128.6 6.1 copy-start
  137.6 157.3 %all-gather.11.cloned.1.call-start = ((), (), s32[]{:S(2)}) async-start(), calls=%async_computation.9 | async-start | bytes 7077888 | tf_op jit(solution)/shard_map/all_gather | solution.py:227
  138.9 204.7 %all-gather.17.cloned.1.call-start = ((), (), s32[]{:S(2)}) async-start(), calls=%async_computation.13 | async-start | bytes 7077888 | tf_op jit(solution)/shard_map/all_gather | solution.py:227
  139.5 228.0 %all-gather.15.cloned.1.call-start = ((), (), s32[]{:S(2)}) async-start(), calls=%async_computation.12 | async-start | bytes 7077888 | tf_op jit(solution)/shard_map/all_gather | solution.py:227
  144.0 118.1 %collective-permute-start.8 = (bf16[2,768,1120]{1,2,0:T(8,128)(2,1)S(1)}, bf16[2,768,1120]{1,2,0:T(8,128)(2,1)}, u32[]{:S(2)}, u32[]{:S(2)}) collective-permute-start(bf16[2,768,1120]{1,2,0:T(8,128)(2,1)S(1)} %copy.50), channel_id=1, source_target_pairs={{0,8},{1,9},{2,10},{3,11},{4,12},{5,13},{6,14},{7,15},{8,0},{9,1},... | collective-permute-start | bytes 10321928 | tf_op jit(solution)/shard_map/ppermute | solution.py:220
  145.6 112.2 %collective-permute-start.7 = (bf16[560,1536]{1,0:T(8,128)(2,1)}, bf16[560,1536]{1,0:T(8,128)(2,1)}, u32[]{:S(2)}, u32[]{:S(2)}) collective-permute-start(bf16[560,1536]{1,0:T(8,128)(2,1)} %param.29), channel_id=1, source_target_pairs={{0,8},{1,9},{2,10},{3,11},{4,12},{5,13},{6,14},{7,15},{8,0},{9,1},... | collective-permute-start | bytes 5160968 | tf_op jit(solution)/shard_map/ppermute | solution.py:220
  262.0 227.0 %reduce-scatter.6.cloned.1.call-start = ((), (), s32[]{:S(2)}) async-start(), calls=%async_computation.11 | async-start | bytes 14155776 | tf_op jit(solution)/shard_map/reduce_scatter | solution.py:231
  271.9 13.1 %copy-start.37 = (bf16[2048,1536]{1,0:T(8,128)(2,1)S(1)}, bf16[2048,1536]{1,0:T(8,128)(2,1)}, u32[]{:S(2)}) copy-start(bf16[2048,1536]{1,0:T(8,128)(2,1)} %all-gather.13.cloned.1.call-done) | copy-start | bytes 18874372
  314.6 14.1 %copy-start.40 = (bf16[2048,1120]{0,1:T(8,128)(2,1)S(1)}, bf16[2048,1120]{0,1:T(8,128)(2,1)}, u32[]{:S(2)}) copy-start(bf16[2048,1120]{0,1:T(8,128)(2,1)} %get-tuple-element.53) | copy-start | bytes 13762564
  343.5 177.2 %reduce-scatter.8.cloned.1.call-start = ((), (), s32[]{:S(2)}) async-start(), calls=%async_computation.14 | async-start | bytes 14155776 | tf_op jit(solution)/shard_map/reduce_scatter | solution.py:231
  343.6 14.1 %copy-start.38 = (bf16[2048,1536]{1,0:T(8,128)(2,1)S(1)}, bf16[2048,1536]{1,0:T(8,128)(2,1)}, u32[]{:S(2)}) copy-start(bf16[2048,1536]{1,0:T(8,128)(2,1)} %all-gather.17.cloned.1.call-done) | copy-start | bytes 18874372
  388.0 14.7 %copy-start.39 = (bf16[2048,1120]{0,1:T(8,128)(2,1)S(1)}, bf16[2048,1120]{0,1:T(8,128)(2,1)}, u32[]{:S(2)}) copy-start(bf16[2048,1120]{0,1:T(8,128)(2,1)} %get-tuple-element.54) | copy-start | bytes 13762564
  417.8 11.1 %slice-start.8 = ((s8[6291456]{0:T(1024)(128)(4,1)}), s8[2097152]{0:T(1024)(128)(4,1)S(1)}, s32[]{:S(2)}) async-start(s8[6291456]{0:T(1024)(128)(4,1)} %bitcast.123), calls=%async_computation.26 | async-start | bytes 4194304
  417.8 517.6 %reduce-scatter.10.cloned.1.call-start = ((), (), s32[]{:S(2)}) async-start(), calls=%async_computation.15 | async-start | bytes 14155776 | tf_op jit(solution)/shard_map/reduce_scatter | solution.py:231
  417.9 11.0 %slice-start.9 = ((s8[6291456]{0:T(1024)(128)(4,1)}), s8[4194304]{0:T(1024)(128)(4,1)S(1)}, s32[]{:S(2)}) async-start(s8[6291456]{0:T(1024)(128)(4,1)} %bitcast.123), calls=%async_computation.27 | async-start | bytes 8388608
  417.9 25.0 %slice-start = ((s8[6291456]{0:T(1024)(128)(4,1)}), s8[4194304]{0:T(1024)(128)(4,1)S(1)}, s32[]{:S(2)}) async-start(s8[6291456]{0:T(1024)(128)(4,1)} %bitcast.115), calls=%async_computation.18 | async-start | bytes 8388608
  428.9 14.0 %slice-start.1 = ((s8[6291456]{0:T(1024)(128)(4,1)}), s8[2097152]{0:T(1024)(128)(4,1)S(1)}, s32[]{:S(2)}) async-start(s8[6291456]{0:T(1024)(128)(4,1)} %bitcast.115), calls=%async_computation.19 | async-start | bytes 4194304
  438.3 11.5 %slice-start.20 = ((s8[4587520]{0:T(1024)(128)(4,1)}), s8[4194304]{0:T(1024)(128)(4,1)S(1)}, s32[]{:S(2)}) async-start(s8[4587520]{0:T(1024)(128)(4,1)} %bitcast.135), calls=%async_computation.38 | async-start | bytes 8388608
  442.9 6.9 slice-start.21
  442.9 10.7 %slice-start.4 = ((s8[6291456]{0:T(1024)(128)(4,1)}), s8[4194304]{0:T(1024)(128)(4,1)S(1)}, s32[]{:S(2)}) async-start(s8[6291456]{0:T(1024)(128)(4,1)} %bitcast.119), calls=%async_computation.22 | async-start | bytes 8388608
  442.9 10.7 %slice-start.14 = ((s8[4587520]{0:T(1024)(128)(4,1)}), s8[4194304]{0:T(1024)(128)(4,1)S(1)}, s32[]{:S(2)}) async-start(s8[4587520]{0:T(1024)(128)(4,1)} %bitcast.129), calls=%async_computation.32 | async-start | bytes 8388608
  442.9 16.3 %slice-start.18 = ((s8[4587520]{0:T(1024)(128)(4,1)}), s8[4194304]{0:T(1024)(128)(4,1)S(1)}, s32[]{:S(2)}) async-start(s8[4587520]{0:T(1024)(128)(4,1)} %bitcast.133), calls=%async_computation.36 | async-start | bytes 8388608
  449.8 9.4 slice-start.19
  453.6 11.2 %slice-start.12 = ((s8[4587520]{0:T(1024)(128)(4,1)}), s8[4194304]{0:T(1024)(128)(4,1)S(1)}, s32[]{:S(2)}) async-start(s8[4587520]{0:T(1024)(128)(4,1)} %bitcast.127), calls=%async_computation.30 | async-start | bytes 8388608
  459.2 5.6 copy-start.24
  459.2 5.6 copy-start.25
  459.2 5.6 slice-start.13
  520.8 414.6 %reduce-scatter.12.cloned.1.call-start = ((), (), s32[]{:S(2)}) async-start(), calls=%async_computation.16 | async-start | bytes 14155776 | tf_op jit(solution)/shard_map/reduce_scatter | solution.py:231
  521.4 417.9 %reduce-scatter.14.cloned.1.call-start = ((), (), s32[]{:S(2)}) async-start(), calls=%async_computation.17 | async-start | bytes 25067520 | tf_op jit(solution)/shard_map/reduce_scatter | solution.py:356
  523.1 6.0 slice-start.10
  556.7 8.6 copy-start.5
  595.6 15.0 %slice-start.2 = ((s8[6291456]{0:T(1024)(128)(4,1)}), s8[2097152]{0:T(1024)(128)(4,1)S(1)}, s32[]{:S(2)}) async-start(s8[6291456]{0:T(1024)(128)(4,1)} %bitcast.117), calls=%async_computation.20 | async-start | bytes 4194304
  595.6 14.9 %slice-start.3 = ((s8[6291456]{0:T(1024)(128)(4,1)}), s8[4194304]{0:T(1024)(128)(4,1)S(1)}, s32[]{:S(2)}) async-start(s8[6291456]{0:T(1024)(128)(4,1)} %bitcast.117), calls=%async_computation.21 | async-start | bytes 8388608
  602.3 13.9 %slice-start.6 = ((s8[6291456]{0:T(1024)(128)(4,1)}), s8[4194304]{0:T(1024)(128)(4,1)S(1)}, s32[]{:S(2)}) async-start(s8[6291456]{0:T(1024)(128)(4,1)} %bitcast.121), calls=%async_computation.24 | async-start | bytes 8388608
  602.3 13.9 %slice-start.16 = ((s8[4587520]{0:T(1024)(128)(4,1)}), s8[4194304]{0:T(1024)(128)(4,1)S(1)}, s32[]{:S(2)}) async-start(s8[4587520]{0:T(1024)(128)(4,1)} %bitcast.131), calls=%async_computation.34 | async-start | bytes 8388608
  609.0 7.2 slice-start.7
  609.0 7.2 slice-start.17
  609.1 77.3 %collective-permute-start.10 = (f32[768,1120]{0,1:T(8,128)S(1)}, f32[768,1120]{0,1:T(8,128)S(1)}, u32[]{:S(2)}, u32[]{:S(2)}) collective-permute-start(f32[768,1120]{0,1:T(8,128)S(1)} %convolution_add_fusion.3), channel_id=1, source_target_pairs={{0,8},{1,9},{2,10},{3,11},{4,12},{5,13},{6,14},{7,15},{8,0},{9,1},... | collective-permute-start | bytes 10321928 | tf_op jit(solution)/shard_map/ppermute | solution.py:220
  616.3 70.1 %copy-start.23 = (f32[768,1120]{0,1:T(8,128)S(1)}, f32[768,1120]{0,1:T(8,128)}, u32[]{:S(2)}) copy-start(f32[768,1120]{0,1:T(8,128)} %convolution_add_fusion.5) | copy-start | bytes 10321924
  622.4 137.8 %collective-permute-start.9 = (f32[768,1120]{0,1:T(8,128)}, f32[768,1120]{0,1:T(8,128)}, u32[]{:S(2)}, u32[]{:S(2)}) collective-permute-start(f32[768,1120]{0,1:T(8,128)} %convolution_add_fusion.4), channel_id=1, source_target_pairs={{0,8},{1,9},{2,10},{3,11},{4,12},{5,13},{6,14},{7,15},{8,0},{9,1},... | collective-permute-start | bytes 10321928 | tf_op jit(solution)/shard_map/ppermute | solution.py:220
  689.8 80.9 %all-to-all-start.1 = ((f32[8,96,1120]{2,1,0:T(8,128)}), f32[8,96,1120]{2,1,0:T(8,128)S(1)}, u32[]{:S(2)}, u32[]{:S(2)}) async-start(f32[8,96,1120]{2,1,0:T(8,128)} %bitcast.103), calls=%async_computation.6 | async-start | bytes 7077888 | tf_op jit(solution)/shard_map/all_to_all | solution.py:337
  693.5 202.3 %collective-permute-start.11 = (f32[560,1536]{1,0:T(8,128)}, f32[560,1536]{1,0:T(8,128)}, u32[]{:S(2)}, u32[]{:S(2)}) collective-permute-start(f32[560,1536]{1,0:T(8,128)} %get-tuple-element.93), channel_id=1, source_target_pairs={{0,8},{1,9},{2,10},{3,11},{4,12},{5,13},{6,14},{7,15},{8,0},{9,1},... | collective-permute-start | bytes 10321928 | tf_op jit(solution)/shard_map/ppermute | solution.py:220
  770.7 147.0 %all-to-all-start = ((f32[8,96,1120]{2,1,0:T(8,128)}), f32[8,96,1120]{2,1,0:T(8,128)}, u32[]{:S(2)}, u32[]{:S(2)}) async-start(f32[8,96,1120]{2,1,0:T(8,128)} %bitcast.102), calls=%async_computation.5 | async-start | bytes 7077888 | tf_op jit(solution)/shard_map/all_to_all | solution.py:337
  935.4 10.1 %copy-start.16 = (bf16[512,1536]{1,0:T(8,128)(2,1)S(1)}, bf16[512,1536]{1,0:T(8,128)(2,1)}, u32[]{:S(2)}) copy-start(bf16[512,1536]{1,0:T(8,128)(2,1)} %copy-done.14) | copy-start | bytes 4718596
  (24 other events, 66.0 us)
Sparse Core Ops, SparseCore 0:
  10.8 72.8 all-gather.6
  85.9 38.2 all-gather.8
  137.7 42.7 all-gather.12
  182.2 41.6 all-gather.10
  226.1 41.6 all-gather.16
  269.5 41.6 all-gather.14
  343.7 86.8 reduce-scatter.5
  434.1 86.6 reduce-scatter.7
  524.3 86.7 reduce-scatter.9
  614.3 89.2 reduce-scatter.11
  708.7 206.1 reduce-scatter.13

commit v3 on v2

--- a/solution.py
+++ b/solution.py
@@ -216,6 +216,167 @@
     return d_hidden, d_gain
 
 
+def cut_kernel(blk, n_rank, gate_ref, up_ref, out_ref):
+    for r in range(n_rank):
+        for g, src in enumerate((gate_ref, up_ref)):
+            out_ref[r, g, :, 0:blk] = src[:, r * blk:(r + 1) * blk]
+            out_ref[r, g, :, blk:2 * blk] = src[:, (n_rank + r) * blk:(n_rank + r + 1) * blk]
+
+
+def cut_columns(w_gate, w_up, blk):
+    rows = w_gate.shape[0]
+    return pl.pallas_call(
+        lambda *refs: cut_kernel(blk, TP, *refs),
+        out_shape=jax.ShapeDtypeStruct((TP, 2, rows, 2 * blk), BF16),
+        in_specs=[pl.BlockSpec(memory_space=pltpu.VMEM)] * 2,
+        out_specs=pl.BlockSpec(memory_space=pltpu.VMEM),
+        compiler_params=pltpu.CompilerParams(vmem_limit_bytes=24 << 20),
+        cost_estimate=pl.CostEstimate(flops=4 << 30, bytes_accessed=8 << 20, transcendentals=0),
+        name='cut_columns',
+    )(w_gate, w_up)
+
+
+def join_kernel(blk, n_rank, src_ref, out_ref):
+    for r in range(n_rank):
+        out_ref[:, r * blk:(r + 1) * blk] = src_ref[r, :, 0:blk]
+        out_ref[:, (n_rank + r) * blk:(n_rank + r + 1) * blk] = src_ref[r, :, blk:2 * blk]
+
+
+def join_columns(parts, blk):
+    rows = parts.shape[1]
+    tile = 32
+    return pl.pallas_call(
+        lambda *refs: join_kernel(blk, TP, *refs),
+        grid=(rows // tile,),
+        out_shape=jax.ShapeDtypeStruct((rows, 2 * TP * blk), F32),
+        in_specs=[pl.BlockSpec((TP, tile, 2 * blk), lambda i: (0, i, 0))],
+        out_specs=pl.BlockSpec((tile, 2 * TP * blk), lambda i: (i, 0)),
+        compiler_params=pltpu.CompilerParams(vmem_limit_bytes=24 << 20),
+        cost_estimate=pl.CostEstimate(flops=4 << 30, bytes_accessed=8 << 20, transcendentals=0),
+        name='join_columns',
+    )(parts)
+
+
+def scatter_kernel(cols, g_ref, out_ref, own, from_core, buf1, buf2, buf3, load_sem, send_sem, recv_sem):
+    dev = lax.axis_index(AX)
+    me = (dev // 8, (dev // 4) % 2, (dev // 2) % 2)
+    core = dev % 2
+    peer_core = dev + 1 - 2 * core
+    peers = tuple(dev + step * (1 - 2 * pos) for step, pos in zip((8, 4, 2), me))
+    barrier_sem = pltpu.get_barrier_semaphore()
+    for peer in (peer_core,) + peers:
+        pl.semaphore_signal(barrier_sem, inc=1, device_id=(peer,), device_id_type=pl.DeviceIdType.MESH)
+    pl.semaphore_wait(barrier_sem, 4)
+    orders = ((2, 1, 0), (1, 0, 2), (0, 2, 1))
+    load = pltpu.make_async_copy(g_ref.at[:, :, :, core], own, load_sem)
+    load.start()
+
+    def pick(fixed):
+        return tuple(fixed.get(d, slice(None)) for d in range(3))
+
+    def remote(slot, src, dst, peer):
+        copy = pltpu.make_async_remote_copy(
+            src_ref=src, dst_ref=dst, send_sem=send_sem.at[slot], recv_sem=recv_sem.at[slot],
+            device_id=(peer,), device_id_type=pl.DeviceIdType.MESH)
+        copy.start()
+        return copy
+
+    def col(k):
+        return pl.ds(k * cols, cols)
+
+    core_copies = {}
+    for half in range(2):
+        for k, order in enumerate(orders):
+            where = pick({order[0]: me[order[0]] if half else 1 - me[order[0]]})
+            core_copies[half, k] = remote(
+                half * 3 + k, g_ref.at[where + (1 - core, slice(None), col(k))],
+                from_core.at[where + (slice(None), col(k))], peer_core)
+    load.wait()
+
+    def add(dst, src, count):
+        def body(i, carry):
+            a, b = i // 2, i % 2
+            dst(a, b)[...] = dst(a, b)[...] + src(a, b)[...]
+            return carry
+
+        lax.fori_loop(0, count, body, 0)
+
+    def at4(ref, k, order, first):
+        def get(a, b):
+            fixed = {order[0]: first, order[1]: a, order[2]: b}
+            return ref.at[tuple(fixed[d] for d in range(3)) + (slice(None), col(k))]
+
+        return get
+
+    def at2(ref, k, order, second):
+        def get(a, b):
+            fixed = {order[0]: me[order[0]], order[1]: second, order[2]: b}
+            return ref.at[tuple(fixed[d] for d in range(3)) + (slice(None), col(k))]
+
+        return get
+
+    stage1, stage2, stage3 = {}, {}, {}
+    for k, order in enumerate(orders):
+        core_copies[0, k].wait_recv()
+        far = 1 - me[order[0]]
+        add(at4(own, k, order, far), at4(from_core, k, order, far), 4)
+    for k, order in enumerate(orders):
+        for a in range(2):
+            for b in range(2):
+                fixed = {order[0]: 1 - me[order[0]], order[1]: a, order[2]: b}
+                src = own.at[tuple(fixed[d] for d in range(3)) + (slice(None), col(k))]
+                stage1[k, a, b] = remote(6 + k * 4 + a * 2 + b, src, buf1.at[k, a, b], peers[order[0]])
+    for k, order in enumerate(orders):
+        core_copies[1, k].wait_recv()
+        near = me[order[0]]
+        add(at4(own, k, order, near), at4(from_core, k, order, near), 4)
+    for k, order in enumerate(orders):
+        for a in range(2):
+            for b in range(2):
+                stage1[k, a, b].wait_recv()
+        add(at4(own, k, order, me[order[0]]), lambda a, b, k=k: buf1.at[k, a, b], 4)
+    for k, order in enumerate(orders):
+        for b in range(2):
+            src = at2(own, k, order, 1 - me[order[1]])(0, b)
+            stage2[k, b] = remote(18 + k * 2 + b, src, buf2.at[k, b], peers[order[1]])
+    for k, order in enumerate(orders):
+        for b in range(2):
+            stage2[k, b].wait_recv()
+        add(at2(own, k, order, me[order[1]]), lambda a, b, k=k: buf2.at[k, b], 2)
+    for k, order in enumerate(orders):
+        src = at2(own, k, order, me[order[1]])(0, 1 - me[order[2]])
+        stage3[k] = remote(24 + k, src, buf3.at[k], peers[order[2]])
+    for k, order in enumerate(orders):
+        stage3[k].wait_recv()
+        out_ref[:, k * cols:(k + 1) * cols] = at2(own, k, order, me[order[1]])(0, me[order[2]])[...] + buf3[k]
+    for copy in list(core_copies.values()) + list(stage1.values()) + list(stage2.values()) + list(stage3.values()):
+        copy.wait_send()
+
+
+def scatter_all(grads, rows):
+    cols = grads.shape[1] // 3
+    g6 = grads.reshape(2, 2, 2, 2, rows, 3 * cols)
+    return pl.pallas_call(
+        lambda *refs: scatter_kernel(cols, *refs),
+        out_shape=jax.ShapeDtypeStruct((rows, 3 * cols), F32),
+        in_specs=[pl.BlockSpec(memory_space=pl.ANY)],
+        out_specs=pl.BlockSpec(memory_space=pltpu.VMEM),
+        scratch_shapes=[
+            pltpu.VMEM((2, 2, 2, rows, 3 * cols), F32),
+            pltpu.VMEM((2, 2, 2, rows, 3 * cols), F32),
+            pltpu.VMEM((3, 2, 2, rows, cols), F32),
+            pltpu.VMEM((3, 2, rows, cols), F32),
+            pltpu.VMEM((3, rows, cols), F32),
+            pltpu.SemaphoreType.DMA,
+            pltpu.SemaphoreType.DMA((27,)),
+            pltpu.SemaphoreType.DMA((27,)),
+        ],
+        compiler_params=pltpu.CompilerParams(collective_id=0, has_side_effects=True, vmem_limit_bytes=52 << 20),
+        cost_estimate=pl.CostEstimate(flops=60 << 30, bytes_accessed=64 << 20, transcendentals=0),
+        name='scatter_all',
+    )(g6)
+
+
 def z_pair(arr):
     return lax.ppermute(arr, AX, Z_PERM)
 
@@ -229,6 +390,28 @@
 
 def group_scatter(arr):
     return lax.psum_scatter(arr, AX, scatter_dimension=0, tiled=True, axis_index_groups=GROUPS)
+
+
+def xor_send(arr, step):
+    return lax.ppermute(arr, AX, [(i, i ^ step) for i in range(N_DEV)])
+
+
+def plane_gather(arr, rank):
+    n_half = arr.shape[0] // CHUNKS
+    via_x, via_y = xor_send(arr, 2), xor_send(arr, 4)
+    halves = {0: (arr[:n_half], arr[n_half:]), 2: (via_x[:n_half], via_x[n_half:]), 4: (via_y[:n_half], via_y[n_half:])}
+    halves[6] = (xor_send(halves[4][0], 2), xor_send(halves[2][1], 4))
+    own_core, x_core, y_core = xor_send(arr, 1), xor_send(via_x, 1), xor_send(via_y, 1)
+    for step, both in ((1, own_core), (3, x_core), (5, y_core)):
+        halves[step] = (both[:n_half], both[n_half:])
+    halves[7] = tuple(xor_send(part, 1) for part in halves[6])
+    out = []
+    for c in range(CHUNKS):
+        buf = jnp.zeros((TP,) + halves[0][c].shape, BF16)
+        for step in range(TP):
+            buf = lax.dynamic_update_slice(buf, halves[step][c][None], (rank ^ step, 0, 0))
+        out.append(buf.reshape(TP * n_half, arr.shape[1]))
+    return out
 
 
 def local_step(hidden, grad_out, positions, gain_attn, w_q, b_q, w_k, b_k, w_v, b_v, w_o, gain_mlp, w_gate, w_up, w_down):
@@ -252,10 +435,8 @@
     qkv_full = lax.all_gather(qkv_loc, AX, axis=0, tiled=True)
     n_qkv = q_width + 2 * kv_width
     w_o_full = lax.all_gather(w_o, AX, axis=0, tiled=True)
-    down_other = z_pair(w_down)
-
-    gu = jnp.stack([w_gate, w_up], axis=0).reshape(2, rows, 2, TP, ff_blk)
-    gu = gu.transpose(3, 0, 1, 2, 4).reshape(TP, 2, rows, ff_loc)
+
+    gu = cut_columns(w_gate, w_up, ff_blk)
     gu, hidden = barrier((gu, hidden))
     gu_rows = jnp.zeros((2, TP, rows, ff_loc), BF16)
     for d in range(TP):
@@ -274,16 +455,15 @@
     cos_t, sin_t = rope_tables(positions[0])
     normed_attn, inv_attn = norm_fwd(hidden, gain_a)
     qkv = dot('sd,de->se', normed_attn, w_qkv) + bias
-    qkv, gu_rows = barrier((qkv, gu_rows))
+    qkv, gu_rows, grad_out, w_down = barrier((qkv, gu_rows, grad_out, w_down))
     gu_other = z_pair(gu_rows)
+    down_other = z_pair(w_down)
+    go_all = plane_gather(grad_out, rank)
     attn_out = attn_fwd(qkv, cos_t, sin_t, n_heads, n_kv)
     resid_mid = (hidden.astype(F32) + dot('se,ed->sd', attn_out, w_o_full)).astype(BF16)
     normed_mlp, inv_mlp = norm_fwd(resid_mid, gain_m)
-    normed_mlp, grad_out = barrier((normed_mlp, grad_out))
-
     n_ch = n_seq // CHUNKS
     h_all = [group_gather(normed_mlp[c * n_ch:(c + 1) * n_ch]) for c in range(CHUNKS)]
-    go_all = [group_gather(grad_out[c * n_ch:(c + 1) * n_ch]) for c in range(CHUNKS)]
 
     gu_lo = jnp.where(z_zero, gu_rows, gu_other)
     gu_hi = jnp.where(z_zero, gu_other, gu_rows)
@@ -331,19 +511,19 @@
     dn_sums, gg_keep, gu_keep, out_part, wd_keep = barrier((dn_sums, gg_keep, gu_keep, out_part, wd_keep))
     d_normed_mlp = jnp.concatenate(dn_sums, axis=0).astype(BF16).astype(F32)
     out_sum = jnp.concatenate([group_scatter(part) for part in out_part], axis=0)
-    g_w_down = wd_keep + wd_recv
 
     def back_rows(grad):
         grad = lax.all_to_all(grad.reshape(TP, rows, ff_loc), AX, 0, 0, axis_index_groups=GROUPS, tiled=True)
-        return grad.reshape(TP, rows, 2, ff_blk).transpose(1, 2, 0, 3).reshape(rows, N_DEV * ff_blk)
-
-    g_w_gate = back_rows(gg_keep + gg_recv)
+        return join_columns(grad, ff_blk)
+
     g_w_up = back_rows(gu_keep + gu_recv)
 
     d_resid_norm, d_gain_m = norm_bwd(resid_mid, inv_mlp, gain_m, d_normed_mlp)
     d_resid = (grad_out.astype(F32) + d_resid_norm).astype(BF16)
     d_attn = dot('sd,ed->se', d_resid, w_o_full).astype(BF16)
     d_q, d_k, d_v, d_b_q, d_b_k, d_b_v = attn_bwd(qkv, d_attn, cos_t, sin_t, n_heads, n_kv)
+    gg_keep, _ = barrier((gg_keep, d_b_k))
+    g_w_gate = back_rows(gg_keep + gg_recv)
     d_qkv = jnp.concatenate([d_q, d_k, d_v], axis=1)
     d_normed_attn = dot('se,de->sd', d_qkv, w_qkv).astype(BF16).astype(F32)
     d_hidden_norm, d_gain_a = norm_bwd(hidden, inv_attn, gain_a, d_normed_attn)
@@ -353,8 +533,9 @@
     d_small = jnp.stack([d_gain_a, d_b_q[0], d_gain_m, d_kvb.reshape(width)], axis=1)
     d_small = jnp.pad(d_small, ((0, 0), (0, GRAD_BLK - 4)))
     grads = attn_grads(attn_out.T, d_resid, normed_attn.T, d_qkv, d_small)
-    grads = lax.psum_scatter(grads, AX, scatter_dimension=0, tiled=True)
-    out_sum, grads = barrier((out_sum, grads))
+    grads = scatter_all(grads, rows)
+    out_sum, wd_keep, grads = barrier((out_sum, wd_keep, grads))
+    g_w_down = wd_keep + wd_recv
     layer_out = (resid_mid.astype(F32) + out_sum).astype(BF16)
     g_w_o, g_qkv = grads[:, :width], grads[:, width:]
     g_w_q = g_qkv[:, :q_width]

time: 966 us -> 893 us (0.924)
  waiting for transfers between devices: 433 us -> 263 us
  Pallas kernels: 45.3 us -> 175 us
  local copies, waits for them, and re-layouts: 126 us -> 95.4 us
  other arithmetic: 53.8 us -> 43 us
    ppermute x5, waiting for transfers between devices: 361 us -> 110 us  [z_pair(): return lax.ppermute(arr, AX, Z_PERM)]
    pallas_call x0 -> x4, Pallas kernels: none -> 129 us  [the longest x1 120 us: scatter_all(): pl.pallas_call(lambda *refs: scatter_kernel(cols, *refs), out_shape=jax.S...]
    ppermute x0 -> x9, waiting for transfers between devices: none -> 79.6 us  [xor_send(): return lax.ppermute(arr, AX, [(i, i ^ step) for i in range(N_DEV)])]
    reshape x5 -> x0, local copies, waits for them, and re-layouts: 28.7 us -> none  [the longest x4 21.1 us: back_rows(): grad.reshape(TP, rows, 2, ff_blk).transpose(1, 2, 0, 3)]
    reduce_scatter x4, waiting for transfers between devices: 31.8 us -> 15.1 us  [group_scatter(): lax.psum_scatter(arr, AX, scatter_dimension=0, tiled=True, axis_index_gro...]
    all_gather x1, waiting for transfers between devices: 0.01 us -> 15.9 us  [local_step(): w_o_full = lax.all_gather(w_o, AX, axis=0, tiled=True)]
    transpose x2 -> x0, local copies, waits for them, and re-layouts: 12.6 us -> none  [back_rows(): grad.reshape(TP, rows, 2, ff_blk).transpose(1, 2, 0, 3)]
    dynamic_update_slice x0 -> x11, local copies, waits for them, and re-layouts: none -> 10.8 us  [plane_gather(): lax.dynamic_update_slice(buf, halves[step][c][None], (rank ^ step, 0, 0))]
  transfers between devices with their start and end apart: 25 -> 31, of which waited for: 7 -> 13; matrix products, arithmetic and copies ran while one was open for 43% -> 42% of each run, Pallas kernels for 5% -> 20%
where the time goes in v3:
time: 893 us; the launch traced here: 883 us
  matrix products  264 us (30%)
  waiting for transfers between devices  263 us (29%)
  Pallas kernels  175 us (20%)
  local copies, waits for them, and re-layouts  95.4 us (11%)
  other arithmetic  43 us (5%)
  starting transfers between devices  28 us (3%)
  between operations  15.7 us (2%)
    dot_general x26, matrix products, dot(): return jnp.einsum(eq_form, lhs_arr, rhs_arr, preferred_element_type=F32)  264 us
    pallas_call x1, Pallas kernels, scatter_all(): pl.pallas_call(lambda *refs: scatter_kernel(cols, *refs), out_shape=jax.S...  120 us
    ppermute x5, waiting for transfers between devices, z_pair(): return lax.ppermute(arr, AX, Z_PERM)  110 us
    ppermute x9, waiting for transfers between devices, xor_send(): return lax.ppermute(arr, AX, [(i, i ^ step) for i in range(N_DEV)])  79.6 us
    ppermute x7, waiting for transfers between devices, local_step(): piece = lax.ppermute(piece, AX, [(i, i ^ d) for i in range(N_DEV)])  34.7 us
    unnamed x145, local copies, waits for them, and re-layouts  22.3 us
    pallas_call x1, Pallas kernels, attn_bwd(): pl.pallas_call(attn_bwd_kernel, grid=(n_kv, group), in_specs=[blk_h, pl.B...  18 us
  transfers between devices with their start and end apart: 31, of which 13 were waited for; matrix products, arithmetic and copies ran while one was open for 42% of the time, Pallas kernels for 20%

profile of v3, /device:TPU:0, one launch (start us, length us, event | category | flops | bytes accessed | tf_op | source)
XLA Modules:
  0.0 883.3 jit_solution(6851191107366266104)
XLA Ops:
  17.3 3.6 collective-permute-start.6
  33.5 22.0 %collective-permute-done.1 = bf16[2,96,1120]{2,1,0:T(8,128)(2,1)S(1)} collective-permute-done((bf16[2,96,1120]{2,1,0:T(8,128)(2,1)S(1)}, bf16[2,96,1120]{2,1,0:T(8,128)(2,1)S(1)}, u32[]{:S(2)}, u32[]{:S(2)}) %collective-permute-start.1) | collective-permute-done | bytes 430112 | tf_op jit(solution)/shard_map/ppermute | solution.py:445
  56.5 12.7 %collective-permute-done.2 = bf16[2,96,1120]{2,1,0:T(8,128)(2,1)S(1)} collective-permute-done((bf16[2,96,1120]{2,1,0:T(8,128)(2,1)S(1)}, bf16[2,96,1120]{2,1,0:T(8,128)(2,1)S(1)}, u32[]{:S(2)}, u32[]{:S(2)}) %collective-permute-start.2) | collective-permute-done | bytes 430112 | tf_op jit(solution)/shard_map/ppermute | solution.py:445
  77.4 6.3 all-gather.5.cloned.1.call-done
  86.7 5.7 fusion.39.q_ref.k_ref.v_ref
  92.4 12.7 %attn_fwd.1 = bf16[512,1536]{1,0:T(8,128)(2,1)S(1)} custom-call(f32[512,2048]{1,0:T(8,128)S(1)} %fusion.39.q_ref.k_ref.v_ref, f32[512,2048]{1,0:T(8,128)S(1)} %fusion.39.q_ref.k_ref.v_ref, f32[512,2048]{1,0:T(8,128)S(1)} %fusion.39.q_ref.k_ref.v_ref, f32[512,128]{1,0:T(8,128)S(1)} %copy-done.9, f32[512,128]{1,0:T(8,128)S(1)} %copy-done.11), custom_call_target="tpu_custom_call" | custom-call | flops 8589934592 | bytes 6291456 | tf_op jit(solution)/shard_map/attn_fwd/pallas_call | solution.py:72
  107.1 15.9 %all-gather.7.cloned.1.call-done = bf16[1536,1536]{1,0:T(8,128)(2,1)} async-done(((bf16[96,1536]{1,0:T(8,128)(2,1)}), bf16[1536,1536]{1,0:T(8,128)(2,1)}) %all-gather.7.cloned.1.call-update) | async-done | bytes 4718608 | tf_op jit(solution)/shard_map/all_gather | solution.py:437
  123.0 5.1 fusion.37
  134.6 5.9 copy.44
  141.9 3.1 broadcast.72.clone
  146.8 43.6 %collective-permute-done.10 = bf16[512,1536]{1,0:T(8,128)(2,1)} collective-permute-done((bf16[512,1536]{1,0:T(8,128)(2,1)S(1)}, bf16[512,1536]{1,0:T(8,128)(2,1)}, u32[]{:S(2)}, u32[]{:S(2)}) %collective-permute-start.10) | collective-permute-done | bytes 1572896 | tf_op jit(solution)/shard_map/ppermute | solution.py:396
  194.1 2.4 fusion.64
  197.5 3.5 broadcast_select_fusion.3
  201.0 15.6 %collective-permute-done.12 = bf16[256,1536]{1,0:T(8,128)(2,1)S(1)} collective-permute-done((bf16[256,1536]{1,0:T(8,128)(2,1)S(1)}, bf16[256,1536]{1,0:T(8,128)(2,1)S(1)}, u32[]{:S(2)}, u32[]{:S(2)}) %collective-permute-start.12) | collective-permute-done | bytes 786464 | tf_op jit(solution)/shard_map/ppermute | solution.py:396
  217.6 2.4 fusion.62
  221.2 3.1 copy-done.22
  224.3 23.7 %collective-permute-done.15 = bf16[2,768,1120]{1,2,0:T(8,128)(2,1)} collective-permute-done((bf16[2,768,1120]{1,2,0:T(8,128)(2,1)}, bf16[2,768,1120]{1,2,0:T(8,128)(2,1)}, u32[]{:S(2)}, u32[]{:S(2)}) %collective-permute-start.15) | collective-permute-done | bytes 3440672 | tf_op jit(solution)/shard_map/ppermute | solution.py:381
  248.0 4.3 copy.45
  252.4 2.6 broadcast_select_fusion.1
  255.0 2.5 slice_bitcast_fusion
  257.5 12.8 %fusion.86 = f32[2048,1120]{0,1:T(8,128)} fusion(bf16[2048,1536]{1,0:T(8,128)(2,1)} %all-gather.9.cloned.1.call-done, bf16[768,1120]{1,0:T(8,128)(2,1)} %get-tuple-element.101, bf16[768,1120]{1,0:T(8,128)(2,1)} %get-tuple-element.141), kind=kOutput, calls=%fused_computation.182 | convolution fusion | flops 7053312000 | bytes 18907136 | tf_op jit(solution)/shard_map/sd,df->sf/dot_general | solution.py:23
  270.4 10.0 %fusion.88 = f32[2048,1120]{0,1:T(8,128)} fusion(bf16[2048,1536]{1,0:T(8,128)(2,1)S(1)} %copy-done.49, bf16[768,1120]{1,0:T(8,128)(2,1)S(1)} %get-tuple-element.102, bf16[768,1120]{1,0:T(8,128)(2,1)S(1)} %copy-done.30), kind=kOutput, calls=%fused_computation.184 | convolution fusion | flops 7053312000 | bytes 18907136 | tf_op jit(solution)/shard_map/sd,df->sf/dot_general | solution.py:23
  280.4 19.6 %multiply_convert_fusion.1 = (bf16[2048,1120]{0,1:T(8,128)(2,1)}, bf16[2048,1120]{0,1:T(8,128)(2,1)}, bf16[2048,1120]{0,1:T(8,128)(2,1)}) fusion(f32[2048,1120]{0,1:T(8,128)} %fusion.88, f32[2048,1120]{0,1:T(8,128)} %fusion.86, bf16[2048,1536]{1,0:T(8,128)(2,1)} %bitcast.145, bf16[560,1536]{1,0:T(8,128)(2,1)} %get-tuple-element.111, ...), kind=kOutput, calls=%fused_computation.16 | convolution fusion | flops 7094599680 | bytes 41844736 | tf_op jit(solution)/shard_map/sd,fd->sf/dot_general | solution.py:23
  300.0 14.1 %fusion.85 = f32[2048,1536]{1,0:T(8,128)} fusion(bf16[2048,1120]{0,1:T(8,128)(2,1)} %get-tuple-element.52, bf16[768,1120]{1,0:T(8,128)(2,1)} %get-tuple-element.101, bf16[768,1120]{1,0:T(8,128)(2,1)} %get-tuple-element.141), kind=kOutput, calls=%fused_computation.181 | convolution fusion | flops 7053312000 | bytes 20611072 | tf_op jit(solution)/shard_map/sf,df->sd/dot_general | solution.py:23
  314.1 14.7 %convolution_add_fusion.2 = f32[2048,1536]{1,0:T(8,128)} fusion(f32[2048,1536]{1,0:T(8,128)} %fusion.85, bf16[2048,1120]{0,1:T(8,128)(2,1)S(1)} %copy-done.52, bf16[768,1120]{1,0:T(8,128)(2,1)S(1)} %get-tuple-element.102, bf16[768,1120]{1,0:T(8,128)(2,1)S(1)} %copy-done.31), kind=kOutput, calls=%fused_computation.20 | convolution fusion | flops 7056457728 | bytes 33193984 | tf_op jit(solution)/shard_map/sf,df->sd/dot_general | solution.py:23
  330.9 18.5 %collective-permute-done.16 = bf16[256,1536]{1,0:T(8,128)(2,1)S(1)} collective-permute-done((bf16[256,1536]{1,0:T(8,128)(2,1)S(1)}, bf16[256,1536]{1,0:T(8,128)(2,1)S(1)}, u32[]{:S(2)}, u32[]{:S(2)}) %collective-permute-start.16) | collective-permute-done | bytes 786464 | tf_op jit(solution)/shard_map/ppermute | solution.py:396
  352.7 14.0 %fusion.84 = f32[2048,1120]{0,1:T(8,128)} fusion(bf16[2048,1536]{1,0:T(8,128)(2,1)} %all-gather.11.cloned.1.call-done, bf16[768,1120]{1,0:T(8,128)(2,1)} %get-tuple-element.101, bf16[768,1120]{1,0:T(8,128)(2,1)} %get-tuple-element.141), kind=kOutput, calls=%fused_computation.180 | convolution fusion | flops 7053312000 | bytes 18907136 | tf_op jit(solution)/shard_map/sd,df->sf/dot_general | solution.py:23
  366.7 10.0 %fusion.87 = f32[2048,1120]{0,1:T(8,128)} fusion(bf16[2048,1536]{1,0:T(8,128)(2,1)S(1)} %copy-done.50, bf16[768,1120]{1,0:T(8,128)(2,1)S(1)} %get-tuple-element.102, bf16[768,1120]{1,0:T(8,128)(2,1)S(1)} %copy-done.32), kind=kOutput, calls=%fused_computation.183 | convolution fusion | flops 7053312000 | bytes 18907136 | tf_op jit(solution)/shard_map/sd,df->sf/dot_general | solution.py:23
  376.7 19.7 %multiply_convert_fusion = (bf16[2048,1120]{0,1:T(8,128)(2,1)}, bf16[2048,1120]{0,1:T(8,128)(2,1)}, bf16[2048,1120]{0,1:T(8,128)(2,1)}) fusion(f32[2048,1120]{0,1:T(8,128)} %fusion.87, f32[2048,1120]{0,1:T(8,128)} %fusion.84, bf16[2048,1536]{1,0:T(8,128)(2,1)} %bitcast.45, bf16[560,1536]{1,0:T(8,128)(2,1)} %get-tuple-element.111, ...), kind=kOutput, calls=%fused_computation.15 | convolution fusion | flops 7094599680 | bytes 41844736 | tf_op jit(solution)/shard_map/sd,fd->sf/dot_general | solution.py:23
  396.4 14.3 %fusion.83 = f32[2048,1536]{1,0:T(8,128)} fusion(bf16[2048,1120]{0,1:T(8,128)(2,1)} %get-tuple-element.54, bf16[768,1120]{1,0:T(8,128)(2,1)} %get-tuple-element.101, bf16[768,1120]{1,0:T(8,128)(2,1)} %get-tuple-element.141), kind=kOutput, calls=%fused_computation.179 | convolution fusion | flops 7053312000 | bytes 20611072 | tf_op jit(solution)/shard_map/sf,df->sd/dot_general | solution.py:23
  410.6 14.8 %convolution_add_fusion.1 = f32[2048,1536]{1,0:T(8,128)} fusion(f32[2048,1536]{1,0:T(8,128)} %fusion.83, bf16[2048,1120]{0,1:T(8,128)(2,1)S(1)} %copy-done.51, bf16[768,1120]{1,0:T(8,128)(2,1)S(1)} %get-tuple-element.102, bf16[768,1120]{1,0:T(8,128)(2,1)S(1)} %copy-done.33), kind=kOutput, calls=%fused_computation.19 | convolution fusion | flops 7056457728 | bytes 33193984 | tf_op jit(solution)/shard_map/sf,df->sd/dot_general | solution.py:23
  425.6 11.3 %fusion.93 = f32[1120,1536]{1,0:T(8,128)S(1)} fusion(bf16[2048,1120]{0,1:T(8,128)(2,1)} %get-tuple-element.58, bf16[2048,1536]{1,0:T(8,128)(2,1)} %bitcast.45), kind=kOutput, calls=%fused_computation.189 | convolution fusion | flops 7046430720 | bytes 17760256 | tf_op jit(solution)/shard_map/sf,sd->fd/dot_general | solution.py:23
  436.9 10.0 %convolution_add_fusion = f32[1120,1536]{1,0:T(8,128)S(1)} fusion(f32[1120,1536]{1,0:T(8,128)S(1)} %fusion.93, bf16[2048,1120]{0,1:T(8,128)(2,1)} %get-tuple-element.57, bf16[2048,1536]{1,0:T(8,128)(2,1)S(1)} %bitcast.148), kind=kOutput, calls=%fused_computation.4 | convolution fusion | flops 7048151040 | bytes 24641536 | tf_op jit(solution)/shard_map/sf,sd->fd/dot_general | solution.py:23
  446.9 4.4 constant_dynamic-slice_fusion
  451.3 6.2 fusion.54
  457.6 3.8 fusion.56
  461.4 5.6 convolution_add_fusion.6
  467.0 5.6 convolution_add_fusion.5
  472.6 11.2 %fusion.82 = f32[2048,1536]{1,0:T(8,128)} fusion(bf16[2048,1120]{0,1:T(8,128)(2,1)S(1)} %bitcast.172, bf16[560,1536]{1,0:T(8,128)(2,1)S(1)} %copy-done.36, bf16[560,1536]{1,0:T(8,128)(2,1)S(1)} %copy-done.35), kind=kOutput, calls=%fused_computation.178 | convolution fusion | flops 7053312000 | bytes 20611072 | tf_op jit(solution)/shard_map/sf,fd->sd/dot_general | solution.py:23
  483.7 13.1 %fusion.81 = f32[2048,1536]{1,0:T(8,128)} fusion(bf16[2048,1120]{0,1:T(8,128)(2,1)} %get-tuple-element.58, bf16[560,1536]{1,0:T(8,128)(2,1)S(1)} %copy-done.36, bf16[560,1536]{1,0:T(8,128)(2,1)S(1)} %copy-done.35), kind=kOutput, calls=%fused_computation.177 | convolution fusion | flops 7053312000 | bytes 20611072 | tf_op jit(solution)/shard_map/sf,fd->sd/dot_general | solution.py:23
  496.9 15.1 %reduce-scatter.7.cloned.1.call-done = f32[256,1536]{1,0:T(8,128)} async-done(((f32[2048,1536]{1,0:T(8,128)}), f32[256,1536]{1,0:T(8,128)}) %reduce-scatter.7.cloned.1.call-update) | async-done | bytes 1572880 | tf_op jit(solution)/shard_map/reduce_scatter | solution.py:392
  512.7 6.7 fusion.50
  519.4 8.0 convolution_add_fusion.3
  529.6 7.4 fusion.48
  537.0 9.0 %convolution_add_fusion.4 = f32[768,1120]{0,1:T(8,128)} fusion(f32[768,1120]{0,1:T(8,128)S(1)} %fusion.48, bf16[2048,1120]{0,1:T(8,128)(2,1)} %get-tuple-element.54, bf16[2048,1536]{1,0:T(8,128)(2,1)} %all-gather.11.cloned.1.call-done, s32[]{:T(128)S(6)} %select_n.116), kind=kOutput, calls=%fused_computation.42 | convolution fusion | flops 3524075520 | bytes 14614532 | tf_op jit(solution)/shard_map/sd,sf->df/dot_general | solution.py:23
  548.1 56.9 %collective-permute-done.19 = f32[768,1120]{0,1:T(8,128)} collective-permute-done((f32[768,1120]{0,1:T(8,128)}, f32[768,1120]{0,1:T(8,128)}, u32[]{:S(2)}, u32[]{:S(2)}) %collective-permute-start.19) | collective-permute-done | bytes 3440672 | tf_op jit(solution)/shard_map/ppermute | solution.py:381
  605.0 4.2 add.193
  609.2 5.7 copy.51
  614.9 5.0 all-to-all-start.1
  624.8 2.7 convolution_convert_fusion.2.do_ref
  627.5 18.0 %attn_bwd.1 = (bf16[512,1536]{1,0:T(8,128)(2,1)S(1)}, bf16[512,256]{1,0:T(8,128)(2,1)S(1)}, bf16[512,256]{1,0:T(8,128)(2,1)S(1)}, f32[1,1536]{1,0:T(1,128)S(1)},...) custom-call(f32[512,2048]{1,0:T(8,128)S(1)} %copy-done.17, f32[512,2048]{1,0:T(8,128)S(1)} %copy-done.17, ...), custom_call_target="tpu_custom_call" | custom-call | flops 17179869184 | bytes 10485760 | tf_op jit(solution)/shard_map/attn_bwd/pallas_call | solution.py:139
  649.6 29.1 %collective-permute-done.18 = f32[768,1120]{0,1:T(8,128)} collective-permute-done((f32[768,1120]{0,1:T(8,128)}, f32[768,1120]{0,1:T(8,128)}, u32[]{:S(2)}, u32[]{:S(2)}) %collective-permute-start.18) | collective-permute-done | bytes 3440672 | tf_op jit(solution)/shard_map/ppermute | solution.py:381
  678.7 5.2 add.191
  683.9 5.2 copy.50
  691.9 8.4 fusion.32
  701.6 2.4 pad.9.refs_4_
  704.0 4.7 fusion.59
  708.7 2.6 copy.49.refs_1_
  715.8 14.7 %attn_grads.1 = f32[1536,3840]{1,0:T(8,128)} custom-call(bf16[1536,512]{1,0:T(8,128)(2,1)S(1)} %bitcast.141, bf16[1536,512]{1,0:T(8,128)(2,1)S(1)} %copy-done.4, bf16[512,1536]{1,0:T(8,128)(2,1)S(1)} %fusion.29.refs_2_, bf16[512,2048]{1,0:T(8,128)(2,1)S(1)} %copy-done.8, f32[1536,256]{1,0:T(8,128)S(1)} %copy-done.3), custom_call_target="tpu_custom_call" | custom-call | flops 12884901888 | bytes 33554432 | tf_op jit(solution)/shard_map/attn_grads/pallas_call | solution.py:188
  730.5 3.7 all-to-all-start
  734.2 120.2 %scatter_all.1 = f32[96,3840]{1,0:T(8,128)S(1)} custom-call(f32[2,2,2,2,96,3840]{5,4,3,2,1,0:T(8,128)} %bitcast.170), custom_call_target="tpu_custom_call" | custom-call | flops 64424509440 | bytes 67108864 | tf_op jit(solution)/shard_map/scatter_all/pallas_call | solution.py:359
  855.4 5.1 join_columns.3
  860.6 2.9 join_columns.2
  871.6 4.4 add.195
  (280 shorter events, 90.1 us)
Async XLA Ops:
  7.2 76.6 %all-gather.5.cloned.1.call-start = ((), (), s32[]{:S(2)}) async-start(), calls=%async_computation.6 | async-start | bytes 7102464 | tf_op jit(solution)/shard_map/all_gather | solution.py:435
  10.6 112.3 %all-gather.7.cloned.1.call-start = ((), (), s32[]{:S(2)}) async-start(), calls=%async_computation.7 | async-start | bytes 5013504 | tf_op jit(solution)/shard_map/all_gather | solution.py:437
  11.4 246.1 %all-gather.9.cloned.1.call-start = ((), (), s32[]{:S(2)}) async-start(), calls=%async_computation.8 | async-start | bytes 7077888 | tf_op jit(solution)/shard_map/all_gather | solution.py:388
  15.5 7.8 copy-start.48
  17.3 58.3 %collective-permute-start.6 = (bf16[2,96,1120]{2,1,0:T(8,128)(2,1)}, bf16[2,96,1120]{2,1,0:T(8,128)(2,1)}, u32[]{:S(2)}, u32[]{:S(2)}) collective-permute-start(bf16[2,96,1120]{2,1,0:T(8,128)(2,1)} %get-tuple-element.103), channel_id=1, source_target_pairs={{0,7},{1,6},{2,5},{3,4},{4,3},{5,2},{6,1},{7,0},{8,15},{9,14},{10,... | collective-permute-start | bytes 1290248 | tf_op jit(solution)/shard_map/ppermute | solution.py:445
  20.9 52.9 %collective-permute-start.5 = (bf16[2,96,1120]{2,1,0:T(8,128)(2,1)}, bf16[2,96,1120]{2,1,0:T(8,128)(2,1)}, u32[]{:S(2)}, u32[]{:S(2)}) collective-permute-start(bf16[2,96,1120]{2,1,0:T(8,128)(2,1)} %get-tuple-element.104), channel_id=1, source_target_pairs={{0,6},{1,7},{2,4},{3,5},{4,2},{5,3},{6,0},{7,1},{8,14},{9,15},{10,... | collective-permute-start | bytes 1290248 | tf_op jit(solution)/shard_map/ppermute | solution.py:445
  21.4 50.4 %collective-permute-start.4 = (bf16[2,96,1120]{2,1,0:T(8,128)(2,1)}, bf16[2,96,1120]{2,1,0:T(8,128)(2,1)}, u32[]{:S(2)}, u32[]{:S(2)}) collective-permute-start(bf16[2,96,1120]{2,1,0:T(8,128)(2,1)} %get-tuple-element.105), channel_id=1, source_target_pairs={{0,5},{1,4},{2,7},{3,6},{4,1},{5,0},{6,3},{7,2},{8,13},{9,12},{10,... | collective-permute-start | bytes 1290248 | tf_op jit(solution)/shard_map/ppermute | solution.py:445
  22.9 47.1 %collective-permute-start.3 = (bf16[2,96,1120]{2,1,0:T(8,128)(2,1)}, bf16[2,96,1120]{2,1,0:T(8,128)(2,1)}, u32[]{:S(2)}, u32[]{:S(2)}) collective-permute-start(bf16[2,96,1120]{2,1,0:T(8,128)(2,1)} %get-tuple-element.106), channel_id=1, source_target_pairs={{0,4},{1,5},{2,6},{3,7},{4,0},{5,1},{6,2},{7,3},{8,12},{9,13},{10,... | collective-permute-start | bytes 1290248 | tf_op jit(solution)/shard_map/ppermute | solution.py:445
  23.2 6.9 collective-permute-start
  25.4 30.1 %copy-start.38 = (bf16[2,96,1120]{2,1,0:T(8,128)(2,1)S(1)}, bf16[2,96,1120]{2,1,0:T(8,128)(2,1)}, u32[]{:S(2)}) copy-start(bf16[2,96,1120]{2,1,0:T(8,128)(2,1)} %get-tuple-element.107) | copy-start | bytes 1290244
  27.3 59.4 %copy-start.46 = (f32[512]{0:T(512)}, f32[512]{0:T(512)S(1)}, u32[]{:S(2)}) copy-start(f32[512]{0:T(512)S(1)} %add_rsqrt_fusion.1) | copy-start | bytes 6148
  30.1 25.4 %collective-permute-start.1 = (bf16[2,96,1120]{2,1,0:T(8,128)(2,1)S(1)}, bf16[2,96,1120]{2,1,0:T(8,128)(2,1)S(1)}, u32[]{:S(2)}, u32[]{:S(2)}) collective-permute-start(bf16[2,96,1120]{2,1,0:T(8,128)(2,1)S(1)} %copy-done.39), channel_id=1, source_target_pairs={{0,2},{1,3},{2,0},{3,1},{4,6},{5,7},{6,4},{7,5},{8,10},{9,11},{10,... | collective-permute-start | bytes 1290248 | tf_op jit(solution)/shard_map/ppermute | solution.py:445
  55.5 13.7 %collective-permute-start.2 = (bf16[2,96,1120]{2,1,0:T(8,128)(2,1)S(1)}, bf16[2,96,1120]{2,1,0:T(8,128)(2,1)S(1)}, u32[]{:S(2)}, u32[]{:S(2)}) collective-permute-start(bf16[2,96,1120]{2,1,0:T(8,128)(2,1)S(1)} %copy-done.38), channel_id=1, source_target_pairs={{0,3},{1,2},{2,1},{3,0},{4,7},{5,6},{6,5},{7,4},{8,11},{9,10},{10,... | collective-permute-start | bytes 1290248 | tf_op jit(solution)/shard_map/ppermute | solution.py:445
  71.8 14.8 %copy-start.25 = (bf16[1,512,1536]{2,1,0:T(8,128)(2,1)S(1)}, bf16[1,512,1536]{2,1,0:T(8,128)(2,1)}, u32[]{:S(2)}) copy-start(bf16[1,512,1536]{2,1,0:T(8,128)(2,1)} %param.15) | copy-start | bytes 4718596
  86.3 6.1 copy-start.44
  86.3 41.8 %copy-start.40 = (f32[1536]{0:T(1024)}, f32[1536]{0:T(1024)S(1)}, u32[]{:S(2)}) copy-start(f32[1536]{0:T(1024)S(1)} %get-tuple-element.80) | copy-start | bytes 18436
  107.1 21.0 %copy-start = (bf16[512,1536]{1,0:T(8,128)(2,1)}, bf16[512,1536]{1,0:T(8,128)(2,1)S(1)}, u32[]{:S(2)}) copy-start(bf16[512,1536]{1,0:T(8,128)(2,1)S(1)} %attn_fwd.1) | copy-start | bytes 4718596
  131.0 221.7 %all-gather.11.cloned.1.call-start = ((), (), s32[]{:S(2)}) async-start(), calls=%async_computation.10 | async-start | bytes 7077888 | tf_op jit(solution)/shard_map/all_gather | solution.py:388
  131.1 59.3 %collective-permute-start.10 = (bf16[512,1536]{1,0:T(8,128)(2,1)S(1)}, bf16[512,1536]{1,0:T(8,128)(2,1)}, u32[]{:S(2)}, u32[]{:S(2)}) collective-permute-start(bf16[512,1536]{1,0:T(8,128)(2,1)S(1)} %bitcast.149), channel_id=1, source_target_pairs={{0,4},{1,5},{2,6},{3,7},{4,0},{5,1},{6,2},{7,3},{8,12},{9,13},{10,... | collective-permute-start | bytes 4718600 | tf_op jit(solution)/shard_map/ppermute | solution.py:396
  132.6 61.0 %collective-permute-start.8 = (bf16[512,1536]{1,0:T(8,128)(2,1)S(1)}, bf16[512,1536]{1,0:T(8,128)(2,1)S(1)}, u32[]{:S(2)}, u32[]{:S(2)}) collective-permute-start(bf16[512,1536]{1,0:T(8,128)(2,1)S(1)} %bitcast.150), channel_id=1, source_target_pairs={{0,2},{1,3},{2,0},{3,1},{4,6},{5,7},{6,4},{7,5},{8,10},{9,11},{10,... | collective-permute-start | bytes 4718600 | tf_op jit(solution)/shard_map/ppermute | solution.py:396
  134.0 59.5 %collective-permute-start.7 = (bf16[512,1536]{1,0:T(8,128)(2,1)S(1)}, bf16[512,1536]{1,0:T(8,128)(2,1)}, u32[]{:S(2)}, u32[]{:S(2)}) collective-permute-start(bf16[512,1536]{1,0:T(8,128)(2,1)S(1)} %bitcast.151), channel_id=1, source_target_pairs={{0,1},{1,0},{2,3},{3,2},{4,5},{5,4},{6,7},{7,6},{8,9},{9,8},{10,11... | collective-permute-start | bytes 4718600 | tf_op jit(solution)/shard_map/ppermute | solution.py:396
  134.0 63.5 %collective-permute-start.14 = (bf16[560,1536]{1,0:T(8,128)(2,1)}, bf16[560,1536]{1,0:T(8,128)(2,1)}, u32[]{:S(2)}, u32[]{:S(2)}) collective-permute-start(bf16[560,1536]{1,0:T(8,128)(2,1)} %param.29), channel_id=1, source_target_pairs={{0,8},{1,9},{2,10},{3,11},{4,12},{5,13},{6,14},{7,15},{8,0},{9,1},... | collective-permute-start | bytes 5160968 | tf_op jit(solution)/shard_map/ppermute | solution.py:381
  140.4 107.6 %collective-permute-start.15 = (bf16[2,768,1120]{1,2,0:T(8,128)(2,1)}, bf16[2,768,1120]{1,2,0:T(8,128)(2,1)}, u32[]{:S(2)}, u32[]{:S(2)}) collective-permute-start(bf16[2,768,1120]{1,2,0:T(8,128)(2,1)} %copy.44), channel_id=1, source_target_pairs={{0,8},{1,9},{2,10},{3,11},{4,12},{5,13},{6,14},{7,15},{8,0},{9,1},... | collective-permute-start | bytes 10321928 | tf_op jit(solution)/shard_map/ppermute | solution.py:381
  145.9 350.9 %reduce-scatter.5.cloned.1.call-start = ((), (), s32[]{:S(2)}) async-start(), calls=%async_computation.9 | async-start | bytes 14155776 | tf_op jit(solution)/shard_map/reduce_scatter | solution.py:392
  191.5 6.0 copy-start.34
  191.5 25.1 %collective-permute-start.12 = (bf16[256,1536]{1,0:T(8,128)(2,1)S(1)}, bf16[256,1536]{1,0:T(8,128)(2,1)S(1)}, u32[]{:S(2)}, u32[]{:S(2)}) collective-permute-start(bf16[256,1536]{1,0:T(8,128)(2,1)S(1)} %slice.170), channel_id=1, source_target_pairs={{0,2},{1,3},{2,0},{3,1},{4,6},{5,7},{6,4},{7,5},{8,10},{9,11},{10,... | collective-permute-start | bytes 2359304 | tf_op jit(solution)/shard_map/ppermute | solution.py:396
  193.6 7.4 copy-start.27
  193.6 26.4 %collective-permute-start.11 = (bf16[512,1536]{1,0:T(8,128)(2,1)}, bf16[512,1536]{1,0:T(8,128)(2,1)S(1)}, u32[]{:S(2)}, u32[]{:S(2)}) collective-permute-start(bf16[512,1536]{1,0:T(8,128)(2,1)} %collective-permute-done.10), channel_id=1, source_target_pairs={{0,1},{1,0},{2,3},{3,2},{4,5},{5,4},{6,7},{7,6},{8,9},{9,8},{10,11... | collective-permute-start | bytes 4718600 | tf_op jit(solution)/shard_map/ppermute | solution.py:396
  193.6 23.1 %collective-permute-start.9 = (bf16[512,1536]{1,0:T(8,128)(2,1)S(1)}, bf16[512,1536]{1,0:T(8,128)(2,1)S(1)}, u32[]{:S(2)}, u32[]{:S(2)}) collective-permute-start(bf16[512,1536]{1,0:T(8,128)(2,1)S(1)} %collective-permute-done.8), channel_id=1, source_target_pairs={{0,1},{1,0},{2,3},{3,2},{4,5},{5,4},{6,7},{7,6},{8,9},{9,8},{10,11... | collective-permute-start | bytes 4718600 | tf_op jit(solution)/shard_map/ppermute | solution.py:396
  216.6 4.5 collective-permute-start.13
  257.5 12.8 %copy-start.30 = (bf16[768,1120]{1,0:T(8,128)(2,1)S(1)}, bf16[768,1120]{1,0:T(8,128)(2,1)}, u32[]{:S(2)}) copy-start(bf16[768,1120]{1,0:T(8,128)(2,1)} %get-tuple-element.140) | copy-start | bytes 5160964
  257.5 12.8 %copy-start.49 = (bf16[2048,1536]{1,0:T(8,128)(2,1)S(1)}, bf16[2048,1536]{1,0:T(8,128)(2,1)}, u32[]{:S(2)}) copy-start(bf16[2048,1536]{1,0:T(8,128)(2,1)} %all-gather.9.cloned.1.call-done) | copy-start | bytes 18874372
  300.0 14.1 %copy-start.31 = (bf16[768,1120]{1,0:T(8,128)(2,1)S(1)}, bf16[768,1120]{1,0:T(8,128)(2,1)}, u32[]{:S(2)}) copy-start(bf16[768,1120]{1,0:T(8,128)(2,1)} %get-tuple-element.140) | copy-start | bytes 5160964
  300.0 14.1 %copy-start.52 = (bf16[2048,1120]{0,1:T(8,128)(2,1)S(1)}, bf16[2048,1120]{0,1:T(8,128)(2,1)}, u32[]{:S(2)}) copy-start(bf16[2048,1120]{0,1:T(8,128)(2,1)} %get-tuple-element.55) | copy-start | bytes 13762564
  328.9 183.0 %reduce-scatter.7.cloned.1.call-start = ((), (), s32[]{:S(2)}) async-start(), calls=%async_computation.11 | async-start | bytes 14155776 | tf_op jit(solution)/shard_map/reduce_scatter | solution.py:392
  330.3 19.1 %collective-permute-start.16 = (bf16[256,1536]{1,0:T(8,128)(2,1)S(1)}, bf16[256,1536]{1,0:T(8,128)(2,1)S(1)}, u32[]{:S(2)}, u32[]{:S(2)}) collective-permute-start(bf16[256,1536]{1,0:T(8,128)(2,1)S(1)} %slice.179), channel_id=1, source_target_pairs={{0,4},{1,5},{2,6},{3,7},{4,0},{5,1},{6,2},{7,3},{8,12},{9,13},{10,... | collective-permute-start | bytes 2359304 | tf_op jit(solution)/shard_map/ppermute | solution.py:396
  349.5 2.3 collective-permute-start.17
  352.7 14.0 %copy-start.32 = (bf16[768,1120]{1,0:T(8,128)(2,1)S(1)}, bf16[768,1120]{1,0:T(8,128)(2,1)}, u32[]{:S(2)}) copy-start(bf16[768,1120]{1,0:T(8,128)(2,1)} %get-tuple-element.140) | copy-start | bytes 5160964
  352.7 14.0 %copy-start.50 = (bf16[2048,1536]{1,0:T(8,128)(2,1)S(1)}, bf16[2048,1536]{1,0:T(8,128)(2,1)}, u32[]{:S(2)}) copy-start(bf16[2048,1536]{1,0:T(8,128)(2,1)} %all-gather.11.cloned.1.call-done) | copy-start | bytes 18874372
  396.4 14.3 %copy-start.33 = (bf16[768,1120]{1,0:T(8,128)(2,1)S(1)}, bf16[768,1120]{1,0:T(8,128)(2,1)}, u32[]{:S(2)}) copy-start(bf16[768,1120]{1,0:T(8,128)(2,1)} %get-tuple-element.140) | copy-start | bytes 5160964
  396.4 14.3 %copy-start.51 = (bf16[2048,1120]{0,1:T(8,128)(2,1)S(1)}, bf16[2048,1120]{0,1:T(8,128)(2,1)}, u32[]{:S(2)}) copy-start(bf16[2048,1120]{0,1:T(8,128)(2,1)} %get-tuple-element.56) | copy-start | bytes 13762564
  425.5 11.4 %slice-start = ((s8[6291456]{0:T(1024)(128)(4,1)}), s8[2097152]{0:T(1024)(128)(4,1)S(1)}, s32[]{:S(2)}) async-start(s8[6291456]{0:T(1024)(128)(4,1)} %bitcast.146), calls=%async_computation.14 | async-start | bytes 4194304
  425.5 438.0 %reduce-scatter.9.cloned.1.call-start = ((), (), s32[]{:S(2)}) async-start(), calls=%async_computation.12 | async-start | bytes 14155776 | tf_op jit(solution)/shard_map/reduce_scatter | solution.py:392
  425.6 11.3 %slice-start.1 = ((s8[6291456]{0:T(1024)(128)(4,1)}), s8[4194304]{0:T(1024)(128)(4,1)S(1)}, s32[]{:S(2)}) async-start(s8[6291456]{0:T(1024)(128)(4,1)} %bitcast.146), calls=%async_computation.15 | async-start | bytes 8388608
  425.6 25.7 %slice-start.2 = ((s8[6291456]{0:T(1024)(128)(4,1)}), s8[4194304]{0:T(1024)(128)(4,1)S(1)}, s32[]{:S(2)}) async-start(s8[6291456]{0:T(1024)(128)(4,1)} %bitcast.164), calls=%async_computation.16 | async-start | bytes 8388608
  436.9 14.4 %slice-start.3 = ((s8[6291456]{0:T(1024)(128)(4,1)}), s8[2097152]{0:T(1024)(128)(4,1)S(1)}, s32[]{:S(2)}) async-start(s8[6291456]{0:T(1024)(128)(4,1)} %bitcast.164), calls=%async_computation.17 | async-start | bytes 4194304
  446.9 10.6 %slice-start.16 = ((s8[4587520]{0:T(1024)(128)(4,1)}), s8[4194304]{0:T(1024)(128)(4,1)S(1)}, s32[]{:S(2)}) async-start(s8[4587520]{0:T(1024)(128)(4,1)} %bitcast.179), calls=%async_computation.30 | async-start | bytes 8388608
  451.3 6.2 slice-start.17
  451.3 10.1 %slice-start.4 = ((s8[6291456]{0:T(1024)(128)(4,1)}), s8[4194304]{0:T(1024)(128)(4,1)S(1)}, s32[]{:S(2)}) async-start(s8[6291456]{0:T(1024)(128)(4,1)} %bitcast.166), calls=%async_computation.18 | async-start | bytes 8388608
  451.3 10.1 %slice-start.10 = ((s8[4587520]{0:T(1024)(128)(4,1)}), s8[4194304]{0:T(1024)(128)(4,1)S(1)}, s32[]{:S(2)}) async-start(s8[4587520]{0:T(1024)(128)(4,1)} %bitcast.173), calls=%async_computation.24 | async-start | bytes 8388608
  451.3 15.7 %slice-start.12 = ((s8[4587520]{0:T(1024)(128)(4,1)}), s8[4194304]{0:T(1024)(128)(4,1)S(1)}, s32[]{:S(2)}) async-start(s8[4587520]{0:T(1024)(128)(4,1)} %bitcast.175), calls=%async_computation.26 | async-start | bytes 8388608
  457.6 9.4 %slice-start.13 = ((s8[4587520]{0:T(1024)(128)(4,1)}), s8[393216]{0:T(1024)(128)(4,1)S(1)}, s32[]{:S(2)}) async-start(s8[4587520]{0:T(1024)(128)(4,1)} %bitcast.175), calls=%async_computation.27 | async-start | bytes 786432
  461.4 11.2 %slice-start.8 = ((s8[4587520]{0:T(1024)(128)(4,1)}), s8[4194304]{0:T(1024)(128)(4,1)S(1)}, s32[]{:S(2)}) async-start(s8[4587520]{0:T(1024)(128)(4,1)} %bitcast.171), calls=%async_computation.22 | async-start | bytes 8388608
  512.0 351.5 %reduce-scatter.11.cloned.1.call-start = ((), (), s32[]{:S(2)}) async-start(), calls=%async_computation.13 | async-start | bytes 14155776 | tf_op jit(solution)/shard_map/reduce_scatter | solution.py:392
  512.0 7.4 slice-start.14
  512.7 6.7 slice-start.15
  519.4 9.5 %copy-start.1 = (bf16[512,1536]{1,0:T(8,128)(2,1)S(1)}, bf16[512,1536]{1,0:T(8,128)(2,1)}, u32[]{:S(2)}) copy-start(bf16[512,1536]{1,0:T(8,128)(2,1)} %copy-done) | copy-start | bytes 4718596
  527.4 77.6 %collective-permute-start.19 = (f32[768,1120]{0,1:T(8,128)}, f32[768,1120]{0,1:T(8,128)}, u32[]{:S(2)}, u32[]{:S(2)}) collective-permute-start(f32[768,1120]{0,1:T(8,128)} %convolution_add_fusion.3), channel_id=1, source_target_pairs={{0,8},{1,9},{2,10},{3,11},{4,12},{5,13},{6,14},{7,15},{8,0},{9,1},... | collective-permute-start | bytes 10321928 | tf_op jit(solution)/shard_map/ppermute | solution.py:381
  537.0 68.0 %copy-start.29 = (f32[768,1120]{0,1:T(8,128)S(1)}, f32[768,1120]{0,1:T(8,128)}, u32[]{:S(2)}) copy-start(f32[768,1120]{0,1:T(8,128)} %convolution_add_fusion.5) | copy-start | bytes 10321924
  546.0 132.7 %collective-permute-start.18 = (f32[768,1120]{0,1:T(8,128)}, f32[768,1120]{0,1:T(8,128)}, u32[]{:S(2)}, u32[]{:S(2)}) collective-permute-start(f32[768,1120]{0,1:T(8,128)} %convolution_add_fusion.4), channel_id=1, source_target_pairs={{0,8},{1,9},{2,10},{3,11},{4,12},{5,13},{6,14},{7,15},{8,0},{9,1},... | collective-permute-start | bytes 10321928 | tf_op jit(solution)/shard_map/ppermute | solution.py:381
  547.0 323.8 %collective-permute-start.20 = (f32[560,1536]{1,0:T(8,128)}, f32[560,1536]{1,0:T(8,128)}, u32[]{:S(2)}, u32[]{:S(2)}) collective-permute-start(f32[560,1536]{1,0:T(8,128)} %get-tuple-element.97), channel_id=1, source_target_pairs={{0,8},{1,9},{2,10},{3,11},{4,12},{5,13},{6,14},{7,15},{8,0},{9,1},... | collective-permute-start | bytes 10321928 | tf_op jit(solution)/shard_map/ppermute | solution.py:381
  614.9 115.6 %all-to-all-start.1 = ((f32[8,96,1120]{2,1,0:T(8,128)}), f32[8,96,1120]{2,1,0:T(8,128)}, u32[]{:S(2)}, u32[]{:S(2)}) async-start(f32[8,96,1120]{2,1,0:T(8,128)} %bitcast.143), calls=%async_computation.5 | async-start | bytes 7077888 | tf_op jit(solution)/shard_map/all_to_all | solution.py:516
  691.9 8.5 copy-start.7
  730.5 130.1 %all-to-all-start = ((f32[8,96,1120]{2,1,0:T(8,128)}), f32[8,96,1120]{2,1,0:T(8,128)S(1)}, u32[]{:S(2)}, u32[]{:S(2)}) async-start(f32[8,96,1120]{2,1,0:T(8,128)} %bitcast.144), calls=%async_computation.4 | async-start | bytes 7077888 | tf_op jit(solution)/shard_map/all_to_all | solution.py:516
  (38 other events, 114.3 us)
Sparse Core Ops, SparseCore 0:
  10.8 72.9 all-gather.4
  86.0 36.9 all-gather.6
  131.1 65.5 all-gather.8
  198.4 45.1 all-gather.10
  329.0 85.6 reduce-scatter.4
  425.6 86.2 reduce-scatter.6
  515.4 86.6 reduce-scatter.8
  605.5 114.8 reduce-scatter.10

commit v4 on v3

--- a/solution.py
+++ b/solution.py
@@ -438,13 +438,18 @@
 
     gu = cut_columns(w_gate, w_up, ff_blk)
     gu, hidden = barrier((gu, hidden))
-    gu_rows = jnp.zeros((2, TP, rows, ff_loc), BF16)
-    for d in range(TP):
-        piece = lax.dynamic_index_in_dim(gu, rank ^ d, 0, keepdims=False)
-        if d:
-            piece = lax.ppermute(piece, AX, [(i, i ^ d) for i in range(N_DEV)])
-        gu_rows = lax.dynamic_update_slice(gu_rows, piece[:, None], (0, rank ^ d, 0, 0))
-    gu_rows = gu_rows.reshape(2, half, ff_loc)
+    own_rows, other_rows = [], []
+    for g in range(2):
+        buf = jnp.zeros((TP, rows, ff_loc), BF16)
+        for d in range(TP):
+            piece = lax.dynamic_slice(gu, (rank ^ d, g, 0, 0), (1, 1, rows, ff_loc))[:, 0]
+            if d:
+                piece = lax.ppermute(piece, AX, [(i, i ^ d) for i in range(N_DEV)])
+            buf = lax.dynamic_update_slice(buf, piece, (rank ^ d, 0, 0))
+        buf = buf.reshape(half, ff_loc)
+        own_rows.append(buf)
+        other_rows.append(z_pair(buf))
+    down_other = z_pair(w_down)
 
     w_qkv = qkv_full[:, :n_qkv]
     small_t = qkv_full[:, n_qkv:n_qkv + 4].T.astype(F32)
@@ -455,9 +460,7 @@
     cos_t, sin_t = rope_tables(positions[0])
     normed_attn, inv_attn = norm_fwd(hidden, gain_a)
     qkv = dot('sd,de->se', normed_attn, w_qkv) + bias
-    qkv, gu_rows, grad_out, w_down = barrier((qkv, gu_rows, grad_out, w_down))
-    gu_other = z_pair(gu_rows)
-    down_other = z_pair(w_down)
+    qkv, grad_out = barrier((qkv, grad_out))
     go_all = plane_gather(grad_out, rank)
     attn_out = attn_fwd(qkv, cos_t, sin_t, n_heads, n_kv)
     resid_mid = (hidden.astype(F32) + dot('se,ed->sd', attn_out, w_o_full)).astype(BF16)
@@ -465,11 +468,11 @@
     n_ch = n_seq // CHUNKS
     h_all = [group_gather(normed_mlp[c * n_ch:(c + 1) * n_ch]) for c in range(CHUNKS)]
 
-    gu_lo = jnp.where(z_zero, gu_rows, gu_other)
-    gu_hi = jnp.where(z_zero, gu_other, gu_rows)
-    w_g = jnp.concatenate([gu_lo[0], gu_hi[0]], axis=0)
-    w_u = jnp.concatenate([gu_lo[1], gu_hi[1]], axis=0)
-    w_d = jnp.concatenate([jnp.where(z_zero, w_down, down_other), jnp.where(z_zero, down_other, w_down)], axis=0)
+    def z_order(own, other):
+        return jnp.concatenate([jnp.where(z_zero, own, other), jnp.where(z_zero, other, own)], axis=0)
+
+    w_g, w_u = z_order(own_rows[0], other_rows[0]), z_order(own_rows[1], other_rows[1])
+    w_d = z_order(w_down, down_other)
 
     pre = []
     for c in range(CHUNKS):
@@ -477,9 +480,14 @@
         up_proj = dot('sd,df->sf', h_all[c], w_u)
         pre.append((gate_pre, up_proj))
     acts, d_gates, d_ups, dn_sums = [], [], [], []
+    gate_pre, up_proj = pre[0]
+    act_first = (jax.nn.silu(gate_pre) * up_proj).astype(BF16)
+    out_first = dot('sf,fd->sd', act_first, w_d)
+    out_first, go_all[0] = barrier((out_first, go_all[0]))
+    out_sums = [group_scatter(out_first)]
     for c in range(CHUNKS):
         gate_pre, up_proj = pre[c]
-        act = (jax.nn.silu(gate_pre) * up_proj).astype(BF16)
+        act = act_first if c == 0 else (jax.nn.silu(gate_pre) * up_proj).astype(BF16)
         d_act = dot('sd,fd->sf', go_all[c], w_d).astype(BF16).astype(F32)
         gate_sig = jax.nn.sigmoid(gate_pre)
         d_gate = (d_act * up_proj * gate_sig * (1.0 + gate_pre * (1.0 - gate_sig))).astype(BF16)
@@ -507,23 +515,25 @@
     gg_recv, gu_recv, wd_recv = z_pair(gg_send), z_pair(gu_send), z_pair(wd_send)
     gg_keep = token_dot('sd,sf->df', h_keep, d_gates)
     gu_keep = token_dot('sd,sf->df', h_keep, d_ups)
-    out_part = [dot('sf,fd->sd', act, w_d) for act in acts]
-    dn_sums, gg_keep, gu_keep, out_part, wd_keep = barrier((dn_sums, gg_keep, gu_keep, out_part, wd_keep))
+    out_part = [dot('sf,fd->sd', act, w_d) for act in acts[1:]]
+    gu_sum = gu_keep + gu_recv
+    dn_sums, gg_keep, gu_sum, out_part, wd_keep = barrier((dn_sums, gg_keep, gu_sum, out_part, wd_keep))
     d_normed_mlp = jnp.concatenate(dn_sums, axis=0).astype(BF16).astype(F32)
-    out_sum = jnp.concatenate([group_scatter(part) for part in out_part], axis=0)
+    out_sum = jnp.concatenate(out_sums + [group_scatter(part) for part in out_part], axis=0)
 
     def back_rows(grad):
         grad = lax.all_to_all(grad.reshape(TP, rows, ff_loc), AX, 0, 0, axis_index_groups=GROUPS, tiled=True)
-        return join_columns(grad, ff_blk)
-
-    g_w_up = back_rows(gu_keep + gu_recv)
+        return grad
+
+    up_parts = back_rows(gu_sum)
+    g_w_up = join_columns(up_parts, ff_blk)
 
     d_resid_norm, d_gain_m = norm_bwd(resid_mid, inv_mlp, gain_m, d_normed_mlp)
     d_resid = (grad_out.astype(F32) + d_resid_norm).astype(BF16)
     d_attn = dot('sd,ed->se', d_resid, w_o_full).astype(BF16)
     d_q, d_k, d_v, d_b_q, d_b_k, d_b_v = attn_bwd(qkv, d_attn, cos_t, sin_t, n_heads, n_kv)
-    gg_keep, _ = barrier((gg_keep, d_b_k))
-    g_w_gate = back_rows(gg_keep + gg_recv)
+    gg_keep, _, _ = barrier((gg_keep, d_b_k, up_parts))
+    g_w_gate = join_columns(back_rows(gg_keep + gg_recv), ff_blk)
     d_qkv = jnp.concatenate([d_q, d_k, d_v], axis=1)
     d_normed_attn = dot('se,de->sd', d_qkv, w_qkv).astype(BF16).astype(F32)
     d_hidden_norm, d_gain_a = norm_bwd(hidden, inv_attn, gain_a, d_normed_attn)

time: 893 us -> 960 us (1.075)
  Pallas kernels: 175 us -> 223 us
  matrix products: 264 us -> 282 us
  waiting for transfers between devices: 263 us -> 252 us
    pallas_call x1, Pallas kernels: 120 us -> 169 us  [scatter_all(): pl.pallas_call(lambda *refs: scatter_kernel(cols, *refs), out_shape=jax.S...]
    all_gather x1, waiting for transfers between devices: 6.28 us -> 38.5 us  [local_step(): qkv_full = lax.all_gather(qkv_loc, AX, axis=0, tiled=True)]
    dot_general x26, matrix products: 264 us -> 282 us  [dot(): return jnp.einsum(eq_form, lhs_arr, rhs_arr, preferred_element_type=F32)]
    reduce_scatter x4, waiting for transfers between devices: 15.1 us -> 0.02 us  [group_scatter(): lax.psum_scatter(arr, AX, scatter_dimension=0, tiled=True, axis_index_gro...]
    ppermute x5 -> x6, waiting for transfers between devices: 110 us -> 101 us  [z_pair(): return lax.ppermute(arr, AX, Z_PERM)]
    ppermute x7 -> x14, waiting for transfers between devices: 34.7 us -> 28 us  [local_step(): piece = lax.ppermute(piece, AX, [(i, i ^ d) for i in range(N_DEV)])]
    unnamed x145 -> x119, local copies, waits for them, and re-layouts: 22.3 us -> 17.1 us
  transfers between devices with their start and end apart: 31 -> 39, of which waited for: 13 -> 16; matrix products, arithmetic and copies ran while one was open for 42% -> 41% of each run, Pallas kernels for 20% -> 23%
where the time goes in v4:
time: 960 us; the launch traced here: 952 us
  matrix products  282 us (29%)
  waiting for transfers between devices  252 us (26%)
  Pallas kernels  223 us (23%)
  local copies, waits for them, and re-layouts  103 us (11%)
  other arithmetic  40.4 us (4%)
  starting transfers between devices  35.2 us (4%)
  between operations  15.3 us (2%)
    dot_general x26, matrix products, dot(): return jnp.einsum(eq_form, lhs_arr, rhs_arr, preferred_element_type=F32)  282 us
    pallas_call x1, Pallas kernels, scatter_all(): pl.pallas_call(lambda *refs: scatter_kernel(cols, *refs), out_shape=jax.S...  169 us
    ppermute x6, waiting for transfers between devices, z_pair(): return lax.ppermute(arr, AX, Z_PERM)  101 us
    ppermute x9, waiting for transfers between devices, xor_send(): return lax.ppermute(arr, AX, [(i, i ^ step) for i in range(N_DEV)])  72.4 us
    all_gather x1, waiting for transfers between devices, local_step(): qkv_full = lax.all_gather(qkv_loc, AX, axis=0, tiled=True)  38.5 us
    ppermute x14, waiting for transfers between devices, local_step(): piece = lax.ppermute(piece, AX, [(i, i ^ d) for i in range(N_DEV)])  28 us
  transfers between devices with their start and end apart: 39, of which 16 were waited for; matrix products, arithmetic and copies ran while one was open for 41% of the time, Pallas kernels for 23%

profile of v4, /device:TPU:0, one launch (start us, length us, event | category | flops | bytes accessed | tf_op | source)
XLA Modules:
  0.0 951.6 jit_solution(18220301237814201818)
XLA Ops:
  18.5 38.5 %all-gather.5.cloned.1.call-done = bf16[1536,2176]{1,0:T(8,128)(2,1)} async-done(((bf16[96,2176]{1,0:T(8,128)(2,1)}), bf16[1536,2176]{1,0:T(8,128)(2,1)}) %all-gather.5.cloned.1.call-update) | async-done | bytes 6684688 | tf_op jit(solution)/shard_map/all_gather | solution.py:435
  63.9 6.4 fusion.40.q_ref.k_ref.v_ref
  70.3 12.7 %attn_fwd.1 = bf16[512,1536]{1,0:T(8,128)(2,1)S(1)} custom-call(f32[512,2048]{1,0:T(8,128)S(1)} %fusion.40.q_ref.k_ref.v_ref, f32[512,2048]{1,0:T(8,128)S(1)} %fusion.40.q_ref.k_ref.v_ref, f32[512,2048]{1,0:T(8,128)S(1)} %fusion.40.q_ref.k_ref.v_ref, f32[512,128]{1,0:T(8,128)S(1)} %copy-done.7, f32[512,128]{1,0:T(8,128)S(1)} %copy-done.9), custom_call_target="tpu_custom_call" | custom-call | flops 8589934592 | bytes 6291456 | tf_op jit(solution)/shard_map/attn_fwd/pallas_call | solution.py:72
  86.2 10.2 %all-gather.7.cloned.1.call-done = bf16[1536,1536]{1,0:T(8,128)(2,1)} async-done(((bf16[96,1536]{1,0:T(8,128)(2,1)}), bf16[1536,1536]{1,0:T(8,128)(2,1)}) %all-gather.7.cloned.1.call-update) | async-done | bytes 4718608 | tf_op jit(solution)/shard_map/all_gather | solution.py:437
  96.3 6.0 fusion.38
  120.8 7.6 collective-permute-done.10
  130.1 2.6 collective-permute-start.1
  134.4 4.8 collective-permute-done.12
  145.9 3.8 copy.53
  160.0 14.0 %collective-permute-done.4 = bf16[1,96,1120]{2,1,0:T(8,128)(2,1)} collective-permute-done((bf16[1,96,1120]{2,1,0:T(8,128)(2,1)}, bf16[1,96,1120]{2,1,0:T(8,128)(2,1)}, u32[]{:S(2)}, u32[]{:S(2)}) %collective-permute-start.4) | collective-permute-done | bytes 215072 | tf_op jit(solution)/shard_map/ppermute | solution.py:447
  178.7 16.4 %collective-permute-done.16 = bf16[560,1536]{1,0:T(8,128)(2,1)} collective-permute-done((bf16[560,1536]{1,0:T(8,128)(2,1)S(1)}, bf16[560,1536]{1,0:T(8,128)(2,1)}, u32[]{:S(2)}, u32[]{:S(2)}) %collective-permute-start.16) | collective-permute-done | bytes 1720352 | tf_op jit(solution)/shard_map/ppermute | solution.py:381
  195.2 3.5 broadcast_select_fusion.5
  198.7 33.4 %collective-permute-done.15 = bf16[768,1120]{0,1:T(8,128)(2,1)} collective-permute-done((bf16[768,1120]{0,1:T(8,128)(2,1)}, bf16[768,1120]{0,1:T(8,128)(2,1)}, u32[]{:S(2)}, u32[]{:S(2)}) %collective-permute-start.15) | collective-permute-done | bytes 1720352 | tf_op jit(solution)/shard_map/ppermute | solution.py:381
  232.0 2.7 copy.54
  234.8 33.3 %collective-permute-done.7 = bf16[768,1120]{0,1:T(8,128)(2,1)} collective-permute-done((bf16[768,1120]{0,1:T(8,128)(2,1)}, bf16[768,1120]{0,1:T(8,128)(2,1)}, u32[]{:S(2)}, u32[]{:S(2)}) %collective-permute-start.7) | collective-permute-done | bytes 1720352 | tf_op jit(solution)/shard_map/ppermute | solution.py:381
  268.1 3.8 copy.51
  273.2 5.2 broadcast_select_fusion.1
  278.7 3.1 broadcast.74.clone
  283.9 3.2 broadcast.74.clone.1
  289.3 31.3 %collective-permute-done.20 = bf16[512,1536]{1,0:T(8,128)(2,1)} collective-permute-done((bf16[512,1536]{1,0:T(8,128)(2,1)}, bf16[512,1536]{1,0:T(8,128)(2,1)}, u32[]{:S(2)}, u32[]{:S(2)}) %collective-permute-start.20) | collective-permute-done | bytes 1572896 | tf_op jit(solution)/shard_map/ppermute | solution.py:396
  321.9 2.7 fusion.65
  324.6 2.6 bitcast_dynamic-update-slice_fusion.2
  327.3 21.1 %collective-permute-done.22 = bf16[256,1536]{1,0:T(8,128)(2,1)S(1)} collective-permute-done((bf16[256,1536]{1,0:T(8,128)(2,1)S(1)}, bf16[256,1536]{1,0:T(8,128)(2,1)S(1)}, u32[]{:S(2)}, u32[]{:S(2)}) %collective-permute-start.22) | collective-permute-done | bytes 786464 | tf_op jit(solution)/shard_map/ppermute | solution.py:396
  349.6 2.7 fusion.63
  355.5 11.8 %fusion.89 = f32[2048,1120]{0,1:T(8,128)} fusion(bf16[2048,1536]{1,0:T(8,128)(2,1)} %all-gather.9.cloned.1.call-done, bf16[768,1120]{1,0:T(8,128)(2,1)S(1)} %copy-done.26, bf16[768,1120]{1,0:T(8,128)(2,1)S(1)} %copy-done.27), kind=kOutput, calls=%fused_computation.198 | convolution fusion | flops 7053312000 | bytes 18907136 | tf_op jit(solution)/shard_map/sd,df->sf/dot_general | solution.py:23
  367.3 15.7 %multiply_convert_fusion.1 = (bf16[2048,1120]{0,1:T(8,128)(2,1)}, f32[2048,1120]{0,1:T(8,128)}) fusion(f32[2048,1120]{0,1:T(8,128)} %fusion.89, bf16[2048,1536]{1,0:T(8,128)(2,1)} %all-gather.9.cloned.1.call-done, bf16[768,1120]{1,0:T(8,128)(2,1)S(1)} %copy-done.29, bf16[768,1120]{1,0:T(8,128)(2,1)S(1)} %copy-done.28), kind=kOutput, calls=%fused_computation.17 | convolution fusion | flops 7067074560 | bytes 32669696 | tf_op jit(solution)/shard_map/sd,df->sf/dot_general | solution.py:23
  383.0 14.3 %fusion.83 = f32[2048,1536]{1,0:T(8,128)} fusion(bf16[2048,1120]{0,1:T(8,128)(2,1)} %get-tuple-element.57, bf16[560,1536]{1,0:T(8,128)(2,1)} %get-tuple-element.113, bf16[560,1536]{1,0:T(8,128)(2,1)} %get-tuple-element.112), kind=kOutput, calls=%fused_computation.192 | convolution fusion | flops 7053312000 | bytes 20611072 | tf_op jit(solution)/shard_map/sf,fd->sd/dot_general | solution.py:23
  397.3 18.2 %fusion.2 = (bf16[2048,1120]{0,1:T(8,128)(2,1)}, bf16[2048,1120]{0,1:T(8,128)(2,1)}) fusion(f32[2048,1120]{0,1:T(8,128)} %get-tuple-element.140, f32[2048,1120]{0,1:T(8,128)} %fusion.89, bf16[2048,1536]{1,0:T(8,128)(2,1)} %bitcast.34, bf16[560,1536]{1,0:T(8,128)(2,1)} %get-tuple-element.113, bf16[560,1536]{1,0:T(8,128)(2,1)} %get-tuple-element.112), kind=kOutput, calls=%fused_computation.7 | convolution fusion | flops 7087718400 | bytes 37257216 | tf_op jit(solution)/shard_map/sd,fd->sf/dot_general | solution.py:23
  415.5 14.1 %fusion.86 = f32[2048,1536]{1,0:T(8,128)} fusion(bf16[2048,1120]{0,1:T(8,128)(2,1)} %get-tuple-element.54, bf16[768,1120]{1,0:T(8,128)(2,1)} %get-tuple-element.95, bf16[768,1120]{1,0:T(8,128)(2,1)} %get-tuple-element.94), kind=kOutput, calls=%fused_computation.195 | convolution fusion | flops 7053312000 | bytes 20611072 | tf_op jit(solution)/shard_map/sf,df->sd/dot_general | solution.py:23
  429.7 14.8 %convolution_add_fusion.2 = f32[2048,1536]{1,0:T(8,128)} fusion(f32[2048,1536]{1,0:T(8,128)} %fusion.86, bf16[2048,1120]{0,1:T(8,128)(2,1)S(1)} %copy-done.47, bf16[768,1120]{1,0:T(8,128)(2,1)S(1)} %copy-done.26, bf16[768,1120]{1,0:T(8,128)(2,1)S(1)} %copy-done.27), kind=kOutput, calls=%fused_computation.20 | convolution fusion | flops 7056457728 | bytes 33193984 | tf_op jit(solution)/shard_map/sf,df->sd/dot_general | solution.py:23
  447.2 18.6 %collective-permute-done.24 = bf16[256,1536]{1,0:T(8,128)(2,1)S(1)} collective-permute-done((bf16[256,1536]{1,0:T(8,128)(2,1)S(1)}, bf16[256,1536]{1,0:T(8,128)(2,1)S(1)}, u32[]{:S(2)}, u32[]{:S(2)}) %collective-permute-start.24) | collective-permute-done | bytes 786464 | tf_op jit(solution)/shard_map/ppermute | solution.py:396
  469.0 14.1 %fusion.85 = f32[2048,1120]{0,1:T(8,128)} fusion(bf16[2048,1536]{1,0:T(8,128)(2,1)} %all-gather.11.cloned.1.call-done, bf16[768,1120]{1,0:T(8,128)(2,1)} %get-tuple-element.95, bf16[768,1120]{1,0:T(8,128)(2,1)} %get-tuple-element.94), kind=kOutput, calls=%fused_computation.194 | convolution fusion | flops 7053312000 | bytes 18907136 | tf_op jit(solution)/shard_map/sd,df->sf/dot_general | solution.py:23
  483.1 9.8 %fusion.88 = f32[2048,1120]{0,1:T(8,128)} fusion(bf16[2048,1536]{1,0:T(8,128)(2,1)S(1)} %copy-done.44, bf16[768,1120]{1,0:T(8,128)(2,1)S(1)} %copy-done.26, bf16[768,1120]{1,0:T(8,128)(2,1)S(1)} %copy-done.27), kind=kOutput, calls=%fused_computation.197 | convolution fusion | flops 7053312000 | bytes 18907136 | tf_op jit(solution)/shard_map/sd,df->sf/dot_general | solution.py:23
  492.9 19.9 %multiply_convert_fusion = (bf16[2048,1120]{0,1:T(8,128)(2,1)}, bf16[2048,1120]{0,1:T(8,128)(2,1)}, bf16[2048,1120]{0,1:T(8,128)(2,1)}) fusion(f32[2048,1120]{0,1:T(8,128)} %fusion.85, f32[2048,1120]{0,1:T(8,128)} %fusion.88, bf16[2048,1536]{1,0:T(8,128)(2,1)} %bitcast.43, bf16[560,1536]{1,0:T(8,128)(2,1)} %get-tuple-element.113, ...), kind=kOutput, calls=%fused_computation.15 | convolution fusion | flops 7094599680 | bytes 41844736 | tf_op jit(solution)/shard_map/sd,fd->sf/dot_general | solution.py:23
  512.7 14.3 %fusion.84 = f32[2048,1536]{1,0:T(8,128)} fusion(bf16[2048,1120]{0,1:T(8,128)(2,1)} %get-tuple-element.55, bf16[768,1120]{1,0:T(8,128)(2,1)} %get-tuple-element.95, bf16[768,1120]{1,0:T(8,128)(2,1)} %get-tuple-element.94), kind=kOutput, calls=%fused_computation.193 | convolution fusion | flops 7053312000 | bytes 20611072 | tf_op jit(solution)/shard_map/sf,df->sd/dot_general | solution.py:23
  527.0 14.8 %convolution_add_fusion.1 = f32[2048,1536]{1,0:T(8,128)} fusion(f32[2048,1536]{1,0:T(8,128)} %fusion.84, bf16[2048,1120]{0,1:T(8,128)(2,1)S(1)} %copy-done.45, bf16[768,1120]{1,0:T(8,128)(2,1)S(1)} %copy-done.26, bf16[768,1120]{1,0:T(8,128)(2,1)S(1)} %copy-done.27), kind=kOutput, calls=%fused_computation.19 | convolution fusion | flops 7056457728 | bytes 33193984 | tf_op jit(solution)/shard_map/sf,df->sd/dot_general | solution.py:23
  542.7 7.0 fusion.49
  549.7 9.4 convolution_add_fusion.4
  560.5 12.8 %fusion.94 = f32[1120,1536]{1,0:T(8,128)} fusion(bf16[2048,1120]{0,1:T(8,128)(2,1)} %get-tuple-element.57, bf16[2048,1536]{1,0:T(8,128)(2,1)} %bitcast.34), kind=kOutput, calls=%fused_computation.203 | convolution fusion | flops 7046430720 | bytes 17760256 | tf_op jit(solution)/shard_map/sf,sd->fd/dot_general | solution.py:23
  573.3 11.6 %convolution_add_fusion = f32[1120,1536]{1,0:T(8,128)S(1)} fusion(f32[1120,1536]{1,0:T(8,128)} %fusion.94, bf16[2048,1120]{0,1:T(8,128)(2,1)S(1)} %bitcast.162, bf16[2048,1536]{1,0:T(8,128)(2,1)} %bitcast.43), kind=kOutput, calls=%fused_computation.4 | convolution fusion | flops 7048151040 | bytes 24641536 | tf_op jit(solution)/shard_map/sf,sd->fd/dot_general | solution.py:23
  584.9 3.5 constant_dynamic-slice_fusion
  588.4 8.0 fusion.57
  596.4 5.7 fusion.55
  602.1 5.6 convolution_add_fusion.6
  607.7 11.3 %fusion.82 = f32[2048,1536]{1,0:T(8,128)} fusion(bf16[2048,1120]{0,1:T(8,128)(2,1)S(1)} %bitcast.162, bf16[560,1536]{1,0:T(8,128)(2,1)S(1)} %copy-done.32, bf16[560,1536]{1,0:T(8,128)(2,1)S(1)} %copy-done.31), kind=kOutput, calls=%fused_computation.191 | convolution fusion | flops 7053312000 | bytes 20611072 | tf_op jit(solution)/shard_map/sf,fd->sd/dot_general | solution.py:23
  619.0 16.9 %collective-permute-done.26 = f32[768,1120]{0,1:T(8,128)} collective-permute-done((f32[768,1120]{0,1:T(8,128)}, f32[768,1120]{0,1:T(8,128)}, u32[]{:S(2)}, u32[]{:S(2)}) %collective-permute-start.26) | collective-permute-done | bytes 3440672 | tf_op jit(solution)/shard_map/ppermute | solution.py:381
  636.0 11.4 %fusion.22 = f32[768,1120]{0,1:T(8,128)} fusion(f32[768,1120]{0,1:T(8,128)} %collective-permute-done.26, f32[768,1120]{0,1:T(8,128)S(1)} %copy-done.46, bf16[2048,1120]{0,1:T(8,128)(2,1)} %get-tuple-element.55, bf16[2048,1536]{1,0:T(8,128)(2,1)} %all-gather.11.cloned.1.call-done, s32[]{:T(128)S(6)} %select_n.139), kind=kOutput, calls=%fused_computation.44 | convolution fusion | flops 3524935680 | bytes 18055172 | tf_op jit(solution)/shard_map/sd,sf->df/dot_general | solution.py:23
  649.8 6.7 fusion.51
  656.5 9.7 %convolution_add_fusion.3 = f32[768,1120]{0,1:T(8,128)} fusion(f32[768,1120]{0,1:T(8,128)S(1)} %fusion.51, bf16[2048,1120]{0,1:T(8,128)(2,1)} %get-tuple-element.53, bf16[2048,1536]{1,0:T(8,128)(2,1)} %all-gather.11.cloned.1.call-done, s32[]{:T(128)S(6)} %select_n.140), kind=kOutput, calls=%fused_computation.41 | convolution fusion | flops 3524075520 | bytes 14614532 | tf_op jit(solution)/shard_map/sd,sf->df/dot_general | solution.py:23
  670.2 5.1 copy.59
  675.3 4.9 all-to-all-start
  685.4 5.2 convolution_convert_fusion.2.do_ref
  690.6 18.0 %attn_bwd.1 = (bf16[512,1536]{1,0:T(8,128)(2,1)S(1)}, bf16[512,256]{1,0:T(8,128)(2,1)S(1)}, bf16[512,256]{1,0:T(8,128)(2,1)S(1)}, f32[1,1536]{1,0:T(1,128)S(1)},...) custom-call(f32[512,2048]{1,0:T(8,128)S(1)} %copy-done.14, f32[512,2048]{1,0:T(8,128)S(1)} %copy-done.14, ...), custom_call_target="tpu_custom_call" | custom-call | flops 17179869184 | bytes 10485760 | tf_op jit(solution)/shard_map/attn_bwd/pallas_call | solution.py:139
  710.1 3.8 fusion.33
  713.9 2.9 fusion.60
  716.8 2.6 copy.58.refs_1_
  727.7 14.7 %attn_grads.1 = f32[1536,3840]{1,0:T(8,128)} custom-call(bf16[1536,512]{1,0:T(8,128)(2,1)S(1)} %bitcast.140, bf16[1536,512]{1,0:T(8,128)(2,1)S(1)} %copy-done.2, bf16[512,1536]{1,0:T(8,128)(2,1)S(1)} %fusion.30.refs_2_, bf16[512,2048]{1,0:T(8,128)(2,1)S(1)} %copy-done.6, f32[1536,256]{1,0:T(8,128)S(1)} %pad.9.refs_4_), custom_call_target="tpu_custom_call" | custom-call | flops 12884901888 | bytes 33554432 | tf_op jit(solution)/shard_map/attn_grads/pallas_call | solution.py:188
  743.8 3.6 add.208
  747.4 3.0 copy.60
  750.4 3.8 all-to-all-start.1
  754.2 168.6 %scatter_all.1 = f32[96,3840]{1,0:T(8,128)S(1)} custom-call(f32[2,2,2,2,96,3840]{5,4,3,2,1,0:T(8,128)} %bitcast.160), custom_call_target="tpu_custom_call" | custom-call | flops 64424509440 | bytes 67108864 | tf_op jit(solution)/shard_map/scatter_all/pallas_call | solution.py:359
  923.9 5.1 join_columns.3
  929.1 2.9 join_columns.2
  940.1 4.4 add.210
  (275 shorter events, 115.8 us)
Async XLA Ops:
  7.2 49.9 %all-gather.5.cloned.1.call-start = ((), (), s32[]{:S(2)}) async-start(), calls=%async_computation.6 | async-start | bytes 7102464 | tf_op jit(solution)/shard_map/all_gather | solution.py:435
  10.6 85.7 %all-gather.7.cloned.1.call-start = ((), (), s32[]{:S(2)}) async-start(), calls=%async_computation.7 | async-start | bytes 5013504 | tf_op jit(solution)/shard_map/all_gather | solution.py:437
  11.4 344.1 %all-gather.9.cloned.1.call-start = ((), (), s32[]{:S(2)}) async-start(), calls=%async_computation.8 | async-start | bytes 7077888 | tf_op jit(solution)/shard_map/all_gather | solution.py:388
  60.2 42.2 %copy-start.37 = (f32[1536]{0:T(1024)}, f32[1536]{0:T(1024)S(1)}, u32[]{:S(2)}) copy-start(f32[1536]{0:T(1024)S(1)} %get-tuple-element.78) | copy-start | bytes 18436
  63.9 6.4 copy-start.7
  63.9 6.4 copy-start.9
  105.2 363.8 %all-gather.11.cloned.1.call-start = ((), (), s32[]{:S(2)}) async-start(), calls=%async_computation.11 | async-start | bytes 7077888 | tf_op jit(solution)/shard_map/all_gather | solution.py:388
  107.5 7.2 collective-permute-start.8
  107.8 11.2 %collective-permute-start.9 = (bf16[1,96,1120]{2,1,0:T(8,128)(2,1)}, bf16[1,96,1120]{2,1,0:T(8,128)(2,1)}, u32[]{:S(2)}, u32[]{:S(2)}) collective-permute-start(bf16[1,96,1120]{2,1,0:T(8,128)(2,1)} %get-tuple-element.101), channel_id=1, source_target_pairs={{0,2},{1,3},{2,0},{3,1},{4,6},{5,7},{6,4},{7,5},{8,10},{9,11},{10,... | collective-permute-start | bytes 645128 | tf_op jit(solution)/shard_map/ppermute | solution.py:447
  109.3 19.2 %collective-permute-start.10 = (bf16[1,96,1120]{2,1,0:T(8,128)(2,1)}, bf16[1,96,1120]{2,1,0:T(8,128)(2,1)}, u32[]{:S(2)}, u32[]{:S(2)}) collective-permute-start(bf16[1,96,1120]{2,1,0:T(8,128)(2,1)} %get-tuple-element.100), channel_id=1, source_target_pairs={{0,3},{1,2},{2,1},{3,0},{4,7},{5,6},{6,5},{7,4},{8,11},{9,10},{10,... | collective-permute-start | bytes 645128 | tf_op jit(solution)/shard_map/ppermute | solution.py:447
  109.4 20.7 %collective-permute-start.11 = (bf16[1,96,1120]{2,1,0:T(8,128)(2,1)}, bf16[1,96,1120]{2,1,0:T(8,128)(2,1)}, u32[]{:S(2)}, u32[]{:S(2)}) collective-permute-start(bf16[1,96,1120]{2,1,0:T(8,128)(2,1)} %get-tuple-element.99), channel_id=1, source_target_pairs={{0,4},{1,5},{2,6},{3,7},{4,0},{5,1},{6,2},{7,3},{8,12},{9,13},{10,... | collective-permute-start | bytes 645128 | tf_op jit(solution)/shard_map/ppermute | solution.py:447
  110.9 28.3 %collective-permute-start.12 = (bf16[1,96,1120]{2,1,0:T(8,128)(2,1)}, bf16[1,96,1120]{2,1,0:T(8,128)(2,1)}, u32[]{:S(2)}, u32[]{:S(2)}) collective-permute-start(bf16[1,96,1120]{2,1,0:T(8,128)(2,1)} %get-tuple-element.98), channel_id=1, source_target_pairs={{0,5},{1,4},{2,7},{3,6},{4,1},{5,0},{6,3},{7,2},{8,13},{9,12},{10,... | collective-permute-start | bytes 645128 | tf_op jit(solution)/shard_map/ppermute | solution.py:447
  111.3 7.7 copy-start.35
  114.7 36.4 %copy-start.20 = (bf16[8,96,1120]{2,1,0:T(8,128)(2,1)S(1)}, bf16[8,96,1120]{2,1,0:T(8,128)(2,1)}, u32[]{:S(2)}) copy-start(bf16[8,96,1120]{2,1,0:T(8,128)(2,1)} %copy-done.19) | copy-start | bytes 5160964
  114.7 28.3 %collective-permute-start.13 = (bf16[1,96,1120]{2,1,0:T(8,128)(2,1)S(1)}, bf16[1,96,1120]{2,1,0:T(8,128)(2,1)S(1)}, u32[]{:S(2)}, u32[]{:S(2)}) collective-permute-start(bf16[1,96,1120]{2,1,0:T(8,128)(2,1)S(1)} %copy-done.36), channel_id=1, source_target_pairs={{0,6},{1,7},{2,4},{3,5},{4,2},{5,3},{6,0},{7,1},{8,14},{9,15},{10,... | collective-permute-start | bytes 645128 | tf_op jit(solution)/shard_map/ppermute | solution.py:447
  119.0 35.6 %copy-start.30 = (bf16[560,1536]{1,0:T(8,128)(2,1)S(1)}, bf16[560,1536]{1,0:T(8,128)(2,1)}, u32[]{:S(2)}) copy-start(bf16[560,1536]{1,0:T(8,128)(2,1)} %param.29) | copy-start | bytes 5160964
  119.0 26.2 %collective-permute-start.14 = (bf16[1,96,1120]{2,1,0:T(8,128)(2,1)S(1)}, bf16[1,96,1120]{2,1,0:T(8,128)(2,1)S(1)}, u32[]{:S(2)}, u32[]{:S(2)}) collective-permute-start(bf16[1,96,1120]{2,1,0:T(8,128)(2,1)S(1)} %copy-done.35), channel_id=1, source_target_pairs={{0,7},{1,6},{2,5},{3,4},{4,3},{5,2},{6,1},{7,0},{8,15},{9,14},{10,... | collective-permute-start | bytes 645128 | tf_op jit(solution)/shard_map/ppermute | solution.py:447
  128.5 21.3 %collective-permute-start = (bf16[1,96,1120]{2,1,0:T(8,128)(2,1)}, bf16[1,96,1120]{2,1,0:T(8,128)(2,1)}, u32[]{:S(2)}, u32[]{:S(2)}) collective-permute-start(bf16[1,96,1120]{2,1,0:T(8,128)(2,1)} %get-tuple-element.109), channel_id=1, source_target_pairs={{0,1},{1,0},{2,3},{3,2},{4,5},{5,4},{6,7},{7,6},{8,9},{9,8},{10,11... | collective-permute-start | bytes 645128 | tf_op jit(solution)/shard_map/ppermute | solution.py:447
  130.1 21.9 %collective-permute-start.1 = (bf16[1,96,1120]{2,1,0:T(8,128)(2,1)}, bf16[1,96,1120]{2,1,0:T(8,128)(2,1)}, u32[]{:S(2)}, u32[]{:S(2)}) collective-permute-start(bf16[1,96,1120]{2,1,0:T(8,128)(2,1)} %get-tuple-element.108), channel_id=1, source_target_pairs={{0,2},{1,3},{2,0},{3,1},{4,6},{5,7},{6,4},{7,5},{8,10},{9,11},{10,... | collective-permute-start | bytes 645128 | tf_op jit(solution)/shard_map/ppermute | solution.py:447
  139.2 15.4 %collective-permute-start.2 = (bf16[1,96,1120]{2,1,0:T(8,128)(2,1)}, bf16[1,96,1120]{2,1,0:T(8,128)(2,1)}, u32[]{:S(2)}, u32[]{:S(2)}) collective-permute-start(bf16[1,96,1120]{2,1,0:T(8,128)(2,1)} %get-tuple-element.107), channel_id=1, source_target_pairs={{0,3},{1,2},{2,1},{3,0},{4,7},{5,6},{6,5},{7,4},{8,11},{9,10},{10,... | collective-permute-start | bytes 645128 | tf_op jit(solution)/shard_map/ppermute | solution.py:447
  143.0 14.9 %collective-permute-start.3 = (bf16[1,96,1120]{2,1,0:T(8,128)(2,1)}, bf16[1,96,1120]{2,1,0:T(8,128)(2,1)}, u32[]{:S(2)}, u32[]{:S(2)}) collective-permute-start(bf16[1,96,1120]{2,1,0:T(8,128)(2,1)} %get-tuple-element.106), channel_id=1, source_target_pairs={{0,4},{1,5},{2,6},{3,7},{4,0},{5,1},{6,2},{7,3},{8,12},{9,13},{10,... | collective-permute-start | bytes 645128 | tf_op jit(solution)/shard_map/ppermute | solution.py:447
  145.2 28.8 %collective-permute-start.4 = (bf16[1,96,1120]{2,1,0:T(8,128)(2,1)}, bf16[1,96,1120]{2,1,0:T(8,128)(2,1)}, u32[]{:S(2)}, u32[]{:S(2)}) collective-permute-start(bf16[1,96,1120]{2,1,0:T(8,128)(2,1)} %get-tuple-element.105), channel_id=1, source_target_pairs={{0,5},{1,4},{2,7},{3,6},{4,1},{5,0},{6,3},{7,2},{8,13},{9,12},{10,... | collective-permute-start | bytes 645128 | tf_op jit(solution)/shard_map/ppermute | solution.py:447
  149.7 25.2 %collective-permute-start.5 = (bf16[1,96,1120]{2,1,0:T(8,128)(2,1)}, bf16[1,96,1120]{2,1,0:T(8,128)(2,1)S(1)}, u32[]{:S(2)}, u32[]{:S(2)}) collective-permute-start(bf16[1,96,1120]{2,1,0:T(8,128)(2,1)} %get-tuple-element.104), channel_id=1, source_target_pairs={{0,6},{1,7},{2,4},{3,5},{4,2},{5,3},{6,0},{7,1},{8,14},{9,15},{10,... | collective-permute-start | bytes 645128 | tf_op jit(solution)/shard_map/ppermute | solution.py:447
  152.1 22.9 %collective-permute-start.6 = (bf16[1,96,1120]{2,1,0:T(8,128)(2,1)}, bf16[1,96,1120]{2,1,0:T(8,128)(2,1)S(1)}, u32[]{:S(2)}, u32[]{:S(2)}) collective-permute-start(bf16[1,96,1120]{2,1,0:T(8,128)(2,1)} %get-tuple-element.103), channel_id=1, source_target_pairs={{0,7},{1,6},{2,5},{3,4},{4,3},{5,2},{6,1},{7,0},{8,15},{9,14},{10,... | collective-permute-start | bytes 645128 | tf_op jit(solution)/shard_map/ppermute | solution.py:447
  154.6 40.6 %collective-permute-start.16 = (bf16[560,1536]{1,0:T(8,128)(2,1)S(1)}, bf16[560,1536]{1,0:T(8,128)(2,1)}, u32[]{:S(2)}, u32[]{:S(2)}) collective-permute-start(bf16[560,1536]{1,0:T(8,128)(2,1)S(1)} %copy-done.30), channel_id=1, source_target_pairs={{0,8},{1,9},{2,10},{3,11},{4,12},{5,13},{6,14},{7,15},{8,0},{9,1},... | collective-permute-start | bytes 5160968 | tf_op jit(solution)/shard_map/ppermute | solution.py:381
  157.9 74.1 %collective-permute-start.15 = (bf16[768,1120]{0,1:T(8,128)(2,1)}, bf16[768,1120]{0,1:T(8,128)(2,1)}, u32[]{:S(2)}, u32[]{:S(2)}) collective-permute-start(bf16[768,1120]{0,1:T(8,128)(2,1)} %copy.53), channel_id=1, source_target_pairs={{0,8},{1,9},{2,10},{3,11},{4,12},{5,13},{6,14},{7,15},{8,0},{9,1},... | collective-permute-start | bytes 5160968 | tf_op jit(solution)/shard_map/ppermute | solution.py:381
  177.2 90.9 %collective-permute-start.7 = (bf16[768,1120]{0,1:T(8,128)(2,1)}, bf16[768,1120]{0,1:T(8,128)(2,1)}, u32[]{:S(2)}, u32[]{:S(2)}) collective-permute-start(bf16[768,1120]{0,1:T(8,128)(2,1)} %copy.50), channel_id=1, source_target_pairs={{0,8},{1,9},{2,10},{3,11},{4,12},{5,13},{6,14},{7,15},{8,0},{9,1},... | collective-permute-start | bytes 5160968 | tf_op jit(solution)/shard_map/ppermute | solution.py:381
  177.4 101.1 %collective-permute-start.18 = (bf16[512,1536]{1,0:T(8,128)(2,1)}, bf16[512,1536]{1,0:T(8,128)(2,1)}, u32[]{:S(2)}, u32[]{:S(2)}) collective-permute-start(bf16[512,1536]{1,0:T(8,128)(2,1)} %bitcast.6), channel_id=1, source_target_pairs={{0,2},{1,3},{2,0},{3,1},{4,6},{5,7},{6,4},{7,5},{8,10},{9,11},{10,... | collective-permute-start | bytes 4718600 | tf_op jit(solution)/shard_map/ppermute | solution.py:396
  271.9 50.0 %collective-permute-start.17 = (bf16[512,1536]{1,0:T(8,128)(2,1)}, bf16[512,1536]{1,0:T(8,128)(2,1)}, u32[]{:S(2)}, u32[]{:S(2)}) collective-permute-start(bf16[512,1536]{1,0:T(8,128)(2,1)} %bitcast.6), channel_id=1, source_target_pairs={{0,1},{1,0},{2,3},{3,2},{4,5},{5,4},{6,7},{7,6},{8,9},{9,8},{10,11... | collective-permute-start | bytes 4718600 | tf_op jit(solution)/shard_map/ppermute | solution.py:396
  271.9 48.7 %collective-permute-start.20 = (bf16[512,1536]{1,0:T(8,128)(2,1)}, bf16[512,1536]{1,0:T(8,128)(2,1)}, u32[]{:S(2)}, u32[]{:S(2)}) collective-permute-start(bf16[512,1536]{1,0:T(8,128)(2,1)} %bitcast.6), channel_id=1, source_target_pairs={{0,4},{1,5},{2,6},{3,7},{4,0},{5,1},{6,2},{7,3},{8,12},{9,13},{10,... | collective-permute-start | bytes 4718600 | tf_op jit(solution)/shard_map/ppermute | solution.py:396
  278.4 70.0 %collective-permute-start.19 = (bf16[512,1536]{1,0:T(8,128)(2,1)}, bf16[512,1536]{1,0:T(8,128)(2,1)S(1)}, u32[]{:S(2)}, u32[]{:S(2)}) collective-permute-start(bf16[512,1536]{1,0:T(8,128)(2,1)} %collective-permute-done.18), channel_id=1, source_target_pairs={{0,1},{1,0},{2,3},{3,2},{4,5},{5,4},{6,7},{7,6},{8,9},{9,8},{10,11... | collective-permute-start | bytes 4718600 | tf_op jit(solution)/shard_map/ppermute | solution.py:396
  283.9 363.5 %reduce-scatter.7.cloned.1.call-start = ((), (), s32[]{:S(2)}) async-start(), calls=%async_computation.10 | async-start | bytes 14155776 | tf_op jit(solution)/shard_map/reduce_scatter | solution.py:392
  321.8 26.6 %collective-permute-start.22 = (bf16[256,1536]{1,0:T(8,128)(2,1)S(1)}, bf16[256,1536]{1,0:T(8,128)(2,1)S(1)}, u32[]{:S(2)}, u32[]{:S(2)}) collective-permute-start(bf16[256,1536]{1,0:T(8,128)(2,1)S(1)} %slice.156), channel_id=1, source_target_pairs={{0,2},{1,3},{2,0},{3,1},{4,6},{5,7},{6,4},{7,5},{8,10},{9,11},{10,... | collective-permute-start | bytes 2359304 | tf_op jit(solution)/shard_map/ppermute | solution.py:396
  321.9 30.5 %collective-permute-start.21 = (bf16[512,1536]{1,0:T(8,128)(2,1)}, bf16[512,1536]{1,0:T(8,128)(2,1)S(1)}, u32[]{:S(2)}, u32[]{:S(2)}) collective-permute-start(bf16[512,1536]{1,0:T(8,128)(2,1)} %collective-permute-done.20), channel_id=1, source_target_pairs={{0,1},{1,0},{2,3},{3,2},{4,5},{5,4},{6,7},{7,6},{8,9},{9,8},{10,11... | collective-permute-start | bytes 4718600 | tf_op jit(solution)/shard_map/ppermute | solution.py:396
  348.4 6.1 collective-permute-start.23
  355.5 11.9 %copy-start.28 = (bf16[768,1120]{1,0:T(8,128)(2,1)S(1)}, bf16[768,1120]{1,0:T(8,128)(2,1)}, u32[]{:S(2)}) copy-start(bf16[768,1120]{1,0:T(8,128)(2,1)} %get-tuple-element.94) | copy-start | bytes 5160964
  355.5 11.8 %copy-start.29 = (bf16[768,1120]{1,0:T(8,128)(2,1)S(1)}, bf16[768,1120]{1,0:T(8,128)(2,1)}, u32[]{:S(2)}) copy-start(bf16[768,1120]{1,0:T(8,128)(2,1)} %get-tuple-element.95) | copy-start | bytes 5160964
  415.5 14.2 %copy-start.47 = (bf16[2048,1120]{0,1:T(8,128)(2,1)S(1)}, bf16[2048,1120]{0,1:T(8,128)(2,1)}, u32[]{:S(2)}) copy-start(bf16[2048,1120]{0,1:T(8,128)(2,1)} %get-tuple-element.51) | copy-start | bytes 13762564
  444.5 202.9 %reduce-scatter.9.cloned.1.call-start = ((), (), s32[]{:S(2)}) async-start(), calls=%async_computation.12 | async-start | bytes 14155776 | tf_op jit(solution)/shard_map/reduce_scatter | solution.py:392
  445.7 20.1 %collective-permute-start.24 = (bf16[256,1536]{1,0:T(8,128)(2,1)S(1)}, bf16[256,1536]{1,0:T(8,128)(2,1)S(1)}, u32[]{:S(2)}, u32[]{:S(2)}) collective-permute-start(bf16[256,1536]{1,0:T(8,128)(2,1)S(1)} %slice.159), channel_id=1, source_target_pairs={{0,4},{1,5},{2,6},{3,7},{4,0},{5,1},{6,2},{7,3},{8,12},{9,13},{10,... | collective-permute-start | bytes 2359304 | tf_op jit(solution)/shard_map/ppermute | solution.py:396
  465.8 2.3 collective-permute-start.25
  469.0 14.1 %copy-start.44 = (bf16[2048,1536]{1,0:T(8,128)(2,1)S(1)}, bf16[2048,1536]{1,0:T(8,128)(2,1)}, u32[]{:S(2)}) copy-start(bf16[2048,1536]{1,0:T(8,128)(2,1)} %all-gather.11.cloned.1.call-done) | copy-start | bytes 18874372
  512.7 14.3 %copy-start.45 = (bf16[2048,1120]{0,1:T(8,128)(2,1)S(1)}, bf16[2048,1120]{0,1:T(8,128)(2,1)}, u32[]{:S(2)}) copy-start(bf16[2048,1120]{0,1:T(8,128)(2,1)} %get-tuple-element.53) | copy-start | bytes 13762564
  541.8 390.1 %reduce-scatter.5.cloned.1.call-start = ((), (), s32[]{:S(2)}) async-start(), calls=%async_computation.9 | async-start | bytes 14155776 | tf_op jit(solution)/shard_map/reduce_scatter | solution.py:392
  541.9 7.8 slice-start.4
  542.6 389.4 %reduce-scatter.11.cloned.1.call-start = ((), (), s32[]{:S(2)}) async-start(), calls=%async_computation.13 | async-start | bytes 14155776 | tf_op jit(solution)/shard_map/reduce_scatter | solution.py:392
  542.7 7.1 slice-start.5
  549.7 23.5 %slice-start.6 = ((s8[4587520]{0:T(1024)(128)(4,1)}), s8[4194304]{0:T(1024)(128)(4,1)S(1)}, s32[]{:S(2)}) async-start(s8[4587520]{0:T(1024)(128)(4,1)} %bitcast.161), calls=%async_computation.20 | async-start | bytes 8388608
  559.1 14.2 %slice-start.7 = ((s8[4587520]{0:T(1024)(128)(4,1)}), s8[393216]{0:T(1024)(128)(4,1)S(1)}, s32[]{:S(2)}) async-start(s8[4587520]{0:T(1024)(128)(4,1)} %bitcast.161), calls=%async_computation.21 | async-start | bytes 786432
  559.1 76.9 %collective-permute-start.26 = (f32[768,1120]{0,1:T(8,128)}, f32[768,1120]{0,1:T(8,128)}, u32[]{:S(2)}, u32[]{:S(2)}) collective-permute-start(f32[768,1120]{0,1:T(8,128)} %convolution_add_fusion.4), channel_id=1, source_target_pairs={{0,8},{1,9},{2,10},{3,11},{4,12},{5,13},{6,14},{7,15},{8,0},{9,1},... | collective-permute-start | bytes 10321928 | tf_op jit(solution)/shard_map/ppermute | solution.py:381
  560.5 27.9 %slice-start.2 = ((s8[6291456]{0:T(1024)(128)(4,1)}), s8[4194304]{0:T(1024)(128)(4,1)S(1)}, s32[]{:S(2)}) async-start(s8[6291456]{0:T(1024)(128)(4,1)} %bitcast.156), calls=%async_computation.16 | async-start | bytes 8388608
  573.3 15.1 %slice-start.3 = ((s8[6291456]{0:T(1024)(128)(4,1)}), s8[2097152]{0:T(1024)(128)(4,1)S(1)}, s32[]{:S(2)}) async-start(s8[6291456]{0:T(1024)(128)(4,1)} %bitcast.156), calls=%async_computation.17 | async-start | bytes 4194304
  588.4 13.7 %slice-start.8 = ((s8[4587520]{0:T(1024)(128)(4,1)}), s8[4194304]{0:T(1024)(128)(4,1)S(1)}, s32[]{:S(2)}) async-start(s8[4587520]{0:T(1024)(128)(4,1)} %bitcast.163), calls=%async_computation.22 | async-start | bytes 8388608
  596.4 5.7 slice-start.9
  602.1 5.6 copy-start.31
  602.1 5.6 copy-start.32
  607.7 28.3 %copy-start.46 = (f32[768,1120]{0,1:T(8,128)S(1)}, f32[768,1120]{0,1:T(8,128)}, u32[]{:S(2)}) copy-start(f32[768,1120]{0,1:T(8,128)} %fusion.57) | copy-start | bytes 10321924
  656.5 11.7 %copy-start.34 = (f32[256,1536]{1,0:T(8,128)S(1)}, f32[256,1536]{1,0:T(8,128)}, u32[]{:S(2)}) copy-start(f32[256,1536]{1,0:T(8,128)} %reduce-scatter.9.cloned.1.call-done) | copy-start | bytes 4718596
  666.2 77.6 %collective-permute-start.27 = (f32[768,1120]{0,1:T(8,128)}, f32[768,1120]{0,1:T(8,128)}, u32[]{:S(2)}, u32[]{:S(2)}) collective-permute-start(f32[768,1120]{0,1:T(8,128)} %convolution_add_fusion.3), channel_id=1, source_target_pairs={{0,8},{1,9},{2,10},{3,11},{4,12},{5,13},{6,14},{7,15},{8,0},{9,1},... | collective-permute-start | bytes 10321928 | tf_op jit(solution)/shard_map/ppermute | solution.py:381
  668.0 271.3 %collective-permute-start.28 = (f32[560,1536]{1,0:T(8,128)}, f32[560,1536]{1,0:T(8,128)}, u32[]{:S(2)}, u32[]{:S(2)}) collective-permute-start(f32[560,1536]{1,0:T(8,128)} %get-tuple-element.92), channel_id=1, source_target_pairs={{0,8},{1,9},{2,10},{3,11},{4,12},{5,13},{6,14},{7,15},{8,0},{9,1},... | collective-permute-start | bytes 10321928 | tf_op jit(solution)/shard_map/ppermute | solution.py:381
  675.3 67.1 %all-to-all-start = ((f32[8,96,1120]{2,1,0:T(8,128)}), f32[8,96,1120]{2,1,0:T(8,128)}, u32[]{:S(2)}, u32[]{:S(2)}) async-start(f32[8,96,1120]{2,1,0:T(8,128)} %bitcast.143), calls=%async_computation.4 | async-start | bytes 7077888 | tf_op jit(solution)/shard_map/all_to_all | solution.py:525
  685.4 23.5 %slice-start = ((s8[6684672]{0:T(1024)(128)(4,1)}), s8[4194304]{0:T(1024)(128)(4,1)S(1)}, s32[]{:S(2)}) async-start(s8[6684672]{0:T(1024)(128)(4,1)} %bitcast.150), calls=%async_computation.14 | async-start | bytes 8388608
  690.6 18.4 %slice-start.1 = ((s8[6684672]{0:T(1024)(128)(4,1)}), s8[2490368]{0:T(1024)(128)(4,1)S(1)}, s32[]{:S(2)}) async-start(s8[6684672]{0:T(1024)(128)(4,1)} %bitcast.150), calls=%async_computation.15 | async-start | bytes 4980736
  750.4 178.6 %all-to-all-start.1 = ((f32[8,96,1120]{2,1,0:T(8,128)}), f32[8,96,1120]{2,1,0:T(8,128)S(1)}, u32[]{:S(2)}, u32[]{:S(2)}) async-start(f32[8,96,1120]{2,1,0:T(8,128)} %bitcast.144), calls=%async_computation.5 | async-start | bytes 7077888 | tf_op jit(solution)/shard_map/all_to_all | solution.py:525
  (33 other events, 91.6 us)
Sparse Core Ops, SparseCore 0:
  10.8 46.2 all-gather.4
  59.3 37.0 all-gather.6
  105.4 77.7 all-gather.8
  284.0 56.9 all-gather.10
  444.6 86.8 reduce-scatter.6
  541.9 86.7 reduce-scatter.8
  632.2 118.2 reduce-scatter.4
  753.9 146.0 reduce-scatter.10

commit v5 on v4

--- a/solution.py
+++ b/solution.py
@@ -257,6 +257,22 @@
     )(parts)
 
 
+def add_kernel(a_ref, b_ref, out_ref):
+    out_ref[...] = a_ref[...] + b_ref[...]
+
+
+def add_rows(lhs, rhs):
+    rows, cols = lhs.shape
+    blk = pl.BlockSpec((rows // 4, cols), lambda i: (i, 0))
+    return pl.pallas_call(
+        add_kernel, grid=(4,), in_specs=[blk, blk], out_specs=blk,
+        out_shape=jax.ShapeDtypeStruct((rows, cols), F32),
+        compiler_params=pltpu.CompilerParams(vmem_limit_bytes=24 << 20),
+        cost_estimate=pl.CostEstimate(flops=4 << 30, bytes_accessed=12 << 20, transcendentals=0),
+        name='add_rows',
+    )(lhs, rhs)
+
+
 def scatter_kernel(cols, g_ref, out_ref, own, from_core, buf1, buf2, buf3, load_sem, send_sem, recv_sem):
     dev = lax.axis_index(AX)
     me = (dev // 8, (dev // 4) % 2, (dev // 2) % 2)
@@ -460,11 +476,11 @@
     cos_t, sin_t = rope_tables(positions[0])
     normed_attn, inv_attn = norm_fwd(hidden, gain_a)
     qkv = dot('sd,de->se', normed_attn, w_qkv) + bias
-    qkv, grad_out = barrier((qkv, grad_out))
-    go_all = plane_gather(grad_out, rank)
     attn_out = attn_fwd(qkv, cos_t, sin_t, n_heads, n_kv)
     resid_mid = (hidden.astype(F32) + dot('se,ed->sd', attn_out, w_o_full)).astype(BF16)
     normed_mlp, inv_mlp = norm_fwd(resid_mid, gain_m)
+    grad_late, _ = barrier((grad_out, resid_mid))
+    go_all = plane_gather(grad_late, rank)
     n_ch = n_seq // CHUNKS
     h_all = [group_gather(normed_mlp[c * n_ch:(c + 1) * n_ch]) for c in range(CHUNKS)]
 
@@ -472,13 +488,14 @@
         return jnp.concatenate([jnp.where(z_zero, own, other), jnp.where(z_zero, other, own)], axis=0)
 
     w_g, w_u = z_order(own_rows[0], other_rows[0]), z_order(own_rows[1], other_rows[1])
-    w_d = z_order(w_down, down_other)
 
     pre = []
     for c in range(CHUNKS):
         gate_pre = dot('sd,df->sf', h_all[c], w_g)
         up_proj = dot('sd,df->sf', h_all[c], w_u)
         pre.append((gate_pre, up_proj))
+    down_late, _ = barrier((down_other, pre[0][0]))
+    w_d = z_order(w_down, down_late)
     acts, d_gates, d_ups, dn_sums = [], [], [], []
     gate_pre, up_proj = pre[0]
     act_first = (jax.nn.silu(gate_pre) * up_proj).astype(BF16)
@@ -516,7 +533,7 @@
     gg_keep = token_dot('sd,sf->df', h_keep, d_gates)
     gu_keep = token_dot('sd,sf->df', h_keep, d_ups)
     out_part = [dot('sf,fd->sd', act, w_d) for act in acts[1:]]
-    gu_sum = gu_keep + gu_recv
+    gu_sum = add_rows(gu_keep, gu_recv)
     dn_sums, gg_keep, gu_sum, out_part, wd_keep = barrier((dn_sums, gg_keep, gu_sum, out_part, wd_keep))
     d_normed_mlp = jnp.concatenate(dn_sums, axis=0).astype(BF16).astype(F32)
     out_sum = jnp.concatenate(out_sums + [group_scatter(part) for part in out_part], axis=0)
@@ -533,7 +550,7 @@
     d_attn = dot('sd,ed->se', d_resid, w_o_full).astype(BF16)
     d_q, d_k, d_v, d_b_q, d_b_k, d_b_v = attn_bwd(qkv, d_attn, cos_t, sin_t, n_heads, n_kv)
     gg_keep, _, _ = barrier((gg_keep, d_b_k, up_parts))
-    g_w_gate = join_columns(back_rows(gg_keep + gg_recv), ff_blk)
+    g_w_gate = join_columns(back_rows(add_rows(gg_keep, gg_recv)), ff_blk)
     d_qkv = jnp.concatenate([d_q, d_k, d_v], axis=1)
     d_normed_attn = dot('se,de->sd', d_qkv, w_qkv).astype(BF16).astype(F32)
     d_hidden_norm, d_gain_a = norm_bwd(hidden, inv_attn, gain_a, d_normed_attn)

time: 960 us -> 963 us (level)
  Pallas kernels: 223 us -> 178 us
  waiting for transfers between devices: 252 us -> 286 us
  local copies, waits for them, and re-layouts: 103 us -> 113 us
    pallas_call x1, Pallas kernels: 169 us -> 121 us  [scatter_all(): pl.pallas_call(lambda *refs: scatter_kernel(cols, *refs), out_shape=jax.S...]
    ppermute x6, waiting for transfers between devices: 101 us -> 133 us  [z_pair(): return lax.ppermute(arr, AX, Z_PERM)]
    ppermute x2 -> x4, local copies, waits for them, and re-layouts: 6.56 us -> 16.9 us  [z_pair(): return lax.ppermute(arr, AX, Z_PERM)]
    unnamed x119 -> x121, local copies, waits for them, and re-layouts: 17.1 us -> 22.7 us
  transfers between devices with their start and end apart: 39 -> 39, of which waited for: 16 -> 15; matrix products, arithmetic and copies ran while one was open for 41% -> 42% of each run, Pallas kernels for 23% -> 19%
where the time goes in v5:
time: 963 us; the launch traced here: 954 us
  matrix products  287 us (30%)
  waiting for transfers between devices  286 us (30%)
  Pallas kernels  178 us (18%)
  local copies, waits for them, and re-layouts  113 us (12%)
  other arithmetic  38.8 us (4%)
  starting transfers between devices  35.9 us (4%)
  between operations  15.3 us (2%)
    dot_general x26, matrix products, dot(): return jnp.einsum(eq_form, lhs_arr, rhs_arr, preferred_element_type=F32)  287 us
    ppermute x6, waiting for transfers between devices, z_pair(): return lax.ppermute(arr, AX, Z_PERM)  133 us
    pallas_call x1, Pallas kernels, scatter_all(): pl.pallas_call(lambda *refs: scatter_kernel(cols, *refs), out_shape=jax.S...  121 us
    ppermute x9, waiting for transfers between devices, xor_send(): return lax.ppermute(arr, AX, [(i, i ^ step) for i in range(N_DEV)])  72.1 us
    all_gather x1, waiting for transfers between devices, local_step(): qkv_full = lax.all_gather(qkv_loc, AX, axis=0, tiled=True)  38.5 us
    ppermute x14, waiting for transfers between devices, local_step(): piece = lax.ppermute(piece, AX, [(i, i ^ d) for i in range(N_DEV)])  30.4 us
    unnamed x121, local copies, waits for them, and re-layouts  22.7 us
  transfers between devices with their start and end apart: 39, of which 15 were waited for; matrix products, arithmetic and copies ran while one was open for 42% of the time, Pallas kernels for 19%

profile of v5, /device:TPU:0, one launch (start us, length us, event | category | flops | bytes accessed | tf_op | source)
XLA Modules:
  0.0 954.2 jit_solution(9690906523738953208)
XLA Ops:
  18.5 38.5 %all-gather.5.cloned.1.call-done = bf16[1536,2176]{1,0:T(8,128)(2,1)} async-done(((bf16[96,2176]{1,0:T(8,128)(2,1)}), bf16[1536,2176]{1,0:T(8,128)(2,1)}) %all-gather.5.cloned.1.call-update) | async-done | bytes 6684688 | tf_op jit(solution)/shard_map/all_gather | solution.py:451
  63.9 6.4 fusion.39.q_ref.k_ref.v_ref
  70.3 12.7 %attn_fwd.1 = bf16[512,1536]{1,0:T(8,128)(2,1)S(1)} custom-call(f32[512,2048]{1,0:T(8,128)S(1)} %fusion.39.q_ref.k_ref.v_ref, f32[512,2048]{1,0:T(8,128)S(1)} %fusion.39.q_ref.k_ref.v_ref, f32[512,2048]{1,0:T(8,128)S(1)} %fusion.39.q_ref.k_ref.v_ref, f32[512,128]{1,0:T(8,128)S(1)} %copy-done.10, f32[512,128]{1,0:T(8,128)S(1)} %copy-done.12), custom_call_target="tpu_custom_call" | custom-call | flops 8589934592 | bytes 6291456 | tf_op jit(solution)/shard_map/attn_fwd/pallas_call | solution.py:72
  86.1 10.2 %all-gather.7.cloned.1.call-done = bf16[1536,1536]{1,0:T(8,128)(2,1)} async-done(((bf16[96,1536]{1,0:T(8,128)(2,1)}), bf16[1536,1536]{1,0:T(8,128)(2,1)}) %all-gather.7.cloned.1.call-update) | async-done | bytes 4718608 | tf_op jit(solution)/shard_map/all_gather | solution.py:453
  96.3 6.0 fusion.37
  120.7 7.8 collective-permute-done.10
  134.4 4.8 collective-permute-done.12
  146.0 2.6 copy.85
  155.5 3.6 collective-permute-done.3
  160.0 14.0 %collective-permute-done.4 = bf16[1,96,1120]{2,1,0:T(8,128)(2,1)} collective-permute-done((bf16[1,96,1120]{2,1,0:T(8,128)(2,1)}, bf16[1,96,1120]{2,1,0:T(8,128)(2,1)}, u32[]{:S(2)}, u32[]{:S(2)}) %collective-permute-start.4) | collective-permute-done | bytes 215072 | tf_op jit(solution)/shard_map/ppermute | solution.py:463
  179.7 14.3 %collective-permute-done.15 = bf16[768,1120]{0,1:T(8,128)(2,1)} collective-permute-done((bf16[768,1120]{0,1:T(8,128)(2,1)S(1)}, bf16[768,1120]{0,1:T(8,128)(2,1)}, u32[]{:S(2)}, u32[]{:S(2)}) %collective-permute-start.15) | collective-permute-done | bytes 1720352 | tf_op jit(solution)/shard_map/ppermute | solution.py:397
  194.1 2.7 copy.86
  196.8 34.1 %collective-permute-done.7 = bf16[768,1120]{0,1:T(8,128)(2,1)} collective-permute-done((bf16[768,1120]{0,1:T(8,128)(2,1)}, bf16[768,1120]{0,1:T(8,128)(2,1)}, u32[]{:S(2)}, u32[]{:S(2)}) %collective-permute-start.7) | collective-permute-done | bytes 1720352 | tf_op jit(solution)/shard_map/ppermute | solution.py:397
  230.9 3.8 copy.83
  236.3 5.2 broadcast_select_fusion.1
  241.7 3.2 broadcast.74.clone
  247.0 3.2 broadcast.74.clone.1
  252.4 31.3 %collective-permute-done.20 = bf16[512,1536]{1,0:T(8,128)(2,1)} collective-permute-done((bf16[512,1536]{1,0:T(8,128)(2,1)}, bf16[512,1536]{1,0:T(8,128)(2,1)}, u32[]{:S(2)}, u32[]{:S(2)}) %collective-permute-start.20) | collective-permute-done | bytes 1572896 | tf_op jit(solution)/shard_map/ppermute | solution.py:412
  285.0 2.6 fusion.64
  287.6 2.6 bitcast_dynamic-update-slice_fusion.2
  290.3 21.0 %collective-permute-done.22 = bf16[256,1536]{1,0:T(8,128)(2,1)S(1)} collective-permute-done((bf16[256,1536]{1,0:T(8,128)(2,1)S(1)}, bf16[256,1536]{1,0:T(8,128)(2,1)S(1)}, u32[]{:S(2)}, u32[]{:S(2)}) %collective-permute-start.22) | collective-permute-done | bytes 786464 | tf_op jit(solution)/shard_map/ppermute | solution.py:412
  312.5 2.6 fusion.62
  318.3 11.9 %fusion.88 = f32[2048,1120]{0,1:T(8,128)} fusion(bf16[2048,1536]{1,0:T(8,128)(2,1)} %all-gather.9.cloned.1.call-done, bf16[768,1120]{1,0:T(8,128)(2,1)S(1)} %copy-done.30, bf16[768,1120]{1,0:T(8,128)(2,1)S(1)} %copy-done.31), kind=kOutput, calls=%fused_computation.197 | convolution fusion | flops 7053312000 | bytes 18907136 | tf_op jit(solution)/shard_map/sd,df->sf/dot_general | solution.py:23
  330.2 4.0 broadcast_select_fusion.5
  334.3 15.5 %multiply_convert_fusion.1 = (bf16[2048,1120]{0,1:T(8,128)(2,1)}, f32[2048,1120]{0,1:T(8,128)}) fusion(f32[2048,1120]{0,1:T(8,128)} %fusion.88, bf16[2048,1536]{1,0:T(8,128)(2,1)} %all-gather.9.cloned.1.call-done, bf16[768,1120]{1,0:T(8,128)(2,1)S(1)} %copy-done.33, bf16[768,1120]{1,0:T(8,128)(2,1)S(1)} %copy-done.32), kind=kOutput, calls=%fused_computation.17 | convolution fusion | flops 7067074560 | bytes 32669696 | tf_op jit(solution)/shard_map/sd,df->sf/dot_general | solution.py:23
  349.8 14.2 %fusion.82 = f32[2048,1536]{1,0:T(8,128)} fusion(bf16[2048,1120]{0,1:T(8,128)(2,1)} %get-tuple-element.57, bf16[560,1536]{1,0:T(8,128)(2,1)} %get-tuple-element.113, bf16[560,1536]{1,0:T(8,128)(2,1)} %get-tuple-element.112), kind=kOutput, calls=%fused_computation.191 | convolution fusion | flops 7053312000 | bytes 20611072 | tf_op jit(solution)/shard_map/sf,fd->sd/dot_general | solution.py:23
  364.1 18.0 %fusion.2 = (bf16[2048,1120]{0,1:T(8,128)(2,1)}, bf16[2048,1120]{0,1:T(8,128)(2,1)}) fusion(f32[2048,1120]{0,1:T(8,128)} %get-tuple-element.140, f32[2048,1120]{0,1:T(8,128)} %fusion.88, bf16[2048,1536]{1,0:T(8,128)(2,1)} %bitcast.34, bf16[560,1536]{1,0:T(8,128)(2,1)} %get-tuple-element.113, bf16[560,1536]{1,0:T(8,128)(2,1)} %get-tuple-element.112), kind=kOutput, calls=%fused_computation.7 | convolution fusion | flops 7087718400 | bytes 37257216 | tf_op jit(solution)/shard_map/sd,fd->sf/dot_general | solution.py:23
  382.1 14.1 %fusion.85 = f32[2048,1536]{1,0:T(8,128)} fusion(bf16[2048,1120]{0,1:T(8,128)(2,1)} %get-tuple-element.54, bf16[768,1120]{1,0:T(8,128)(2,1)} %get-tuple-element.95, bf16[768,1120]{1,0:T(8,128)(2,1)} %get-tuple-element.94), kind=kOutput, calls=%fused_computation.194 | convolution fusion | flops 7053312000 | bytes 20611072 | tf_op jit(solution)/shard_map/sf,df->sd/dot_general | solution.py:23
  396.2 14.7 %convolution_add_fusion.2 = f32[2048,1536]{1,0:T(8,128)} fusion(f32[2048,1536]{1,0:T(8,128)} %fusion.85, bf16[2048,1120]{0,1:T(8,128)(2,1)S(1)} %copy-done.48, bf16[768,1120]{1,0:T(8,128)(2,1)S(1)} %copy-done.30, bf16[768,1120]{1,0:T(8,128)(2,1)S(1)} %copy-done.31), kind=kOutput, calls=%fused_computation.20 | convolution fusion | flops 7056457728 | bytes 33193984 | tf_op jit(solution)/shard_map/sf,df->sd/dot_general | solution.py:23
  413.7 18.5 %collective-permute-done.24 = bf16[256,1536]{1,0:T(8,128)(2,1)S(1)} collective-permute-done((bf16[256,1536]{1,0:T(8,128)(2,1)S(1)}, bf16[256,1536]{1,0:T(8,128)(2,1)S(1)}, u32[]{:S(2)}, u32[]{:S(2)}) %collective-permute-start.24) | collective-permute-done | bytes 786464 | tf_op jit(solution)/shard_map/ppermute | solution.py:412
  435.4 14.3 %fusion.84 = f32[2048,1120]{0,1:T(8,128)} fusion(bf16[2048,1536]{1,0:T(8,128)(2,1)} %all-gather.11.cloned.1.call-done, bf16[768,1120]{1,0:T(8,128)(2,1)} %get-tuple-element.95, bf16[768,1120]{1,0:T(8,128)(2,1)} %get-tuple-element.94), kind=kOutput, calls=%fused_computation.193 | convolution fusion | flops 7053312000 | bytes 18907136 | tf_op jit(solution)/shard_map/sd,df->sf/dot_general | solution.py:23
  449.8 9.9 %fusion.87 = f32[2048,1120]{0,1:T(8,128)} fusion(bf16[2048,1536]{1,0:T(8,128)(2,1)S(1)} %copy-done.46, bf16[768,1120]{1,0:T(8,128)(2,1)S(1)} %copy-done.30, bf16[768,1120]{1,0:T(8,128)(2,1)S(1)} %copy-done.31), kind=kOutput, calls=%fused_computation.196 | convolution fusion | flops 7053312000 | bytes 18907136 | tf_op jit(solution)/shard_map/sd,df->sf/dot_general | solution.py:23
  459.6 19.8 %multiply_convert_fusion = (bf16[2048,1120]{0,1:T(8,128)(2,1)}, bf16[2048,1120]{0,1:T(8,128)(2,1)}, bf16[2048,1120]{0,1:T(8,128)(2,1)}) fusion(f32[2048,1120]{0,1:T(8,128)} %fusion.84, f32[2048,1120]{0,1:T(8,128)} %fusion.87, bf16[2048,1536]{1,0:T(8,128)(2,1)} %bitcast.43, bf16[560,1536]{1,0:T(8,128)(2,1)} %get-tuple-element.113, ...), kind=kOutput, calls=%fused_computation.15 | convolution fusion | flops 7094599680 | bytes 41844736 | tf_op jit(solution)/shard_map/sd,fd->sf/dot_general | solution.py:23
  479.5 14.3 %fusion.83 = f32[2048,1536]{1,0:T(8,128)} fusion(bf16[2048,1120]{0,1:T(8,128)(2,1)} %get-tuple-element.55, bf16[768,1120]{1,0:T(8,128)(2,1)} %get-tuple-element.95, bf16[768,1120]{1,0:T(8,128)(2,1)} %get-tuple-element.94), kind=kOutput, calls=%fused_computation.192 | convolution fusion | flops 7053312000 | bytes 20611072 | tf_op jit(solution)/shard_map/sf,df->sd/dot_general | solution.py:23
  493.8 14.8 %convolution_add_fusion.1 = f32[2048,1536]{1,0:T(8,128)} fusion(f32[2048,1536]{1,0:T(8,128)} %fusion.83, bf16[2048,1120]{0,1:T(8,128)(2,1)S(1)} %copy-done.47, bf16[768,1120]{1,0:T(8,128)(2,1)S(1)} %copy-done.30, bf16[768,1120]{1,0:T(8,128)(2,1)S(1)} %copy-done.31), kind=kOutput, calls=%fused_computation.19 | convolution fusion | flops 7056457728 | bytes 33193984 | tf_op jit(solution)/shard_map/sf,df->sd/dot_general | solution.py:23
  509.4 7.0 fusion.54
  516.4 9.2 convolution_add_fusion.5
  525.6 3.4 copy.90.a_ref
  529.0 6.5 fusion.48
  535.5 8.9 convolution_add_fusion.4
  546.0 13.1 %fusion.93 = f32[1120,1536]{1,0:T(8,128)} fusion(bf16[2048,1120]{0,1:T(8,128)(2,1)} %get-tuple-element.57, bf16[2048,1536]{1,0:T(8,128)(2,1)} %bitcast.34), kind=kOutput, calls=%fused_computation.202 | convolution fusion | flops 7046430720 | bytes 17760256 | tf_op jit(solution)/shard_map/sf,sd->fd/dot_general | solution.py:23
  559.1 11.3 %convolution_add_fusion = f32[1120,1536]{1,0:T(8,128)S(1)} fusion(f32[1120,1536]{1,0:T(8,128)} %fusion.93, bf16[2048,1120]{0,1:T(8,128)(2,1)S(1)} %bitcast.164, bf16[2048,1536]{1,0:T(8,128)(2,1)} %bitcast.43), kind=kOutput, calls=%fused_computation.4 | convolution fusion | flops 7048151040 | bytes 24641536 | tf_op jit(solution)/shard_map/sf,sd->fd/dot_general | solution.py:23
  570.4 3.3 constant_dynamic-slice_fusion
  573.8 9.5 fusion.56
  583.3 7.9 fusion.50
  591.2 8.9 convolution_add_fusion.6.a_ref
  600.1 11.7 %fusion.81 = f32[2048,1536]{1,0:T(8,128)} fusion(bf16[2048,1120]{0,1:T(8,128)(2,1)S(1)} %bitcast.164, bf16[560,1536]{1,0:T(8,128)(2,1)S(1)} %copy-done.35, bf16[560,1536]{1,0:T(8,128)(2,1)S(1)} %copy-done.34), kind=kOutput, calls=%fused_computation.190 | convolution fusion | flops 7053312000 | bytes 20611072 | tf_op jit(solution)/shard_map/sf,fd->sd/dot_general | solution.py:23
  611.8 9.5 collective-permute-done.26
  621.4 5.2 copy.91.b_ref
  631.0 10.2 %convolution_add_fusion.3 = f32[768,1120]{0,1:T(8,128)} fusion(f32[768,1120]{0,1:T(8,128)} %fusion.50, bf16[2048,1120]{0,1:T(8,128)(2,1)} %get-tuple-element.53, bf16[2048,1536]{1,0:T(8,128)(2,1)} %all-gather.11.cloned.1.call-done, s32[]{:T(128)S(6)} %select_n.140), kind=kOutput, calls=%fused_computation.41 | convolution fusion | flops 3524075520 | bytes 14614532 | tf_op jit(solution)/shard_map/sd,sf->df/dot_general | solution.py:23
  644.1 74.7 %collective-permute-done.27 = f32[768,1120]{0,1:T(8,128)} collective-permute-done((f32[768,1120]{0,1:T(8,128)}, f32[768,1120]{0,1:T(8,128)}, u32[]{:S(2)}, u32[]{:S(2)}) %collective-permute-start.27) | collective-permute-done | bytes 3440672 | tf_op jit(solution)/shard_map/ppermute | solution.py:397
  718.9 5.1 copy.95.b_ref
  727.3 4.8 all-to-all-start
  734.8 2.6 fusion.29.refs_2_
  737.5 5.1 convolution_convert_fusion.2.do_ref
  742.6 18.0 %attn_bwd.1 = (bf16[512,1536]{1,0:T(8,128)(2,1)S(1)}, bf16[512,256]{1,0:T(8,128)(2,1)S(1)}, bf16[512,256]{1,0:T(8,128)(2,1)S(1)}, f32[1,1536]{1,0:T(1,128)S(1)},...) custom-call(f32[512,2048]{1,0:T(8,128)S(1)} %copy-done.18, f32[512,2048]{1,0:T(8,128)S(1)} %copy-done.18, ...), custom_call_target="tpu_custom_call" | custom-call | flops 17179869184 | bytes 10485760 | tf_op jit(solution)/shard_map/attn_bwd/pallas_call | solution.py:139
  762.1 3.8 fusion.32
  765.9 2.9 fusion.59
  779.1 14.3 %attn_grads.1 = f32[1536,3840]{1,0:T(8,128)} custom-call(bf16[1536,512]{1,0:T(8,128)(2,1)S(1)} %bitcast.142, bf16[1536,512]{1,0:T(8,128)(2,1)S(1)} %copy-done.5, bf16[512,1536]{1,0:T(8,128)(2,1)S(1)} %fusion.29.refs_2_, bf16[512,2048]{1,0:T(8,128)(2,1)S(1)} %copy-done.9, f32[1536,256]{1,0:T(8,128)S(1)} %pad.9.refs_4_), custom_call_target="tpu_custom_call" | custom-call | flops 12884901888 | bytes 33554432 | tf_op jit(solution)/shard_map/attn_grads/pallas_call | solution.py:188
  799.6 4.4 all-to-all-start.1
  804.0 121.4 %scatter_all.1 = f32[96,3840]{1,0:T(8,128)S(1)} custom-call(f32[2,2,2,2,96,3840]{5,4,3,2,1,0:T(8,128)} %bitcast.162), custom_call_target="tpu_custom_call" | custom-call | flops 64424509440 | bytes 67108864 | tf_op jit(solution)/shard_map/scatter_all/pallas_call | solution.py:375
  926.5 5.1 join_columns.3
  931.6 2.9 join_columns.2
  942.7 4.4 add.202
  (279 shorter events, 126.0 us)
Async XLA Ops:
  7.2 49.9 %all-gather.5.cloned.1.call-start = ((), (), s32[]{:S(2)}) async-start(), calls=%async_computation.6 | async-start | bytes 7102464 | tf_op jit(solution)/shard_map/all_gather | solution.py:451
  10.6 85.7 %all-gather.7.cloned.1.call-start = ((), (), s32[]{:S(2)}) async-start(), calls=%async_computation.7 | async-start | bytes 5013504 | tf_op jit(solution)/shard_map/all_gather | solution.py:453
  11.4 306.9 %all-gather.9.cloned.1.call-start = ((), (), s32[]{:S(2)}) async-start(), calls=%async_computation.8 | async-start | bytes 7077888 | tf_op jit(solution)/shard_map/all_gather | solution.py:404
  60.2 42.2 %copy-start.39 = (f32[1536]{0:T(1024)}, f32[1536]{0:T(1024)S(1)}, u32[]{:S(2)}) copy-start(f32[1536]{0:T(1024)S(1)} %get-tuple-element.78) | copy-start | bytes 18436
  63.9 6.4 copy-start.10
  63.9 6.4 copy-start.12
  105.2 330.2 %all-gather.11.cloned.1.call-start = ((), (), s32[]{:S(2)}) async-start(), calls=%async_computation.11 | async-start | bytes 7077888 | tf_op jit(solution)/shard_map/all_gather | solution.py:404
  107.6 7.2 collective-permute-start.8
  107.8 11.2 %collective-permute-start.9 = (bf16[1,96,1120]{2,1,0:T(8,128)(2,1)}, bf16[1,96,1120]{2,1,0:T(8,128)(2,1)}, u32[]{:S(2)}, u32[]{:S(2)}) collective-permute-start(bf16[1,96,1120]{2,1,0:T(8,128)(2,1)} %get-tuple-element.101), channel_id=1, source_target_pairs={{0,2},{1,3},{2,0},{3,1},{4,6},{5,7},{6,4},{7,5},{8,10},{9,11},{10,... | collective-permute-start | bytes 645128 | tf_op jit(solution)/shard_map/ppermute | solution.py:463
  109.3 19.2 %collective-permute-start.10 = (bf16[1,96,1120]{2,1,0:T(8,128)(2,1)}, bf16[1,96,1120]{2,1,0:T(8,128)(2,1)}, u32[]{:S(2)}, u32[]{:S(2)}) collective-permute-start(bf16[1,96,1120]{2,1,0:T(8,128)(2,1)} %get-tuple-element.100), channel_id=1, source_target_pairs={{0,3},{1,2},{2,1},{3,0},{4,7},{5,6},{6,5},{7,4},{8,11},{9,10},{10,... | collective-permute-start | bytes 645128 | tf_op jit(solution)/shard_map/ppermute | solution.py:463
  109.4 20.7 %collective-permute-start.11 = (bf16[1,96,1120]{2,1,0:T(8,128)(2,1)}, bf16[1,96,1120]{2,1,0:T(8,128)(2,1)}, u32[]{:S(2)}, u32[]{:S(2)}) collective-permute-start(bf16[1,96,1120]{2,1,0:T(8,128)(2,1)} %get-tuple-element.99), channel_id=1, source_target_pairs={{0,4},{1,5},{2,6},{3,7},{4,0},{5,1},{6,2},{7,3},{8,12},{9,13},{10,... | collective-permute-start | bytes 645128 | tf_op jit(solution)/shard_map/ppermute | solution.py:463
  110.9 28.3 %collective-permute-start.12 = (bf16[1,96,1120]{2,1,0:T(8,128)(2,1)}, bf16[1,96,1120]{2,1,0:T(8,128)(2,1)}, u32[]{:S(2)}, u32[]{:S(2)}) collective-permute-start(bf16[1,96,1120]{2,1,0:T(8,128)(2,1)} %get-tuple-element.98), channel_id=1, source_target_pairs={{0,5},{1,4},{2,7},{3,6},{4,1},{5,0},{6,3},{7,2},{8,13},{9,12},{10,... | collective-permute-start | bytes 645128 | tf_op jit(solution)/shard_map/ppermute | solution.py:463
  111.3 7.7 copy-start.37
  114.7 35.3 %copy-start.24 = (bf16[8,96,1120]{2,1,0:T(8,128)(2,1)S(1)}, bf16[8,96,1120]{2,1,0:T(8,128)(2,1)}, u32[]{:S(2)}) copy-start(bf16[8,96,1120]{2,1,0:T(8,128)(2,1)} %copy-done.23) | copy-start | bytes 5160964
  114.7 28.3 %collective-permute-start.13 = (bf16[1,96,1120]{2,1,0:T(8,128)(2,1)S(1)}, bf16[1,96,1120]{2,1,0:T(8,128)(2,1)S(1)}, u32[]{:S(2)}, u32[]{:S(2)}) collective-permute-start(bf16[1,96,1120]{2,1,0:T(8,128)(2,1)S(1)} %copy-done.38), channel_id=1, source_target_pairs={{0,6},{1,7},{2,4},{3,5},{4,2},{5,3},{6,0},{7,1},{8,14},{9,15},{10,... | collective-permute-start | bytes 645128 | tf_op jit(solution)/shard_map/ppermute | solution.py:463
  119.0 26.2 %collective-permute-start.14 = (bf16[1,96,1120]{2,1,0:T(8,128)(2,1)S(1)}, bf16[1,96,1120]{2,1,0:T(8,128)(2,1)S(1)}, u32[]{:S(2)}, u32[]{:S(2)}) collective-permute-start(bf16[1,96,1120]{2,1,0:T(8,128)(2,1)S(1)} %copy-done.37), channel_id=1, source_target_pairs={{0,7},{1,6},{2,5},{3,4},{4,3},{5,2},{6,1},{7,0},{8,15},{9,14},{10,... | collective-permute-start | bytes 645128 | tf_op jit(solution)/shard_map/ppermute | solution.py:463
  128.5 20.0 %collective-permute-start = (bf16[1,96,1120]{2,1,0:T(8,128)(2,1)}, bf16[1,96,1120]{2,1,0:T(8,128)(2,1)}, u32[]{:S(2)}, u32[]{:S(2)}) collective-permute-start(bf16[1,96,1120]{2,1,0:T(8,128)(2,1)} %get-tuple-element.109), channel_id=1, source_target_pairs={{0,1},{1,0},{2,3},{3,2},{4,5},{5,4},{6,7},{7,6},{8,9},{9,8},{10,11... | collective-permute-start | bytes 645128 | tf_op jit(solution)/shard_map/ppermute | solution.py:463
  130.2 20.8 %collective-permute-start.1 = (bf16[1,96,1120]{2,1,0:T(8,128)(2,1)}, bf16[1,96,1120]{2,1,0:T(8,128)(2,1)}, u32[]{:S(2)}, u32[]{:S(2)}) collective-permute-start(bf16[1,96,1120]{2,1,0:T(8,128)(2,1)} %get-tuple-element.108), channel_id=1, source_target_pairs={{0,2},{1,3},{2,0},{3,1},{4,6},{5,7},{6,4},{7,5},{8,10},{9,11},{10,... | collective-permute-start | bytes 645128 | tf_op jit(solution)/shard_map/ppermute | solution.py:463
  139.2 14.2 %collective-permute-start.2 = (bf16[1,96,1120]{2,1,0:T(8,128)(2,1)}, bf16[1,96,1120]{2,1,0:T(8,128)(2,1)}, u32[]{:S(2)}, u32[]{:S(2)}) collective-permute-start(bf16[1,96,1120]{2,1,0:T(8,128)(2,1)} %get-tuple-element.107), channel_id=1, source_target_pairs={{0,3},{1,2},{2,1},{3,0},{4,7},{5,6},{6,5},{7,4},{8,11},{9,10},{10,... | collective-permute-start | bytes 645128 | tf_op jit(solution)/shard_map/ppermute | solution.py:463
  143.0 16.0 %collective-permute-start.3 = (bf16[1,96,1120]{2,1,0:T(8,128)(2,1)}, bf16[1,96,1120]{2,1,0:T(8,128)(2,1)}, u32[]{:S(2)}, u32[]{:S(2)}) collective-permute-start(bf16[1,96,1120]{2,1,0:T(8,128)(2,1)} %get-tuple-element.106), channel_id=1, source_target_pairs={{0,4},{1,5},{2,6},{3,7},{4,0},{5,1},{6,2},{7,3},{8,12},{9,13},{10,... | collective-permute-start | bytes 645128 | tf_op jit(solution)/shard_map/ppermute | solution.py:463
  145.3 28.8 %collective-permute-start.4 = (bf16[1,96,1120]{2,1,0:T(8,128)(2,1)}, bf16[1,96,1120]{2,1,0:T(8,128)(2,1)}, u32[]{:S(2)}, u32[]{:S(2)}) collective-permute-start(bf16[1,96,1120]{2,1,0:T(8,128)(2,1)} %get-tuple-element.105), channel_id=1, source_target_pairs={{0,5},{1,4},{2,7},{3,6},{4,1},{5,0},{6,3},{7,2},{8,13},{9,12},{10,... | collective-permute-start | bytes 645128 | tf_op jit(solution)/shard_map/ppermute | solution.py:463
  148.6 26.4 %collective-permute-start.5 = (bf16[1,96,1120]{2,1,0:T(8,128)(2,1)}, bf16[1,96,1120]{2,1,0:T(8,128)(2,1)S(1)}, u32[]{:S(2)}, u32[]{:S(2)}) collective-permute-start(bf16[1,96,1120]{2,1,0:T(8,128)(2,1)} %get-tuple-element.104), channel_id=1, source_target_pairs={{0,6},{1,7},{2,4},{3,5},{4,2},{5,3},{6,0},{7,1},{8,14},{9,15},{10,... | collective-permute-start | bytes 645128 | tf_op jit(solution)/shard_map/ppermute | solution.py:463
  151.0 24.0 %collective-permute-start.6 = (bf16[1,96,1120]{2,1,0:T(8,128)(2,1)}, bf16[1,96,1120]{2,1,0:T(8,128)(2,1)S(1)}, u32[]{:S(2)}, u32[]{:S(2)}) collective-permute-start(bf16[1,96,1120]{2,1,0:T(8,128)(2,1)} %get-tuple-element.103), channel_id=1, source_target_pairs={{0,7},{1,6},{2,5},{3,4},{4,3},{5,2},{6,1},{7,0},{8,15},{9,14},{10,... | collective-permute-start | bytes 645128 | tf_op jit(solution)/shard_map/ppermute | solution.py:463
  153.5 40.6 %collective-permute-start.15 = (bf16[768,1120]{0,1:T(8,128)(2,1)S(1)}, bf16[768,1120]{0,1:T(8,128)(2,1)}, u32[]{:S(2)}, u32[]{:S(2)}) collective-permute-start(bf16[768,1120]{0,1:T(8,128)(2,1)S(1)} %copy.85), channel_id=1, source_target_pairs={{0,8},{1,9},{2,10},{3,11},{4,12},{5,13},{6,14},{7,15},{8,0},{9,1},... | collective-permute-start | bytes 5160968 | tf_op jit(solution)/shard_map/ppermute | solution.py:397
  177.3 53.6 %collective-permute-start.7 = (bf16[768,1120]{0,1:T(8,128)(2,1)}, bf16[768,1120]{0,1:T(8,128)(2,1)}, u32[]{:S(2)}, u32[]{:S(2)}) collective-permute-start(bf16[768,1120]{0,1:T(8,128)(2,1)} %copy.82), channel_id=1, source_target_pairs={{0,8},{1,9},{2,10},{3,11},{4,12},{5,13},{6,14},{7,15},{8,0},{9,1},... | collective-permute-start | bytes 5160968 | tf_op jit(solution)/shard_map/ppermute | solution.py:397
  177.4 64.1 %collective-permute-start.18 = (bf16[512,1536]{1,0:T(8,128)(2,1)}, bf16[512,1536]{1,0:T(8,128)(2,1)}, u32[]{:S(2)}, u32[]{:S(2)}) collective-permute-start(bf16[512,1536]{1,0:T(8,128)(2,1)} %bitcast.25), channel_id=1, source_target_pairs={{0,2},{1,3},{2,0},{3,1},{4,6},{5,7},{6,4},{7,5},{8,10},{9,11},{10,... | collective-permute-start | bytes 4718600 | tf_op jit(solution)/shard_map/ppermute | solution.py:412
  178.8 151.5 %collective-permute-start.16 = (bf16[560,1536]{1,0:T(8,128)(2,1)}, bf16[560,1536]{1,0:T(8,128)(2,1)}, u32[]{:S(2)}, u32[]{:S(2)}) collective-permute-start(bf16[560,1536]{1,0:T(8,128)(2,1)} %param.29), channel_id=1, source_target_pairs={{0,8},{1,9},{2,10},{3,11},{4,12},{5,13},{6,14},{7,15},{8,0},{9,1},... | collective-permute-start | bytes 5160968 | tf_op jit(solution)/shard_map/ppermute | solution.py:397
  234.8 50.2 %collective-permute-start.17 = (bf16[512,1536]{1,0:T(8,128)(2,1)}, bf16[512,1536]{1,0:T(8,128)(2,1)}, u32[]{:S(2)}, u32[]{:S(2)}) collective-permute-start(bf16[512,1536]{1,0:T(8,128)(2,1)} %bitcast.25), channel_id=1, source_target_pairs={{0,1},{1,0},{2,3},{3,2},{4,5},{5,4},{6,7},{7,6},{8,9},{9,8},{10,11... | collective-permute-start | bytes 4718600 | tf_op jit(solution)/shard_map/ppermute | solution.py:412
  234.8 48.9 %collective-permute-start.20 = (bf16[512,1536]{1,0:T(8,128)(2,1)}, bf16[512,1536]{1,0:T(8,128)(2,1)}, u32[]{:S(2)}, u32[]{:S(2)}) collective-permute-start(bf16[512,1536]{1,0:T(8,128)(2,1)} %bitcast.25), channel_id=1, source_target_pairs={{0,4},{1,5},{2,6},{3,7},{4,0},{5,1},{6,2},{7,3},{8,12},{9,13},{10,... | collective-permute-start | bytes 4718600 | tf_op jit(solution)/shard_map/ppermute | solution.py:412
  241.5 69.8 %collective-permute-start.19 = (bf16[512,1536]{1,0:T(8,128)(2,1)}, bf16[512,1536]{1,0:T(8,128)(2,1)S(1)}, u32[]{:S(2)}, u32[]{:S(2)}) collective-permute-start(bf16[512,1536]{1,0:T(8,128)(2,1)} %collective-permute-done.18), channel_id=1, source_target_pairs={{0,1},{1,0},{2,3},{3,2},{4,5},{5,4},{6,7},{7,6},{8,9},{9,8},{10,11... | collective-permute-start | bytes 4718600 | tf_op jit(solution)/shard_map/ppermute | solution.py:412
  247.0 384.0 %reduce-scatter.7.cloned.1.call-start = ((), (), s32[]{:S(2)}) async-start(), calls=%async_computation.10 | async-start | bytes 14155776 | tf_op jit(solution)/shard_map/reduce_scatter | solution.py:408
  284.9 26.4 %collective-permute-start.22 = (bf16[256,1536]{1,0:T(8,128)(2,1)S(1)}, bf16[256,1536]{1,0:T(8,128)(2,1)S(1)}, u32[]{:S(2)}, u32[]{:S(2)}) collective-permute-start(bf16[256,1536]{1,0:T(8,128)(2,1)S(1)} %slice.156), channel_id=1, source_target_pairs={{0,2},{1,3},{2,0},{3,1},{4,6},{5,7},{6,4},{7,5},{8,10},{9,11},{10,... | collective-permute-start | bytes 2359304 | tf_op jit(solution)/shard_map/ppermute | solution.py:412
  284.9 30.2 %collective-permute-start.21 = (bf16[512,1536]{1,0:T(8,128)(2,1)}, bf16[512,1536]{1,0:T(8,128)(2,1)S(1)}, u32[]{:S(2)}, u32[]{:S(2)}) collective-permute-start(bf16[512,1536]{1,0:T(8,128)(2,1)} %collective-permute-done.20), channel_id=1, source_target_pairs={{0,1},{1,0},{2,3},{3,2},{4,5},{5,4},{6,7},{7,6},{8,9},{9,8},{10,11... | collective-permute-start | bytes 4718600 | tf_op jit(solution)/shard_map/ppermute | solution.py:412
  311.2 6.1 collective-permute-start.23
  382.1 14.1 %copy-start.48 = (bf16[2048,1120]{0,1:T(8,128)(2,1)S(1)}, bf16[2048,1120]{0,1:T(8,128)(2,1)}, u32[]{:S(2)}) copy-start(bf16[2048,1120]{0,1:T(8,128)(2,1)} %get-tuple-element.51) | copy-start | bytes 13762564
  410.9 220.0 %reduce-scatter.9.cloned.1.call-start = ((), (), s32[]{:S(2)}) async-start(), calls=%async_computation.12 | async-start | bytes 14155776 | tf_op jit(solution)/shard_map/reduce_scatter | solution.py:408
  412.2 20.0 %collective-permute-start.24 = (bf16[256,1536]{1,0:T(8,128)(2,1)S(1)}, bf16[256,1536]{1,0:T(8,128)(2,1)S(1)}, u32[]{:S(2)}, u32[]{:S(2)}) collective-permute-start(bf16[256,1536]{1,0:T(8,128)(2,1)S(1)} %slice.159), channel_id=1, source_target_pairs={{0,4},{1,5},{2,6},{3,7},{4,0},{5,1},{6,2},{7,3},{8,12},{9,13},{10,... | collective-permute-start | bytes 2359304 | tf_op jit(solution)/shard_map/ppermute | solution.py:412
  432.2 2.3 collective-permute-start.25
  435.4 14.3 %copy-start.46 = (bf16[2048,1536]{1,0:T(8,128)(2,1)S(1)}, bf16[2048,1536]{1,0:T(8,128)(2,1)}, u32[]{:S(2)}) copy-start(bf16[2048,1536]{1,0:T(8,128)(2,1)} %all-gather.11.cloned.1.call-done) | copy-start | bytes 18874372
  479.5 14.3 %copy-start.47 = (bf16[2048,1120]{0,1:T(8,128)(2,1)S(1)}, bf16[2048,1120]{0,1:T(8,128)(2,1)}, u32[]{:S(2)}) copy-start(bf16[2048,1120]{0,1:T(8,128)(2,1)} %get-tuple-element.53) | copy-start | bytes 13762564
  508.6 425.9 %reduce-scatter.5.cloned.1.call-start = ((), (), s32[]{:S(2)}) async-start(), calls=%async_computation.9 | async-start | bytes 14155776 | tf_op jit(solution)/shard_map/reduce_scatter | solution.py:408
  508.6 7.8 slice-start.4
  509.4 425.2 %reduce-scatter.11.cloned.1.call-start = ((), (), s32[]{:S(2)}) async-start(), calls=%async_computation.13 | async-start | bytes 14155776 | tf_op jit(solution)/shard_map/reduce_scatter | solution.py:408
  509.4 7.0 slice-start.5
  535.5 23.6 %slice-start.8 = ((s8[4587520]{0:T(1024)(128)(4,1)}), s8[4194304]{0:T(1024)(128)(4,1)S(1)}, s32[]{:S(2)}) async-start(s8[4587520]{0:T(1024)(128)(4,1)} %bitcast.163), calls=%async_computation.22 | async-start | bytes 8388608
  544.5 14.7 %slice-start.9 = ((s8[4587520]{0:T(1024)(128)(4,1)}), s8[393216]{0:T(1024)(128)(4,1)S(1)}, s32[]{:S(2)}) async-start(s8[4587520]{0:T(1024)(128)(4,1)} %bitcast.163), calls=%async_computation.23 | async-start | bytes 786432
  544.5 76.9 %collective-permute-start.26 = (f32[768,1120]{0,1:T(8,128)}, f32[768,1120]{0,1:T(8,128)}, u32[]{:S(2)}, u32[]{:S(2)}) collective-permute-start(f32[768,1120]{0,1:T(8,128)} %convolution_add_fusion.4), channel_id=1, source_target_pairs={{0,8},{1,9},{2,10},{3,11},{4,12},{5,13},{6,14},{7,15},{8,0},{9,1},... | collective-permute-start | bytes 10321928 | tf_op jit(solution)/shard_map/ppermute | solution.py:397
  546.0 27.8 %slice-start.2 = ((s8[6291456]{0:T(1024)(128)(4,1)}), s8[4194304]{0:T(1024)(128)(4,1)S(1)}, s32[]{:S(2)}) async-start(s8[6291456]{0:T(1024)(128)(4,1)} %bitcast.156), calls=%async_computation.16 | async-start | bytes 8388608
  559.1 14.6 %slice-start.3 = ((s8[6291456]{0:T(1024)(128)(4,1)}), s8[2097152]{0:T(1024)(128)(4,1)S(1)}, s32[]{:S(2)}) async-start(s8[6291456]{0:T(1024)(128)(4,1)} %bitcast.156), calls=%async_computation.17 | async-start | bytes 4194304
  573.7 17.5 %slice-start.6 = ((s8[6291456]{0:T(1024)(128)(4,1)}), s8[4194304]{0:T(1024)(128)(4,1)S(1)}, s32[]{:S(2)}) async-start(s8[6291456]{0:T(1024)(128)(4,1)} %bitcast.160), calls=%async_computation.20 | async-start | bytes 8388608
  583.3 8.0 slice-start.7
  591.2 8.9 copy-start.34
  591.2 8.9 copy-start.35
  631.0 11.8 %copy-start.4 = (bf16[512,1536]{1,0:T(8,128)(2,1)S(1)}, bf16[512,1536]{1,0:T(8,128)(2,1)}, u32[]{:S(2)}) copy-start(bf16[512,1536]{1,0:T(8,128)(2,1)} %copy-done.3) | copy-start | bytes 4718596
  641.3 77.6 %collective-permute-start.27 = (f32[768,1120]{0,1:T(8,128)}, f32[768,1120]{0,1:T(8,128)}, u32[]{:S(2)}, u32[]{:S(2)}) collective-permute-start(f32[768,1120]{0,1:T(8,128)} %convolution_add_fusion.3), channel_id=1, source_target_pairs={{0,8},{1,9},{2,10},{3,11},{4,12},{5,13},{6,14},{7,15},{8,0},{9,1},... | collective-permute-start | bytes 10321928 | tf_op jit(solution)/shard_map/ppermute | solution.py:397
  643.5 82.9 %copy-start.36 = (f32[256,1536]{1,0:T(8,128)S(1)}, f32[256,1536]{1,0:T(8,128)}, u32[]{:S(2)}) copy-start(f32[256,1536]{1,0:T(8,128)} %reduce-scatter.7.cloned.1.call-done) | copy-start | bytes 4718596
  643.5 298.4 %collective-permute-start.28 = (f32[560,1536]{1,0:T(8,128)}, f32[560,1536]{1,0:T(8,128)}, u32[]{:S(2)}, u32[]{:S(2)}) collective-permute-start(f32[560,1536]{1,0:T(8,128)} %get-tuple-element.92), channel_id=1, source_target_pairs={{0,8},{1,9},{2,10},{3,11},{4,12},{5,13},{6,14},{7,15},{8,0},{9,1},... | collective-permute-start | bytes 10321928 | tf_op jit(solution)/shard_map/ppermute | solution.py:397
  727.3 66.0 %all-to-all-start = ((f32[8,96,1120]{2,1,0:T(8,128)}), f32[8,96,1120]{2,1,0:T(8,128)}, u32[]{:S(2)}, u32[]{:S(2)}) async-start(f32[8,96,1120]{2,1,0:T(8,128)} %bitcast.51), calls=%async_computation.4 | async-start | bytes 7077888 | tf_op jit(solution)/shard_map/all_to_all | solution.py:542
  737.4 5.2 copy-start.11
  737.5 5.2 copy-start.13
  737.5 23.5 %slice-start = ((s8[6684672]{0:T(1024)(128)(4,1)}), s8[4194304]{0:T(1024)(128)(4,1)S(1)}, s32[]{:S(2)}) async-start(s8[6684672]{0:T(1024)(128)(4,1)} %bitcast.150), calls=%async_computation.14 | async-start | bytes 8388608
  742.6 18.4 %slice-start.1 = ((s8[6684672]{0:T(1024)(128)(4,1)}), s8[2490368]{0:T(1024)(128)(4,1)S(1)}, s32[]{:S(2)}) async-start(s8[6684672]{0:T(1024)(128)(4,1)} %bitcast.150), calls=%async_computation.15 | async-start | bytes 4980736
  799.6 132.0 %all-to-all-start.1 = ((f32[8,96,1120]{2,1,0:T(8,128)}), f32[8,96,1120]{2,1,0:T(8,128)S(1)}, u32[]{:S(2)}, u32[]{:S(2)}) async-start(f32[8,96,1120]{2,1,0:T(8,128)} %bitcast.141), calls=%async_computation.5 | async-start | bytes 7077888 | tf_op jit(solution)/shard_map/all_to_all | solution.py:542
  934.5 5.6 copy-start.22
  (34 other events, 85.8 us)
Sparse Core Ops, SparseCore 0:
  10.8 46.2 all-gather.4
  59.3 37.0 all-gather.6
  105.4 77.7 all-gather.8
  247.1 56.4 all-gather.10
  411.1 86.7 reduce-scatter.6
  508.7 86.7 reduce-scatter.8
  599.0 86.6 reduce-scatter.4
  689.2 121.5 reduce-scatter.10
